TPU v7x, 16 devices: a whole 2x2x2 slice. The times are simulated.
16 devices in a mesh: dp: 2 (over z), tp: 8 (over y, x, core).
Axes of the slice: x: 2, y: 2, z: 2, core: 2. Of those that a mesh axis runs over, the one named last changes fastest.
Arguments:
- x: bfloat16 [64, 256, 1152], P('dp', 'tp'), parts along dimension 0
- d_out: bfloat16 [64, 256, 1152], P('dp', 'tp'), parts along dimension 0
- ln1_gain: float32 [1152], replicated
- ln1_bias: float32 [1152], replicated
- w_q: bfloat16 [1152, 16, 72], P(None, 'tp')
- b_q: bfloat16 [16, 72], P('tp')
- w_k: bfloat16 [1152, 16, 72], P(None, 'tp')
- w_v: bfloat16 [1152, 16, 72], P(None, 'tp')
- b_v: bfloat16 [16, 72], P('tp')
- w_o: bfloat16 [16, 72, 1152], P('tp')
- b_o: bfloat16 [1152], replicated
- ln2_gain: float32 [1152], replicated
- ln2_bias: float32 [1152], replicated
- w_1: bfloat16 [1152, 4304], P(None, 'tp')
- b_1: bfloat16 [4304], P('tp')
- w_2: bfloat16 [4304, 1152], P('tp')
- b_2: bfloat16 [1152], replicated
Outputs:
- output 1: bfloat16 [64, 256, 1152], P('dp', 'tp'), parts along dimension 0
- output 2: bfloat16 [64, 256, 1152], P('dp', 'tp'), parts along dimension 0
- output 3: float32 [2304], P('dp'), parts along dimension 0
- output 4: float32 [2304], P('dp'), parts along dimension 0
- output 5: bfloat16 [2304, 16, 72], P('dp', 'tp'), parts along dimension 0
- output 6: bfloat16 [32, 72], P(('dp', 'tp')), parts along dimension 0
- output 7: bfloat16 [2304, 16, 72], P('dp', 'tp'), parts along dimension 0
- output 8: bfloat16 [2304, 16, 72], P('dp', 'tp'), parts along dimension 0
- output 9: bfloat16 [32, 72], P(('dp', 'tp')), parts along dimension 0
- output 10: bfloat16 [32, 72, 1152], P(('dp', 'tp')), parts along dimension 0
- output 11: bfloat16 [2304], P('dp'), parts along dimension 0
- output 12: float32 [2304], P('dp'), parts along dimension 0
- output 13: float32 [2304], P('dp'), parts along dimension 0
- output 14: bfloat16 [2304, 4304], P('dp', 'tp'), parts along dimension 0
- output 15: bfloat16 [8608], P(('dp', 'tp')), parts along dimension 0
- output 16: bfloat16 [8608, 1152], P(('dp', 'tp')), parts along dimension 0
- output 17: bfloat16 [2304], P('dp'), parts along dimension 0
There are 2 independent parts. A program takes and returns all parts, laid end to end along the dimension named above; an argument that names none is the same for every part.
All inputs are finite; a program needn't handle non-finite values.
Results may differ from a plain program's by a relative error of at most 0.0189534.
Values are sent between devices in bfloat16 or wider.
A program may use at most 1 GiB of HBM per device.

v0:
```python
import math
import jax
import jax.numpy as jnp
from jax import lax
from jax.experimental import pallas as pl
from jax.experimental.pallas import tpu as pltpu
from jax.sharding import Mesh, PartitionSpec as P

LN_EPS = 1e-6
BF16 = jnp.bfloat16
F32 = jnp.float32

CHIPS = 4
HEADS = 2
HEAD_DIM = 72
QROWS = HEADS * HEAD_DIM
WIDTH = 1152
MLP = 538
MLP_PAD = 544
HALF = MLP_PAD // 2
ALL_AXES = ('dp', 'chip', 'core')
N_HEADS = 16
WIN_LANES = 256
ATT_SCALE = 1.0 / math.sqrt(HEAD_DIM)


def layer_norm(rows, ln_gain, ln_bias):
    row_mean = jnp.mean(rows, axis=-1, keepdims=True)
    centered = rows - row_mean
    variance = jnp.mean(centered * centered, axis=-1, keepdims=True)
    return centered * lax.rsqrt(variance + LN_EPS) * ln_gain + ln_bias


def gelu_tanh(pre_act):
    return jax.nn.gelu(pre_act, approximate=True)


def dot_nt(a, b):
    return lax.dot_general(a, b, (((1,), (1,)), ((), ())), preferred_element_type=F32)
def dot_nn(a, b):
    return lax.dot_general(a, b, (((1,), (0,)), ((), ())), preferred_element_type=F32)
def dot_tn(a, b):
    return lax.dot_general(a, b, (((0,), (0,)), ((), ())), preferred_element_type=F32)

def head_window(head):
    low = head * HEAD_DIM
    base = jnp.minimum(low // 128, WIDTH // 128 - 2) * 128
    base = pl.multiple_of(base, 128)
    lane = lax.broadcasted_iota(jnp.int32, (1, WIN_LANES), 1)
    mask = (lane >= low - base) & (lane < low - base + HEAD_DIM)
    return pl.ds(base, WIN_LANES), base, mask

def probs_t(keys, queries):
    scores = dot_nt(keys, queries) * ATT_SCALE
    scores = jnp.exp(scores - jnp.max(scores, axis=0, keepdims=True))
    return scores * (1.0 / jnp.sum(scores, axis=0, keepdims=True))

def attn_fwd(q_ref, k_ref, v_ref, out_ref, acc):
    acc[...] = jnp.zeros_like(acc)

    def body(head, _):
        win, _, mask = head_window(head)
        zero = jnp.zeros((), BF16)
        keys = jnp.where(mask, k_ref[:, win], zero)
        vals = jnp.where(mask, v_ref[:, win], zero)
        probs = probs_t(keys, q_ref[:, win]).astype(BF16)
        acc[:, win] += dot_tn(probs, vals)
        return 0

    lax.fori_loop(0, N_HEADS, body, 0, unroll=2)
    out_ref[...] = acc[...].astype(BF16)

def attn_bwd(q_ref, k_ref, v_ref, do_ref, out_ref, acc):
    acc[...] = jnp.zeros_like(acc)

    def body(head, _):
        win, base, mask = head_window(head)
        zero = jnp.zeros((), BF16)
        queries = jnp.where(mask, q_ref[:, win], zero)
        keys = jnp.where(mask, k_ref[:, win], zero)
        d_out = jnp.where(mask, do_ref[:, win], zero)
        probs = probs_t(keys, queries)
        d_probs = dot_nt(v_ref[:, win], d_out).astype(BF16).astype(F32)
        prod = d_probs * probs
        d_scores = (prod - probs * jnp.sum(prod, axis=0, keepdims=True)) * ATT_SCALE
        d_scores = d_scores.astype(BF16)
        acc[:, win] += dot_tn(d_scores, keys)
        acc[:, pl.ds(pl.multiple_of(base + WIDTH, 128), WIN_LANES)] += dot_nn(d_scores, queries)
        acc[:, pl.ds(pl.multiple_of(base + 2 * WIDTH, 128), WIN_LANES)] += dot_nn(probs.astype(BF16), d_out)
        return 0

    lax.fori_loop(0, N_HEADS, body, 0, unroll=2)
    out_ref[...] = acc[...].astype(BF16)

def part_spec(toks, part):
    return pl.BlockSpec((toks, WIDTH), lambda i: (i, part))

def attention_forward(qkv, toks):
    rows = qkv.shape[0]
    flops = 2 * 2 * rows * toks * 256 * N_HEADS
    return pl.pallas_call(attn_fwd, grid=(rows // toks,), out_shape=jax.ShapeDtypeStruct((rows, WIDTH), BF16),
        in_specs=[part_spec(toks, p) for p in range(3)], out_specs=part_spec(toks, 0),
        scratch_shapes=[pltpu.VMEM((toks, WIDTH), F32)], name='attn_fwd',
        cost_estimate=pl.CostEstimate(flops=4*flops, bytes_accessed=rows * WIDTH * 8, transcendentals=rows * toks * N_HEADS),
    )(qkv, qkv, qkv)

def attention_backward(qkv, d_mixed, toks):
    rows = qkv.shape[0]
    flops = 5 * 2 * rows * toks * 256 * N_HEADS
    return pl.pallas_call(attn_bwd, grid=(rows // toks,), out_shape=jax.ShapeDtypeStruct((rows, 3 * WIDTH), BF16),
        in_specs=[part_spec(toks, p) for p in range(3)] + [part_spec(toks, 0)],
        out_specs=pl.BlockSpec((toks, 3 * WIDTH), lambda i: (i, 0)),
        scratch_shapes=[pltpu.VMEM((toks, 3 * WIDTH), F32)], name='attn_bwd',
        cost_estimate=pl.CostEstimate(flops=4*flops, bytes_accessed=rows * WIDTH * 14, transcendentals=rows * toks * N_HEADS),
    )(qkv, qkv, qkv, d_mixed)


def tie(val, *deps):
    return lax.optimization_barrier((val,) + deps)[0]


def solution(mesh):
    mesh3 = Mesh(mesh.devices.reshape(2, CHIPS, 2), ALL_AXES)
    tp = ('chip', 'core')
    act_spec = P('dp', tp, None)
    replicated = P()
    head_w = P(None, tp, None)
    head_b = P(tp, None)
    grad_head_w = P('dp', tp, None)
    dp_tp = ('dp', 'chip', 'core')
    grad_head_b = P(dp_tp, None)
    grad_vec = P('dp')
    in_specs = (act_spec, act_spec, replicated, replicated, head_w, head_b, head_w, head_w, head_b,
                P(tp, None, None), replicated, replicated, replicated, P(None, tp), P(tp), P(tp, None), replicated)
    out_specs = (act_spec, act_spec, grad_vec, grad_vec, grad_head_w, grad_head_b, grad_head_w, grad_head_w, grad_head_b,
                 P(dp_tp, None, None), grad_vec, grad_vec, grad_vec, P('dp', tp), P(dp_tp),
                 P(dp_tp, None), grad_vec)

    def tp_perm(fn):
        return [(i, fn(i)) for i in range(8)]

    def permute(val, fn):
        return lax.ppermute(val, tp, tp_perm(fn))

    def core_swap(val):
        return permute(val, lambda i: i ^ 1)

    def pick(val, idx, axis=0):
        return lax.dynamic_index_in_dim(val, idx, axis, keepdims=False)

    def layer_step(x, d_out, ln1_gain, ln1_bias, w_q, b_q, w_k, w_v, b_v, w_o, b_o, ln2_gain, ln2_bias, w_1, b_1, w_2, b_2):
        dp = lax.axis_index('dp')
        chip = lax.axis_index('chip')
        core = lax.axis_index('core')
        cx, cy = chip % 2, chip // 2
        rank = chip * 2 + core
        core0 = core == 0
        images = x.shape[0] // 8
        toks = x.shape[1]
        rows = images * toks * 8

        def to_images(val):
            blocks = val.reshape(8, images, toks, WIDTH)
            pieces = []
            for k in range(8):
                piece = pick(blocks, rank ^ k)
                if k:
                    piece = permute(piece, lambda i: i ^ k)
                pieces.append(piece[:, None])
            return jnp.concatenate(pieces, axis=1).reshape(rows, WIDTH)

        def to_tokens(val):
            blocks = val.reshape(images, 8, toks, WIDTH)
            pieces = []
            for k in range(8):
                piece = blocks[:, k]
                if k:
                    piece = permute(piece, lambda i: i ^ k)
                pieces.append(piece)
            for bit in (1, 2, 4):
                odd = (rank & bit) != 0
                pieces = [jnp.where(odd, pieces[k ^ bit], pieces[k]) for k in range(8)]
            return jnp.concatenate(pieces, axis=0)

        first = lambda i: (i ^ 2) if i % 2 == 0 else (i ^ 4)
        second = lambda i: (i ^ 4) if i % 2 == 0 else (i ^ 2)
        me = jnp.where(core0, cy, cx)
        away = lambda k: jnp.where(core0, k * 2 + (1 - cx), (1 - cy) * 2 + k)
        near = lambda k: jnp.where(core0, k * 2 + cx, cy * 2 + k)

        def stage2(own, got, axis):
            blk = lambda i: pick(own, i, axis) + pick(got, i, axis)
            send = (blk(away(1 - me)), blk(away(me)))
            far = permute(send[0], first)
            close = permute(send[1], first)
            return send, (far, close)

        def stage3(own, got, axis, far):
            send = pick(own, near(1 - me), axis) + pick(got, near(1 - me), axis) + far
            return send, permute(send, second)

        def finish(own, got, axis, close, part):
            return pick(own, near(me), axis) + pick(got, near(me), axis) + close + part

        def gather(half0, half1):
            mine = jnp.where(dp == 0, half0, half1)
            own = lax.all_gather(mine, ('dp', 'chip'), axis=0, tiled=False)
            own = own.reshape(2, CHIPS, *mine.shape)
            return own, core_swap(own)

        def rows_of(w):
            return jnp.transpose(w, (1, 2, 0)).reshape(QROWS, WIDTH)

        b1_pad = jnp.pad(b_1, (0, MLP_PAD - MLP))

        def bias_rows(head_bias, mlp_bias):
            row = jnp.concatenate([head_bias.reshape(QROWS), mlp_bias])
            return jnp.pad(row[None], ((0, 15), (0, WIDTH - row.shape[0])))

        att0 = jnp.concatenate([rows_of(w_q), rows_of(w_k), bias_rows(b_q, b1_pad[:HALF])])
        att1 = jnp.concatenate([rows_of(w_v), w_o.reshape(QROWS, WIDTH), bias_rows(b_v, b1_pad[HALF:])])
        att = gather(att0, att1)
        w1_rows = jnp.pad(w_1.T, ((0, MLP_PAD - MLP), (0, 0)))
        w2_rows = jnp.pad(w_2, ((0, MLP_PAD - MLP), (0, 0)))
        w1_all = [w.reshape(2 * CHIPS * HALF, WIDTH) for w in gather(w1_rows[:HALF], w1_rows[HALF:])]
        w2_all = [w.reshape(2 * CHIPS * HALF, WIDTH) for w in gather(w2_rows[:HALF], w2_rows[HALF:])]

        flat = CHIPS * QROWS
        part = lambda half, first: [a[half, :, first:first + QROWS].reshape(flat, WIDTH) for a in att]
        bias = lambda half: [a[half, :, 2 * QROWS, :QROWS].reshape(flat) for a in att]
        wqkv = jnp.concatenate(part(0, 0) + part(0, QROWS) + part(1, 0))
        wo_all = jnp.concatenate(part(1, QROWS))
        bqkv = jnp.concatenate(bias(0) + [jnp.zeros((2 * flat,), BF16)] + bias(1)).astype(F32)
        b1_all = [a[:, :, 2 * QROWS, QROWS:QROWS + HALF].reshape(2 * CHIPS * HALF).astype(F32) for a in att]

        x_rows = to_images(x)
        g_out = to_images(tie(d_out, att[0]))

        x_f32 = x_rows.astype(F32)
        h_one_f, ln1_pull = jax.vjp(layer_norm, x_f32, ln1_gain, ln1_bias)
        h_one = h_one_f.astype(BF16)
        qkv = (dot_nt(h_one, wqkv) + bqkv).astype(BF16)
        mixed = attention_forward(qkv, 8 * toks)
        attn_out = dot_nn(mixed, wo_all)
        x_mid = (x_f32 + attn_out + b_o).astype(BF16)
        mid_f32 = x_mid.astype(F32)
        h_two_f, ln2_pull = jax.vjp(layer_norm, mid_f32, ln2_gain, ln2_bias)
        h_two = h_two_f.astype(BF16)
        blocks = (2, CHIPS, HALF, WIDTH)
        hidden, gelu_pulls = [], []
        for w1, b1 in zip(w1_all, b1_all):
            pre_act = (dot_nt(h_two, w1) + b1).astype(BF16)
            hid_f, gelu_pull = jax.vjp(gelu_tanh, pre_act.astype(F32))
            hidden.append(hid_f.astype(BF16))
            gelu_pulls.append(gelu_pull)
        w2_oth = dot_tn(hidden[1], g_out).reshape(blocks)
        w2_got = core_swap(w2_oth)
        w2_own = dot_tn(tie(hidden[0], w2_oth), g_out).reshape(blocks)
        w2_send, w2_in = stage2(w2_own, w2_got, 1)
        g_mlp = tie(g_out, *w2_send)
        d_pre = [None, None]
        for c in (1, 0):
            d_hidden = dot_nt(g_mlp, w2_all[c]).astype(BF16)
            (d_pre_f,) = gelu_pulls[c](d_hidden.astype(F32))
            d_pre[c] = d_pre_f.astype(BF16)
        w1_oth = dot_tn(d_pre[1], h_two).reshape(blocks)
        w1_got = core_swap(w1_oth)
        w1_own = dot_tn(tie(d_pre[0], w1_oth), h_two).reshape(blocks)
        w1_send, w1_in = stage2(w1_own, w1_got, 1)
        d_pre_t = [tie(d, *w1_send) for d in d_pre]
        d_h_two = (dot_nn(d_pre_t[0], w1_all[0]) + dot_nn(d_pre_t[1], w1_all[1])).astype(BF16)
        d_mid_ln, g_ln2_gain, g_ln2_bias = ln2_pull(d_h_two.astype(F32))
        d_mid = (g_out.astype(F32) + d_mid_ln).astype(BF16)
        d_mixed = dot_nt(d_mid, wo_all).astype(BF16)
        wo_oth = dot_tn(mixed[:, flat:], d_mid).reshape(CHIPS, QROWS, WIDTH)
        wo_got = core_swap(wo_oth)
        wo_own = dot_tn(mixed[:, :flat], d_mid).reshape(CHIPS, QROWS, WIDTH)
        w2_last, w2_part = stage3(w2_own, w2_got, 1, w2_in[0])
        wo_send, wo_in = stage2(wo_own, wo_got, 0)
        d_qkv = attention_backward(qkv, tie(d_mixed, w2_last, *wo_send), 8 * toks)
        w1_last, w1_part = stage3(w1_own, w1_got, 1, w1_in[0])
        wo_last, wo_part = stage3(wo_own, wo_got, 0, wo_in[0])
        d_qkv = tie(d_qkv, w1_last, wo_last)
        dw_qkv = dot_tn(d_qkv, h_one).reshape(3, 2, CHIPS, QROWS, WIDTH)
        qkv_own, qkv_oth = dw_qkv[:, 0], dw_qkv[:, 1]
        qkv_got = core_swap(qkv_oth)
        d_h_one = dot_nn(tie(d_qkv, qkv_oth), wqkv).astype(BF16)
        qkv_send, qkv_in = stage2(qkv_own, qkv_got, 1)
        d_h_one = tie(d_h_one, *qkv_send)
        d_in_ln, g_ln1_gain, g_ln1_bias = ln1_pull(d_h_one.astype(F32))
        g_x = (d_mid.astype(F32) + d_in_ln).astype(BF16)
        grad_x = to_tokens(g_x)
        mlp_out = dot_nn(tie(hidden[0], d_h_one), w2_all[0])
        mlp_out = mlp_out + dot_nn(hidden[1], w2_all[1])
        y_rows = (mid_f32 + mlp_out + b_2).astype(BF16)
        y_out = to_tokens(y_rows)
        _, qkv_part = stage3(qkv_own, qkv_got, 1, qkv_in[0])

        grad_w2 = finish(w2_own, w2_got, 1, w2_in[1], w2_part)
        grad_w2 = grad_w2.reshape(MLP_PAD, WIDTH)[:MLP].astype(BF16)
        grad_w1 = finish(w1_own, w1_got, 1, w1_in[1], w1_part)
        grad_w1 = grad_w1.reshape(MLP_PAD, WIDTH)[:MLP].T.astype(BF16)
        grad_wo = finish(wo_own, wo_got, 0, wo_in[1], wo_part)
        grad_wo = grad_wo.reshape(HEADS, HEAD_DIM, WIDTH).astype(BF16)
        grad_qkv = finish(qkv_own, qkv_got, 1, qkv_in[1], qkv_part).astype(BF16)
        unrow = lambda w: jnp.transpose(w.reshape(HEADS, HEAD_DIM, WIDTH), (2, 0, 1))

        col_sum = lambda v: jnp.sum(v, axis=0, dtype=F32)
        vecs = jnp.stack([g_ln1_gain, g_ln1_bias, col_sum(d_mid), g_ln2_gain, g_ln2_bias, col_sum(g_out)])

        qkv_sums = col_sum(d_qkv).reshape(3, 2, CHIPS, QROWS)

        def extra_rows(c):
            sums = qkv_sums[:, c]
            b1_sum = jnp.transpose(col_sum(d_pre[c]).reshape(2, CHIPS, HALF), (1, 0, 2)).reshape(CHIPS, MLP_PAD)
            row = jnp.concatenate([sums[0], sums[2], b1_sum, jnp.zeros((CHIPS, WIDTH - 2 * QROWS - MLP_PAD), F32)], axis=1)
            return jnp.concatenate([jnp.broadcast_to(vecs, (CHIPS, 6, WIDTH)), row[:, None],
                                    jnp.zeros((CHIPS, 1, WIDTH), F32)], axis=1)

        ex_own, ex_got = extra_rows(0), core_swap(extra_rows(1))
        _, ex_in = stage2(ex_own, ex_got, 0)
        _, ex_part = stage3(ex_own, ex_got, 0, ex_in[0])
        extra = finish(ex_own, ex_got, 0, ex_in[1], ex_part)
        b_row = extra[6].astype(BF16)
        return (y_out, grad_x, extra[0], extra[1], unrow(grad_qkv[0]), b_row[:QROWS].reshape(HEADS, HEAD_DIM),
                unrow(grad_qkv[1]), unrow(grad_qkv[2]), b_row[QROWS:2 * QROWS].reshape(HEADS, HEAD_DIM), grad_wo,
                extra[2].astype(BF16), extra[3], extra[4], grad_w1, b_row[2 * QROWS:2 * QROWS + MLP], grad_w2,
                extra[5].astype(BF16))

    return jax.shard_map(layer_step, mesh=mesh3, in_specs=in_specs, out_specs=out_specs, check_vma=False)
```

profile of v0, /device:TPU:0, one launch (start us, length us, event | category | flops | bytes accessed | tf_op | source)
XLA Modules:
  0.0 832.1 jit_solution(8667661127301191661)
XLA Ops:
  17.1 3.6 collective-permute-start.6
  28.4 18.3 %collective-permute-done.1 = bf16[4,32,1152]{2,1,0:T(8,128)(2,1)S(1)} collective-permute-done((bf16[4,32,1152]{2,1,0:T(8,128)(2,1)}, bf16[4,32,1152]{2,1,0:T(8,128)(2,1)S(1)}, u32[]{:S(2)}, u32[]{:S(2)}) %collective-permute-start.1) | collective-permute-done | bytes 294944 | tf_op jit(solution)/shard_map/ppermute | solution.py:143
  48.1 13.2 %collective-permute-done.2 = bf16[4,32,1152]{2,1,0:T(8,128)(2,1)S(1)} collective-permute-done((bf16[4,32,1152]{2,1,0:T(8,128)(2,1)}, bf16[4,32,1152]{2,1,0:T(8,128)(2,1)S(1)}, u32[]{:S(2)}, u32[]{:S(2)}) %collective-permute-start.2) | collective-permute-done | bytes 294944 | tf_op jit(solution)/shard_map/ppermute | solution.py:143
  67.3 25.2 %all-gather.6.cloned.1.call-done = bf16[8,304,1152]{2,1,0:T(8,128)(2,1)} async-done(((bf16[1,304,1152]{2,1,0:T(8,128)(2,1)}), bf16[8,304,1152]{2,1,0:T(8,128)(2,1)}) %all-gather.6.cloned.1.call-update) | async-done | bytes 5603344 | tf_op jit(solution)/shard_map/all_gather | solution.py:207
  94.8 52.9 %all-gather.8.cloned.1.call-done = bf16[2176,1152]{1,0:T(8,128)(2,1)} async-done(((bf16[272,1152]{1,0:T(8,128)(2,1)}), bf16[2176,1152]{1,0:T(8,128)(2,1)}) %all-gather.8.cloned.1.call-update) | async-done | bytes 5013520 | tf_op jit(solution)/shard_map/all_gather | solution.py:207
  152.6 5.0 fusion.115
  166.7 15.7 %collective-permute-done.9 = bf16[4,32,1152]{2,1,0:T(8,128)(2,1)S(1)} collective-permute-done((bf16[4,32,1152]{2,1,0:T(8,128)(2,1)}, bf16[4,32,1152]{2,1,0:T(8,128)(2,1)S(1)}, u32[]{:S(2)}, u32[]{:S(2)}) %collective-permute-start.9) | collective-permute-done | bytes 294944 | tf_op jit(solution)/shard_map/ppermute | solution.py:143
  183.6 13.9 %collective-permute-done.10 = bf16[4,32,1152]{2,1,0:T(8,128)(2,1)S(1)} collective-permute-done((bf16[4,32,1152]{2,1,0:T(8,128)(2,1)}, bf16[4,32,1152]{2,1,0:T(8,128)(2,1)S(1)}, u32[]{:S(2)}, u32[]{:S(2)}) %collective-permute-start.10) | collective-permute-done | bytes 294944 | tf_op jit(solution)/shard_map/ppermute | solution.py:143
  199.6 11.9 %collective-permute-done.11 = bf16[4,32,1152]{2,1,0:T(8,128)(2,1)S(1)} collective-permute-done((bf16[4,32,1152]{2,1,0:T(8,128)(2,1)S(1)}, bf16[4,32,1152]{2,1,0:T(8,128)(2,1)S(1)}, u32[]{:S(2)}, u32[]{:S(2)}) %collective-permute-start.11) | collective-permute-done | bytes 294944 | tf_op jit(solution)/shard_map/ppermute | solution.py:143
  212.2 14.7 %collective-permute-done.12 = bf16[4,32,1152]{2,1,0:T(8,128)(2,1)S(1)} collective-permute-done((bf16[4,32,1152]{2,1,0:T(8,128)(2,1)S(1)}, bf16[4,32,1152]{2,1,0:T(8,128)(2,1)S(1)}, u32[]{:S(2)}, u32[]{:S(2)}) %collective-permute-start.12) | collective-permute-done | bytes 294944 | tf_op jit(solution)/shard_map/ppermute | solution.py:143
  231.3 4.1 fusion.116
  241.1 11.7 %add_convert_fusion.q_ref.k_ref.v_ref = bf16[1024,3456]{1,0:T(8,128)(2,1)} fusion(bf16[1024,1152]{1,0:T(8,128)(2,1)S(1)} %copy-done.21, bf16[3456,1152]{1,0:T(8,128)(2,1)S(1)} %constant_dynamic-update-slice_fusion, f32[3456]{0:T(1024)S(1)} %convert_element_type.208), kind=kOutput, calls=%fused_computation.16 | convolution fusion | flops 8160804864 | bytes 17413632 | tf_op jit(solution)/shard_map/dot_general | solution.py:39
  252.7 32.3 %attn_fwd.1 = bf16[1024,1152]{1,0:T(8,128)(2,1)} custom-call(bf16[1024,3456]{1,0:T(8,128)(2,1)} %add_convert_fusion.q_ref.k_ref.v_ref, bf16[1024,3456]{1,0:T(8,128)(2,1)} %add_convert_fusion.q_ref.k_ref.v_ref, bf16[1024,3456]{1,0:T(8,128)(2,1)} %add_convert_fusion.q_ref.k_ref.v_ref), custom_call_target="tpu_custom_call" | custom-call | flops 17179869184 | bytes 9437184 | tf_op jit(solution)/shard_map/attn_fwd/pallas_call | solution.py:101
  285.0 6.0 convert_reduce_fusion.5
  291.9 13.2 %fusion.19 = (bf16[2176,1024]{0,1:T(8,128)(2,1)}, bf16[1024,2176]{1,0:T(8,128)(2,1)}) fusion(f32[2176]{0:T(1024)S(1)} %reshape.510, bf16[2176,1152]{1,0:T(8,128)(2,1)} %bitcast.54, bf16[1024,1152]{1,0:T(8,128)(2,1)S(1)} %get-tuple-element.145, f32[1152]{0:T(1024)S(1)} %copy-done.49, f32[1152]{0:T(1024)S(1)} %copy-done.42, f32[1024]{0:T(1024)S(1)} %fusion.98, ...), kind=kOutput, calls=%fused_computation.34 | convolution fusion | flops 5167644672 | bytes 16311808 | tf_op jit(solution)/shard_map/dot_general | solution.py:39
  305.1 6.6 copy.131
  311.7 10.9 %fusion.118 = f32[2,4,272,1152]{3,2,1,0:T(8,128)} fusion(bf16[2,4,272,1024]{3,2,1,0:T(8,128)(2,1)} %bitcast.445, bf16[1024,1152,1,1]{1,0,3,2:T(8,128)(2,1)} %bitcast.425), kind=kOutput, calls=%fused_computation.316 | convolution fusion | flops 5133828096 | bytes 16842752 | tf_op jit(solution)/shard_map/dot_general | solution.py:43
  324.8 13.5 %fusion.23 = (bf16[1024,2176]{1,0:T(8,128)(2,1)}, bf16[1024,2176]{1,0:T(8,128)(2,1)}) fusion(f32[2176]{0:T(1024)S(1)} %reshape.509, bf16[2176,1152]{1,0:T(8,128)(2,1)} %all-gather.8.cloned.1.call-done, bf16[1024,1152]{1,0:T(8,128)(2,1)S(1)} %copy-done.5, f32[1152]{0:T(1024)S(1)} %copy-done.49, f32[1152]{0:T(1024)S(1)} %copy-done.42, f32[1024]{0:T(1024)S(1)} %fusion.98, ...), kind=kOutput, calls=%fused_computation.38 | convolution fusion | flops 5167644672 | bytes 16311808 | tf_op jit(solution)/shard_map/dot_general | solution.py:39
  338.3 6.5 copy.132
  344.8 8.5 %fusion.119 = f32[2,4,272,1152]{3,2,1,0:T(8,128)S(1)} fusion(bf16[2,4,272,1024]{3,2,1,0:T(8,128)(2,1)} %bitcast.446, bf16[1024,1152,1,1]{1,0,3,2:T(8,128)(2,1)} %bitcast.426), kind=kOutput, calls=%fused_computation.317 | convolution fusion | flops 5133828096 | bytes 16842752 | tf_op jit(solution)/shard_map/dot_general | solution.py:43
  353.3 9.1 %fusion.75 = (f32[2,272,1152]{2,1,0:T(8,128)}, f32[2,272,1152]{2,1,0:T(8,128)}) fusion(f32[2,4,272,1152]{3,2,1,0:T(8,128)} %collective-permute-done.16, s32[]{:T(128)S(6)} %select_n.385, f32[2,4,272,1152]{3,2,1,0:T(8,128)S(1)} %fusion.119, s32[]{:T(128)S(6)} %select_n.383), kind=kLoop, calls=%fused_computation.124 | loop fusion | flops 1253376 | bytes 15040520 | tf_op jit(solution)/shard_map/add | solution.py:192
  362.4 13.6 %convert_reduce_fusion.1 = (f32[2176]{0:T(1024)}, bf16[1024,2176]{1,0:T(8,128)(2,1)S(1)}) fusion(bf16[1024,2176]{1,0:T(8,128)(2,1)} %get-tuple-element.149, bf16[1024,1152]{1,0:T(8,128)(2,1)S(1)} %bitcast.428, bf16[2176,1152]{1,0:T(8,128)(2,1)} %bitcast.64), kind=kOutput, calls=%fused_computation.47 | convolution fusion | flops 5189531648 | bytes 16294400 | tf_op jit(solution)/shard_map/dot_general | solution.py:39
  376.0 9.5 %fusion.108 = f32[2176,1152]{1,0:T(8,128)} fusion(bf16[1024,2176]{1,0:T(8,128)(2,1)S(1)} %get-tuple-element.33, bf16[1024,1152]{1,0:T(8,128)(2,1)S(1)} %copy-done.5, f32[1152]{0:T(1024)S(1)} %copy-done.49, f32[1152]{0:T(1024)S(1)} %copy-done.42, f32[1024]{0:T(1024)S(1)} %fusion.98, f32[1024]{0:T(1024)S(1)} %broadcast_multiply_fusion.1), kind=kOutput, calls=%fused_computation.310 | convolution fusion | flops 5140905984 | bytes 16860160 | tf_op jit(solution)/shard_map/dot_general | solution.py:43
  385.9 13.5 %convert_reduce_fusion.2 = (f32[2176]{0:T(1024)S(1)}, bf16[1024,2176]{1,0:T(8,128)(2,1)S(1)}) fusion(bf16[1024,2176]{1,0:T(8,128)(2,1)} %get-tuple-element.147, bf16[1024,1152]{1,0:T(8,128)(2,1)} %bitcast.427, bf16[2176,1152]{1,0:T(8,128)(2,1)} %all-gather.10.cloned.1.call-done), kind=kOutput, calls=%fused_computation.48 | convolution fusion | flops 5189531648 | bytes 16294400 | tf_op jit(solution)/shard_map/dot_general | solution.py:39
  399.4 6.2 fusion.106
  405.6 8.3 fusion.73
  415.6 9.5 %fusion.120 = f32[1024,1152]{1,0:T(8,128)S(1)} fusion(bf16[1024,2176]{1,0:T(8,128)(2,1)} %copy-done.50, bf16[2176,1152]{1,0:T(8,128)(2,1)} %all-gather.8.cloned.1.call-done), kind=kOutput, calls=%fused_computation.318 | convolution fusion | flops 5133828096 | bytes 14188544 | tf_op jit(solution)/shard_map/dot_general | solution.py:41
  425.1 9.8 %convert_reduce_fusion.4 = (f32[1152]{0:T(1024)S(1)}, f32[1024]{0:T(1024)S(1)}, bf16[1024,1152]{1,0:T(8,128)(2,1)S(1)}) fusion(f32[1152]{0:T(1024)S(1)} %copy-done.42, f32[1024]{0:T(1024)S(1)} %broadcast_multiply_fusion.1, bf16[1024,1152]{1,0:T(8,128)(2,1)S(1)} %copy-done.5, f32[1024,1152]{1,0:T(8,128)S(1)} %fusion.120, bf16[1024,2176]{1,0:T(8,128)(2,1)} %copy-done.51, ...), kind=kOutput, calls=%fused_computation.57 | convolution fusion | flops 5144442880 | bytes 18924544 | tf_op jit(solution)/shard_map/dot_general | solution.py:41
  445.4 4.2 fusion.72
  451.4 4.8 convolution_convert_fusion.3.do_ref
  461.8 40.6 %attn_bwd.1 = bf16[1024,3456]{1,0:T(8,128)(2,1)} custom-call(bf16[1024,3456]{1,0:T(8,128)(2,1)} %add_convert_fusion.q_ref.k_ref.v_ref, bf16[1024,3456]{1,0:T(8,128)(2,1)} %add_convert_fusion.q_ref.k_ref.v_ref, bf16[1024,3456]{1,0:T(8,128)(2,1)} %add_convert_fusion.q_ref.k_ref.v_ref, bf16[1024,1152]{1,0:T(8,128)(2,1)} %convolution_convert_fusion.3.do_ref), custom_call_target="tpu_custom_call" | custom-call | flops 42949672960 | bytes 16515072 | tf_op jit(solution)/shard_map/attn_bwd/pallas_call | solution.py:110
  504.8 10.3 %copy.145 = bf16[3456,1024]{1,0:T(8,128)(2,1)} copy(bf16[3456,1024]{0,1:T(8,128)(2,1)} %bitcast.418) | data formatting | bytes 14155776 | tf_op jit(solution)/shard_map/dot_general | solution.py:43
  515.1 12.9 %fusion.121 = f32[3,2,4,144,1152]{4,3,2,1,0:T(8,128)S(1)} fusion(bf16[3,2,4,144,1024]{4,3,2,1,0:T(8,128)(2,1)} %bitcast.432, bf16[1024,1152,1,1,1]{1,0,4,3,2:T(8,128)(2,1)} %bitcast.452), kind=kOutput, calls=%fused_computation.319 | convolution fusion | flops 8153726976 | bytes 25362432 | tf_op jit(solution)/shard_map/dot_general | solution.py:43
  528.1 6.2 fusion.114
  541.6 8.0 collective-permute-done.45
  550.5 15.1 %convolution_convert_fusion.2 = bf16[1024,1152]{1,0:T(8,128)(2,1)} fusion(bf16[1024,3456]{1,0:T(8,128)(2,1)} %attn_bwd.1, bf16[3456,1152]{1,0:T(8,128)(2,1)} %copy-done.29), kind=kOutput, calls=%fused_computation.108 | convolution fusion | flops 8154906624 | bytes 17399808 | tf_op jit(solution)/shard_map/dot_general | solution.py:41
  566.7 4.0 convert_reduce_fusion
  573.5 85.7 %collective-permute-done.46 = f32[144,1152]{1,0:T(8,128)S(1)} collective-permute-done((f32[144,1152]{1,0:T(8,128)}, f32[144,1152]{1,0:T(8,128)S(1)}, u32[]{:S(2)}, u32[]{:S(2)}) %collective-permute-start.46) | collective-permute-done | bytes 663584 | tf_op jit(solution)/shard_map/ppermute | solution.py:143
  663.0 8.7 %fusion.78 = (bf16[2,272,1152]{2,1,0:T(8,128)(2,1)}, bf16[2,272,1152]{2,1,0:T(8,128)(2,1)S(1)}) fusion(f32[2,272,1152]{2,1,0:T(8,128)} %collective-permute-done.50, f32[2,272,1152]{2,1,0:T(8,128)} %collective-permute-done.49, f32[2,4,272,1152]{3,2,1,0:T(8,128)} %collective-permute-done.16, s32[]{:T(128)S(6)} %select_n.438, ...), kind=kLoop, calls=%fused_computation.129 | loop fusion | flops 5013504 | bytes 22560772 | tf_op jit(solution)/shard_map/convert.6
  672.9 11.3 %collective-permute-done.43 = f32[3,144,1152]{2,1,0:T(8,128)} collective-permute-done((f32[3,144,1152]{2,1,0:T(8,128)S(1)}, f32[3,144,1152]{2,1,0:T(8,128)}, u32[]{:S(2)}, u32[]{:S(2)}) %collective-permute-start.43) | collective-permute-done | bytes 1990688 | tf_op jit(solution)/shard_map/ppermute | solution.py:143
  684.2 6.3 fusion.81
  695.1 9.7 %fusion.122 = f32[1024,1152]{1,0:T(8,128)S(1)} fusion(bf16[1024,2176]{1,0:T(8,128)(2,1)} %get-tuple-element.38, bf16[2176,1152]{1,0:T(8,128)(2,1)} %all-gather.10.cloned.1.call-done), kind=kOutput, calls=%fused_computation.320 | convolution fusion | flops 5133828096 | bytes 14188544 | tf_op jit(solution)/shard_map/dot_general | solution.py:41
  704.8 11.0 %fusion.47 = bf16[1024,1152]{1,0:T(8,128)(2,1)S(1)} fusion(bf16[1024,1152]{1,0:T(8,128)(2,1)S(1)} %copy-done.6, f32[1024,1152]{1,0:T(8,128)S(1)} %fusion.122, bf16[2176,1152]{1,0:T(8,128)(2,1)} %bitcast.64, bf16[1024,2176]{1,0:T(8,128)(2,1)S(1)} %bitcast.477, f32[1152]{0:T(1024)S(1)} %convert_element_type.241), kind=kOutput, calls=%fused_computation.82 | convolution fusion | flops 5162008576 | bytes 18911744 | tf_op jit(solution)/shard_map/dot_general | solution.py:41
  731.9 3.7 collective-permute-done.25
  749.4 3.7 collective-permute-done.24
  768.2 3.8 collective-permute-done.35
  773.4 5.0 collective-permute-done.31
  782.7 39.0 %collective-permute-done.44 = f32[3,144,1152]{2,1,0:T(8,128)S(1)} collective-permute-done((f32[3,144,1152]{2,1,0:T(8,128)S(1)}, f32[3,144,1152]{2,1,0:T(8,128)S(1)}, u32[]{:S(2)}, u32[]{:S(2)}) %collective-permute-start.44) | collective-permute-done | bytes 1990688 | tf_op jit(solution)/shard_map/ppermute | solution.py:143
  (336 shorter events, 155.9 us)
Async XLA Ops:
  7.2 85.3 %all-gather.6.cloned.1.call-start = ((), (), s32[]{:S(2)}) async-start(), calls=%async_computation | async-start | bytes 6303744 | tf_op jit(solution)/shard_map/all_gather | solution.py:207
  12.1 135.7 %all-gather.8.cloned.1.call-start = ((), (), s32[]{:S(2)}) async-start(), calls=%async_computation.1 | async-start | bytes 5640192 | tf_op jit(solution)/shard_map/all_gather | solution.py:207
  14.5 309.3 %all-gather.10.cloned.1.call-start = ((), (), s32[]{:S(2)}) async-start(), calls=%async_computation.2 | async-start | bytes 5640192 | tf_op jit(solution)/shard_map/all_gather | solution.py:207
  17.1 47.2 %collective-permute-start.6 = (bf16[4,32,1152]{2,1,0:T(8,128)(2,1)S(1)}, bf16[4,32,1152]{2,1,0:T(8,128)(2,1)}, u32[]{:S(2)}, u32[]{:S(2)}) collective-permute-start(bf16[4,32,1152]{2,1,0:T(8,128)(2,1)S(1)} %get-tuple-element.122), channel_id=1, source_target_pairs={{0,7},{1,6},{2,5},{3,4},{4,3},{5,2},{6,1},{7,0},{8,15},{9,14},{10,... | collective-permute-start | bytes 884744 | tf_op jit(solution)/shard_map/ppermute | solution.py:143
  20.7 42.6 %collective-permute-start.5 = (bf16[4,32,1152]{2,1,0:T(8,128)(2,1)S(1)}, bf16[4,32,1152]{2,1,0:T(8,128)(2,1)}, u32[]{:S(2)}, u32[]{:S(2)}) collective-permute-start(bf16[4,32,1152]{2,1,0:T(8,128)(2,1)S(1)} %get-tuple-element.123), channel_id=1, source_target_pairs={{0,6},{1,7},{2,4},{3,5},{4,2},{5,3},{6,0},{7,1},{8,14},{9,15},{10,... | collective-permute-start | bytes 884744 | tf_op jit(solution)/shard_map/ppermute | solution.py:143
  21.3 41.0 %collective-permute-start.4 = (bf16[4,32,1152]{2,1,0:T(8,128)(2,1)S(1)}, bf16[4,32,1152]{2,1,0:T(8,128)(2,1)}, u32[]{:S(2)}, u32[]{:S(2)}) collective-permute-start(bf16[4,32,1152]{2,1,0:T(8,128)(2,1)S(1)} %get-tuple-element.124), channel_id=1, source_target_pairs={{0,5},{1,4},{2,7},{3,6},{4,1},{5,0},{6,3},{7,2},{8,13},{9,12},{10,... | collective-permute-start | bytes 884744 | tf_op jit(solution)/shard_map/ppermute | solution.py:143
  22.7 38.6 %collective-permute-start.3 = (bf16[4,32,1152]{2,1,0:T(8,128)(2,1)S(1)}, bf16[4,32,1152]{2,1,0:T(8,128)(2,1)}, u32[]{:S(2)}, u32[]{:S(2)}) collective-permute-start(bf16[4,32,1152]{2,1,0:T(8,128)(2,1)S(1)} %get-tuple-element.125), channel_id=1, source_target_pairs={{0,4},{1,5},{2,6},{3,7},{4,0},{5,1},{6,2},{7,3},{8,12},{9,13},{10,... | collective-permute-start | bytes 884744 | tf_op jit(solution)/shard_map/ppermute | solution.py:143
  25.8 20.9 %collective-permute-start.1 = (bf16[4,32,1152]{2,1,0:T(8,128)(2,1)}, bf16[4,32,1152]{2,1,0:T(8,128)(2,1)S(1)}, u32[]{:S(2)}, u32[]{:S(2)}) collective-permute-start(bf16[4,32,1152]{2,1,0:T(8,128)(2,1)} %get-tuple-element.127), channel_id=1, source_target_pairs={{0,2},{1,3},{2,0},{3,1},{4,6},{5,7},{6,4},{7,5},{8,10},{9,11},{10,... | collective-permute-start | bytes 884744 | tf_op jit(solution)/shard_map/ppermute | solution.py:143
  46.7 14.5 %collective-permute-start.2 = (bf16[4,32,1152]{2,1,0:T(8,128)(2,1)}, bf16[4,32,1152]{2,1,0:T(8,128)(2,1)S(1)}, u32[]{:S(2)}, u32[]{:S(2)}) collective-permute-start(bf16[4,32,1152]{2,1,0:T(8,128)(2,1)} %get-tuple-element.126), channel_id=1, source_target_pairs={{0,3},{1,2},{2,1},{3,0},{4,7},{5,6},{6,5},{7,4},{8,11},{9,10},{10,... | collective-permute-start | bytes 884744 | tf_op jit(solution)/shard_map/ppermute | solution.py:143
  92.5 136.7 %collective-permute-start.7 = (bf16[2,4,304,1152]{3,2,1,0:T(8,128)(2,1)}, bf16[2,4,304,1152]{3,2,1,0:T(8,128)(2,1)}, u32[]{:S(2)}, u32[]{:S(2)}) collective-permute-start(bf16[2,4,304,1152]{3,2,1,0:T(8,128)(2,1)} %bitcast.439), channel_id=1, source_target_pairs={{0,1},{1,0},{2,3},{3,2},{4,5},{5,4},{6,7},{7,6},{8,9},{9,8},{10,11... | collective-permute-start | bytes 16809992 | tf_op jit(solution)/shard_map/ppermute | solution.py:143
  147.7 144.1 %collective-permute-start.15 = (bf16[2,4,272,1152]{3,2,1,0:T(8,128)(2,1)}, bf16[2,4,272,1152]{3,2,1,0:T(8,128)(2,1)}, u32[]{:S(2)}, u32[]{:S(2)}) collective-permute-start(bf16[2,4,272,1152]{3,2,1,0:T(8,128)(2,1)} %bitcast.475), channel_id=1, source_target_pairs={{0,1},{1,0},{2,3},{3,2},{4,5},{5,4},{6,7},{7,6},{8,9},{9,8},{10,11... | collective-permute-start | bytes 15040520 | tf_op jit(solution)/shard_map/ppermute | solution.py:143
  150.3 13.2 %collective-permute-start.8 = (bf16[4,32,1152]{2,1,0:T(8,128)(2,1)}, bf16[4,32,1152]{2,1,0:T(8,128)(2,1)}, u32[]{:S(2)}, u32[]{:S(2)}) collective-permute-start(bf16[4,32,1152]{2,1,0:T(8,128)(2,1)} %get-tuple-element.121), channel_id=1, source_target_pairs={{0,1},{1,0},{2,3},{3,2},{4,5},{5,4},{6,7},{7,6},{8,9},{9,8},{10,11... | collective-permute-start | bytes 884744 | tf_op jit(solution)/shard_map/ppermute | solution.py:143
  158.5 69.9 %collective-permute-start.14 = (bf16[4,32,1152]{2,1,0:T(8,128)(2,1)S(1)}, bf16[4,32,1152]{2,1,0:T(8,128)(2,1)S(1)}, u32[]{:S(2)}, u32[]{:S(2)}) collective-permute-start(bf16[4,32,1152]{2,1,0:T(8,128)(2,1)S(1)} %get-tuple-element.115), channel_id=1, source_target_pairs={{0,7},{1,6},{2,5},{3,4},{4,3},{5,2},{6,1},{7,0},{8,15},{9,14},{10,... | collective-permute-start | bytes 884744 | tf_op jit(solution)/shard_map/ppermute | solution.py:143
  160.5 67.2 %collective-permute-start.13 = (bf16[4,32,1152]{2,1,0:T(8,128)(2,1)S(1)}, bf16[4,32,1152]{2,1,0:T(8,128)(2,1)S(1)}, u32[]{:S(2)}, u32[]{:S(2)}) collective-permute-start(bf16[4,32,1152]{2,1,0:T(8,128)(2,1)S(1)} %get-tuple-element.116), channel_id=1, source_target_pairs={{0,6},{1,7},{2,4},{3,5},{4,2},{5,3},{6,0},{7,1},{8,14},{9,15},{10,... | collective-permute-start | bytes 884744 | tf_op jit(solution)/shard_map/ppermute | solution.py:143
  163.6 18.9 %collective-permute-start.9 = (bf16[4,32,1152]{2,1,0:T(8,128)(2,1)}, bf16[4,32,1152]{2,1,0:T(8,128)(2,1)S(1)}, u32[]{:S(2)}, u32[]{:S(2)}) collective-permute-start(bf16[4,32,1152]{2,1,0:T(8,128)(2,1)} %get-tuple-element.120), channel_id=1, source_target_pairs={{0,2},{1,3},{2,0},{3,1},{4,6},{5,7},{6,4},{7,5},{8,10},{9,11},{10,... | collective-permute-start | bytes 884744 | tf_op jit(solution)/shard_map/ppermute | solution.py:143
  182.5 15.0 %collective-permute-start.10 = (bf16[4,32,1152]{2,1,0:T(8,128)(2,1)}, bf16[4,32,1152]{2,1,0:T(8,128)(2,1)S(1)}, u32[]{:S(2)}, u32[]{:S(2)}) collective-permute-start(bf16[4,32,1152]{2,1,0:T(8,128)(2,1)} %get-tuple-element.119), channel_id=1, source_target_pairs={{0,3},{1,2},{2,1},{3,0},{4,7},{5,6},{6,5},{7,4},{8,11},{9,10},{10,... | collective-permute-start | bytes 884744 | tf_op jit(solution)/shard_map/ppermute | solution.py:143
  197.5 14.0 %collective-permute-start.11 = (bf16[4,32,1152]{2,1,0:T(8,128)(2,1)S(1)}, bf16[4,32,1152]{2,1,0:T(8,128)(2,1)S(1)}, u32[]{:S(2)}, u32[]{:S(2)}) collective-permute-start(bf16[4,32,1152]{2,1,0:T(8,128)(2,1)S(1)} %get-tuple-element.118), channel_id=1, source_target_pairs={{0,4},{1,5},{2,6},{3,7},{4,0},{5,1},{6,2},{7,3},{8,12},{9,13},{10,... | collective-permute-start | bytes 884744 | tf_op jit(solution)/shard_map/ppermute | solution.py:143
  211.5 15.4 %collective-permute-start.12 = (bf16[4,32,1152]{2,1,0:T(8,128)(2,1)S(1)}, bf16[4,32,1152]{2,1,0:T(8,128)(2,1)S(1)}, u32[]{:S(2)}, u32[]{:S(2)}) collective-permute-start(bf16[4,32,1152]{2,1,0:T(8,128)(2,1)S(1)} %get-tuple-element.117), channel_id=1, source_target_pairs={{0,5},{1,4},{2,7},{3,6},{4,1},{5,0},{6,3},{7,2},{8,13},{9,12},{10,... | collective-permute-start | bytes 884744 | tf_op jit(solution)/shard_map/ppermute | solution.py:143
  322.6 30.7 %collective-permute-start.16 = (f32[2,4,272,1152]{3,2,1,0:T(8,128)}, f32[2,4,272,1152]{3,2,1,0:T(8,128)}, u32[]{:S(2)}, u32[]{:S(2)}) collective-permute-start(f32[2,4,272,1152]{3,2,1,0:T(8,128)} %fusion.118), channel_id=1, source_target_pairs={{0,1},{1,0},{2,3},{3,2},{4,5},{5,4},{6,7},{7,6},{8,9},{9,8},{10,11... | collective-permute-start | bytes 30081032 | tf_op jit(solution)/shard_map/ppermute | solution.py:143
  323.8 38.7 %collective-permute-start.17 = (bf16[2,4,272,1152]{3,2,1,0:T(8,128)(2,1)}, bf16[2,4,272,1152]{3,2,1,0:T(8,128)(2,1)}, u32[]{:S(2)}, u32[]{:S(2)}) collective-permute-start(bf16[2,4,272,1152]{3,2,1,0:T(8,128)(2,1)} %bitcast.474), channel_id=1, source_target_pairs={{0,1},{1,0},{2,3},{3,2},{4,5},{5,4},{6,7},{7,6},{8,9},{9,8},{10,11... | collective-permute-start | bytes 15040520 | tf_op jit(solution)/shard_map/ppermute | solution.py:143
  385.5 20.1 %collective-permute-start.18 = (f32[2,4,272,1152]{3,2,1,0:T(8,128)}, f32[2,4,272,1152]{3,2,1,0:T(8,128)}, u32[]{:S(2)}, u32[]{:S(2)}) collective-permute-start(f32[2,4,272,1152]{3,2,1,0:T(8,128)} %bitcast.65), channel_id=1, source_target_pairs={{0,1},{1,0},{2,3},{3,2},{4,5},{5,4},{6,7},{7,6},{8,9},{9,8},{10,11... | collective-permute-start | bytes 30081032 | tf_op jit(solution)/shard_map/ppermute | solution.py:143
  385.9 59.5 %collective-permute-start.19 = (f32[2,272,1152]{2,1,0:T(8,128)}, f32[2,272,1152]{2,1,0:T(8,128)S(1)}, u32[]{:S(2)}, u32[]{:S(2)}) collective-permute-start(f32[2,272,1152]{2,1,0:T(8,128)} %get-tuple-element.86), channel_id=1, source_target_pairs={{0,2},{1,5},{2,0},{3,7},{4,6},{5,1},{6,4},{7,3},{8,10},{9,13},{10,... | collective-permute-start | bytes 7520264 | tf_op jit(solution)/shard_map/ppermute | solution.py:143
  413.9 42.3 %collective-permute-start.21 = (f32[2,272,1152]{2,1,0:T(8,128)S(1)}, f32[2,272,1152]{2,1,0:T(8,128)S(1)}, u32[]{:S(2)}, u32[]{:S(2)}) collective-permute-start(f32[2,272,1152]{2,1,0:T(8,128)S(1)} %get-tuple-element.84), channel_id=1, source_target_pairs={{0,2},{1,5},{2,0},{3,7},{4,6},{5,1},{6,4},{7,3},{8,10},{9,13},{10,... | collective-permute-start | bytes 7520264 | tf_op jit(solution)/shard_map/ppermute | solution.py:143
  442.6 17.1 %collective-permute-start.20 = (f32[4,144,1152]{2,1,0:T(8,128)S(1)}, f32[4,144,1152]{2,1,0:T(8,128)S(1)}, u32[]{:S(2)}, u32[]{:S(2)}) collective-permute-start(f32[4,144,1152]{2,1,0:T(8,128)S(1)} %bitcast.447), channel_id=1, source_target_pairs={{0,1},{1,0},{2,3},{3,2},{4,5},{5,4},{6,7},{7,6},{8,9},{9,8},{10,11... | collective-permute-start | bytes 7962632 | tf_op jit(solution)/shard_map/ppermute | solution.py:143
  461.4 41.0 %collective-permute-start.22 = (f32[144,1152]{1,0:T(8,128)}, f32[144,1152]{1,0:T(8,128)}, u32[]{:S(2)}, u32[]{:S(2)}) collective-permute-start(f32[144,1152]{1,0:T(8,128)} %get-tuple-element.100), channel_id=1, source_target_pairs={{0,2},{1,5},{2,0},{3,7},{4,6},{5,1},{6,4},{7,3},{8,10},{9,13},{10,... | collective-permute-start | bytes 1990664 | tf_op jit(solution)/shard_map/ppermute | solution.py:143
  534.3 31.3 %collective-permute-start.23 = (f32[3,4,144,1152]{3,2,1,0:T(8,128)}, f32[3,4,144,1152]{3,2,1,0:T(8,128)}, u32[]{:S(2)}, u32[]{:S(2)}) collective-permute-start(f32[3,4,144,1152]{3,2,1,0:T(8,128)} %get-tuple-element.90), channel_id=1, source_target_pairs={{0,1},{1,0},{2,3},{3,2},{4,5},{5,4},{6,7},{7,6},{8,9},{9,8},{10,11... | collective-permute-start | bytes 23887880 | tf_op jit(solution)/shard_map/ppermute | solution.py:143
  534.9 14.6 %collective-permute-start.45 = (f32[144,1152]{1,0:T(8,128)S(1)}, f32[144,1152]{1,0:T(8,128)}, u32[]{:S(2)}, u32[]{:S(2)}) collective-permute-start(f32[144,1152]{1,0:T(8,128)S(1)} %get-tuple-element.99), channel_id=1, source_target_pairs={{0,2},{1,5},{2,0},{3,7},{4,6},{5,1},{6,4},{7,3},{8,10},{9,13},{10,... | collective-permute-start | bytes 1990664 | tf_op jit(solution)/shard_map/ppermute | solution.py:143
  538.1 125.0 %collective-permute-start.49 = (f32[2,272,1152]{2,1,0:T(8,128)}, f32[2,272,1152]{2,1,0:T(8,128)}, u32[]{:S(2)}, u32[]{:S(2)}) collective-permute-start(f32[2,272,1152]{2,1,0:T(8,128)} %get-tuple-element.85), channel_id=1, source_target_pairs={{0,2},{1,5},{2,0},{3,7},{4,6},{5,1},{6,4},{7,3},{8,10},{9,13},{10,... | collective-permute-start | bytes 7520264 | tf_op jit(solution)/shard_map/ppermute | solution.py:143
  539.5 123.5 %collective-permute-start.50 = (f32[2,272,1152]{2,1,0:T(8,128)}, f32[2,272,1152]{2,1,0:T(8,128)}, u32[]{:S(2)}, u32[]{:S(2)}) collective-permute-start(f32[2,272,1152]{2,1,0:T(8,128)} %fusion.72), channel_id=1, source_target_pairs={{0,4},{1,3},{2,6},{3,1},{4,0},{5,7},{6,2},{7,5},{8,12},{9,11},{10,... | collective-permute-start | bytes 7520264 | tf_op jit(solution)/shard_map/ppermute | solution.py:143
  540.5 122.5 %collective-permute-start.47 = (f32[2,272,1152]{2,1,0:T(8,128)}, f32[2,272,1152]{2,1,0:T(8,128)}, u32[]{:S(2)}, u32[]{:S(2)}) collective-permute-start(f32[2,272,1152]{2,1,0:T(8,128)} %get-tuple-element.83), channel_id=1, source_target_pairs={{0,2},{1,5},{2,0},{3,7},{4,6},{5,1},{6,4},{7,3},{8,10},{9,13},{10,... | collective-permute-start | bytes 7520264 | tf_op jit(solution)/shard_map/ppermute | solution.py:143
  549.5 113.5 %collective-permute-start.48 = (f32[2,272,1152]{2,1,0:T(8,128)}, f32[2,272,1152]{2,1,0:T(8,128)}, u32[]{:S(2)}, u32[]{:S(2)}) collective-permute-start(f32[2,272,1152]{2,1,0:T(8,128)} %fusion.70), channel_id=1, source_target_pairs={{0,4},{1,3},{2,6},{3,1},{4,0},{5,7},{6,2},{7,5},{8,12},{9,11},{10,... | collective-permute-start | bytes 7520264 | tf_op jit(solution)/shard_map/ppermute | solution.py:143
  565.6 93.6 %collective-permute-start.46 = (f32[144,1152]{1,0:T(8,128)}, f32[144,1152]{1,0:T(8,128)S(1)}, u32[]{:S(2)}, u32[]{:S(2)}) collective-permute-start(f32[144,1152]{1,0:T(8,128)} %bitcast_add_fusion.14), channel_id=1, source_target_pairs={{0,4},{1,3},{2,6},{3,1},{4,0},{5,7},{6,2},{7,5},{8,12},{9,11},{10,... | collective-permute-start | bytes 1990664 | tf_op jit(solution)/shard_map/ppermute | solution.py:143
  659.2 25.0 %collective-permute-start.43 = (f32[3,144,1152]{2,1,0:T(8,128)S(1)}, f32[3,144,1152]{2,1,0:T(8,128)}, u32[]{:S(2)}, u32[]{:S(2)}) collective-permute-start(f32[3,144,1152]{2,1,0:T(8,128)S(1)} %bitcast_add_fusion.12), channel_id=1, source_target_pairs={{0,2},{1,5},{2,0},{3,7},{4,6},{5,1},{6,4},{7,3},{8,10},{9,13},{10,... | collective-permute-start | bytes 5971976 | tf_op jit(solution)/shard_map/ppermute | solution.py:143
  695.0 23.1 %collective-permute-start.38 = (f32[4,8,1152]{2,1,0:T(8,128)S(1)}, f32[4,8,1152]{2,1,0:T(8,128)S(1)}, u32[]{:S(2)}, u32[]{:S(2)}) collective-permute-start(f32[4,8,1152]{2,1,0:T(8,128)S(1)} %get-tuple-element.135), channel_id=1, source_target_pairs={{0,1},{1,0},{2,3},{3,2},{4,5},{5,4},{6,7},{7,6},{8,9},{9,8},{10,11... | collective-permute-start | bytes 442376 | tf_op jit(solution)/shard_map/ppermute | solution.py:143
  726.5 15.4 %collective-permute-start.29 = (bf16[4,32,1152]{2,1,0:T(8,128)(2,1)}, bf16[4,32,1152]{2,1,0:T(8,128)(2,1)S(1)}, u32[]{:S(2)}, u32[]{:S(2)}) collective-permute-start(bf16[4,32,1152]{2,1,0:T(8,128)(2,1)} %get-tuple-element.110), channel_id=1, source_target_pairs={{0,2},{1,3},{2,0},{3,1},{4,6},{5,7},{6,4},{7,5},{8,10},{9,11},{10,... | collective-permute-start | bytes 884744 | tf_op jit(solution)/shard_map/ppermute | solution.py:143
  727.0 19.8 %collective-permute-start.28 = (bf16[4,32,1152]{2,1,0:T(8,128)(2,1)}, bf16[4,32,1152]{2,1,0:T(8,128)(2,1)S(1)}, u32[]{:S(2)}, u32[]{:S(2)}) collective-permute-start(bf16[4,32,1152]{2,1,0:T(8,128)(2,1)} %get-tuple-element.111), channel_id=1, source_target_pairs={{0,3},{1,2},{2,1},{3,0},{4,7},{5,6},{6,5},{7,4},{8,11},{9,10},{10,... | collective-permute-start | bytes 884744 | tf_op jit(solution)/shard_map/ppermute | solution.py:143
  728.3 19.5 %collective-permute-start.27 = (bf16[4,32,1152]{2,1,0:T(8,128)(2,1)}, bf16[4,32,1152]{2,1,0:T(8,128)(2,1)S(1)}, u32[]{:S(2)}, u32[]{:S(2)}) collective-permute-start(bf16[4,32,1152]{2,1,0:T(8,128)(2,1)} %get-tuple-element.112), channel_id=1, source_target_pairs={{0,4},{1,5},{2,6},{3,7},{4,0},{5,1},{6,2},{7,3},{8,12},{9,13},{10,... | collective-permute-start | bytes 884744 | tf_op jit(solution)/shard_map/ppermute | solution.py:143
  735.5 13.8 %collective-permute-start.26 = (bf16[4,32,1152]{2,1,0:T(8,128)(2,1)}, bf16[4,32,1152]{2,1,0:T(8,128)(2,1)S(1)}, u32[]{:S(2)}, u32[]{:S(2)}) collective-permute-start(bf16[4,32,1152]{2,1,0:T(8,128)(2,1)} %get-tuple-element.113), channel_id=1, source_target_pairs={{0,5},{1,4},{2,7},{3,6},{4,1},{5,0},{6,3},{7,2},{8,13},{9,12},{10,... | collective-permute-start | bytes 884744 | tf_op jit(solution)/shard_map/ppermute | solution.py:143
  735.5 17.6 %collective-permute-start.24 = (bf16[4,32,1152]{2,1,0:T(8,128)(2,1)}, bf16[4,32,1152]{2,1,0:T(8,128)(2,1)S(1)}, u32[]{:S(2)}, u32[]{:S(2)}) collective-permute-start(bf16[4,32,1152]{2,1,0:T(8,128)(2,1)} %get-tuple-element.114), channel_id=1, source_target_pairs={{0,7},{1,6},{2,5},{3,4},{4,3},{5,2},{6,1},{7,0},{8,15},{9,14},{10,... | collective-permute-start | bytes 884744 | tf_op jit(solution)/shard_map/ppermute | solution.py:143
  741.9 19.0 %collective-permute-start.32 = (bf16[4,32,1152]{2,1,0:T(8,128)(2,1)S(1)}, bf16[4,32,1152]{2,1,0:T(8,128)(2,1)S(1)}, u32[]{:S(2)}, u32[]{:S(2)}) collective-permute-start(bf16[4,32,1152]{2,1,0:T(8,128)(2,1)S(1)} %get-tuple-element.101), channel_id=1, source_target_pairs={{0,6},{1,7},{2,4},{3,5},{4,2},{5,3},{6,0},{7,1},{8,14},{9,15},{10,... | collective-permute-start | bytes 884744 | tf_op jit(solution)/shard_map/ppermute | solution.py:143
  746.8 14.1 %collective-permute-start.37 = (bf16[4,32,1152]{2,1,0:T(8,128)(2,1)S(1)}, bf16[4,32,1152]{2,1,0:T(8,128)(2,1)S(1)}, u32[]{:S(2)}, u32[]{:S(2)}) collective-permute-start(bf16[4,32,1152]{2,1,0:T(8,128)(2,1)S(1)} %get-tuple-element.102), channel_id=1, source_target_pairs={{0,1},{1,0},{2,3},{3,2},{4,5},{5,4},{6,7},{7,6},{8,9},{9,8},{10,11... | collective-permute-start | bytes 884744 | tf_op jit(solution)/shard_map/ppermute | solution.py:143
  747.9 18.9 %collective-permute-start.36 = (bf16[4,32,1152]{2,1,0:T(8,128)(2,1)S(1)}, bf16[4,32,1152]{2,1,0:T(8,128)(2,1)S(1)}, u32[]{:S(2)}, u32[]{:S(2)}) collective-permute-start(bf16[4,32,1152]{2,1,0:T(8,128)(2,1)S(1)} %get-tuple-element.103), channel_id=1, source_target_pairs={{0,2},{1,3},{2,0},{3,1},{4,6},{5,7},{6,4},{7,5},{8,10},{9,11},{10,... | collective-permute-start | bytes 884744 | tf_op jit(solution)/shard_map/ppermute | solution.py:143
  749.3 22.7 %collective-permute-start.35 = (bf16[4,32,1152]{2,1,0:T(8,128)(2,1)S(1)}, bf16[4,32,1152]{2,1,0:T(8,128)(2,1)S(1)}, u32[]{:S(2)}, u32[]{:S(2)}) collective-permute-start(bf16[4,32,1152]{2,1,0:T(8,128)(2,1)S(1)} %get-tuple-element.104), channel_id=1, source_target_pairs={{0,3},{1,2},{2,1},{3,0},{4,7},{5,6},{6,5},{7,4},{8,11},{9,10},{10,... | collective-permute-start | bytes 884744 | tf_op jit(solution)/shard_map/ppermute | solution.py:143
  753.1 19.9 %collective-permute-start.34 = (bf16[4,32,1152]{2,1,0:T(8,128)(2,1)S(1)}, bf16[4,32,1152]{2,1,0:T(8,128)(2,1)S(1)}, u32[]{:S(2)}, u32[]{:S(2)}) collective-permute-start(bf16[4,32,1152]{2,1,0:T(8,128)(2,1)S(1)} %get-tuple-element.105), channel_id=1, source_target_pairs={{0,4},{1,5},{2,6},{3,7},{4,0},{5,1},{6,2},{7,3},{8,12},{9,13},{10,... | collective-permute-start | bytes 884744 | tf_op jit(solution)/shard_map/ppermute | solution.py:143
  760.9 12.6 %collective-permute-start.33 = (bf16[4,32,1152]{2,1,0:T(8,128)(2,1)S(1)}, bf16[4,32,1152]{2,1,0:T(8,128)(2,1)S(1)}, u32[]{:S(2)}, u32[]{:S(2)}) collective-permute-start(bf16[4,32,1152]{2,1,0:T(8,128)(2,1)S(1)} %get-tuple-element.106), channel_id=1, source_target_pairs={{0,5},{1,4},{2,7},{3,6},{4,1},{5,0},{6,3},{7,2},{8,13},{9,12},{10,... | collective-permute-start | bytes 884744 | tf_op jit(solution)/shard_map/ppermute | solution.py:143
  760.9 17.6 %collective-permute-start.31 = (bf16[4,32,1152]{2,1,0:T(8,128)(2,1)S(1)}, bf16[4,32,1152]{2,1,0:T(8,128)(2,1)S(1)}, u32[]{:S(2)}, u32[]{:S(2)}) collective-permute-start(bf16[4,32,1152]{2,1,0:T(8,128)(2,1)S(1)} %get-tuple-element.107), channel_id=1, source_target_pairs={{0,7},{1,6},{2,5},{3,4},{4,3},{5,2},{6,1},{7,0},{8,15},{9,14},{10,... | collective-permute-start | bytes 884744 | tf_op jit(solution)/shard_map/ppermute | solution.py:143
  766.8 54.9 %collective-permute-start.42 = (f32[3,144,1152]{2,1,0:T(8,128)S(1)}, f32[3,144,1152]{2,1,0:T(8,128)S(1)}, u32[]{:S(2)}, u32[]{:S(2)}) collective-permute-start(f32[3,144,1152]{2,1,0:T(8,128)S(1)} %copy-done.22), channel_id=1, source_target_pairs={{0,2},{1,5},{2,0},{3,7},{4,6},{5,1},{6,4},{7,3},{8,10},{9,13},{10,... | collective-permute-start | bytes 5971976 | tf_op jit(solution)/shard_map/ppermute | solution.py:143
  772.0 49.7 %collective-permute-start.44 = (f32[3,144,1152]{2,1,0:T(8,128)S(1)}, f32[3,144,1152]{2,1,0:T(8,128)S(1)}, u32[]{:S(2)}, u32[]{:S(2)}) collective-permute-start(f32[3,144,1152]{2,1,0:T(8,128)S(1)} %copy-done.23), channel_id=1, source_target_pairs={{0,4},{1,3},{2,6},{3,1},{4,0},{5,7},{6,2},{7,5},{8,12},{9,11},{10,... | collective-permute-start | bytes 5971976 | tf_op jit(solution)/shard_map/ppermute | solution.py:143
  (60 other events, 1189.1 us)
Sparse Core Ops, SparseCore 0:
  12.2 80.2 all-gather.5
  95.2 52.4 all-gather.7
  149.9 81.1 all-gather.9
where the time goes:
time: 839 us; the launch traced here: 832 us
  waiting for transfers between devices  337 us (40%)
  matrix products  183 us (22%)
  other arithmetic  93.1 us (11%)
  local copies, waits for them, and re-layouts  81.6 us (10%)
  Pallas kernels  72.8 us (9%)
  starting transfers between devices  48.9 us (6%)
  between operations  15.1 us (2%)
    ppermute x51, waiting for transfers between devices, permute(): return lax.ppermute(val, tp, tp_perm(fn))  259 us
    all_gather x3, waiting for transfers between devices, gather(): own = lax.all_gather(mine, ('dp', 'chip'), axis=0, tiled=False)  78.1 us
    dot_general x6, matrix products, dot_nt(): lax.dot_general(a, b, (((1,), (1,)), ((), ())), preferred_element_type=F32)  70.2 us
    dot_general x6, matrix products, dot_nn(): lax.dot_general(a, b, (((1,), (0,)), ((), ())), preferred_element_type=F32)  61 us
    dot_general x7, matrix products, dot_tn(): lax.dot_general(a, b, (((0,), (0,)), ((), ())), preferred_element_type=F32)  51.8 us
    ppermute x51, starting transfers between devices, permute(): return lax.ppermute(val, tp, tp_perm(fn))  48.7 us
    pallas_call x1, Pallas kernels, attention_backward(): pl.pallas_call(attn_bwd, grid=(rows // toks,), out_shape=jax.ShapeDtypeSt...  40.6 us
    pallas_call x1, Pallas kernels, attention_forward(): pl.pallas_call(attn_fwd, grid=(rows // toks,), out_shape=jax.ShapeDtypeSt...  32.3 us
  transfers between devices with their start and end apart: 54, of which 21 were waited for; matrix products, arithmetic and copies ran while one was open for 33% of the time, Pallas kernels for 9%

commit v1 on v0

v1 whole, which is shorter than its diff:
```python
import math
import jax
import jax.numpy as jnp
from jax import lax
from jax.experimental import pallas as pl
from jax.experimental.pallas import tpu as pltpu
from jax.sharding import Mesh, PartitionSpec as P

LN_EPS = 1e-6
BF16 = jnp.bfloat16
F32 = jnp.float32

CHIPS = 4
HEADS = 2
HEAD_DIM = 72
QROWS = HEADS * HEAD_DIM
WIDTH = 1152
MLP = 538
MLP_PAD = 544
HALF = MLP_PAD // 2
ALL_AXES = ('dp', 'chip', 'core')
N_HEADS = 16
WIN_LANES = 256
UNROLL_F = 16
UNROLL_B = 16
ATT_SCALE = 1.0 / math.sqrt(HEAD_DIM)


def layer_norm(rows, ln_gain, ln_bias):
    row_mean = jnp.mean(rows, axis=-1, keepdims=True)
    centered = rows - row_mean
    variance = jnp.mean(centered * centered, axis=-1, keepdims=True)
    return centered * lax.rsqrt(variance + LN_EPS) * ln_gain + ln_bias


def gelu_tanh(pre_act):
    return jax.nn.gelu(pre_act, approximate=True)


def dot_nt(a, b):
    return lax.dot_general(a, b, (((1,), (1,)), ((), ())), preferred_element_type=F32)


def dot_nn(a, b):
    return lax.dot_general(a, b, (((1,), (0,)), ((), ())), preferred_element_type=F32)


def dot_tn(a, b):
    return lax.dot_general(a, b, (((0,), (0,)), ((), ())), preferred_element_type=F32)


def head_window(head):
    low = head * HEAD_DIM
    base = jnp.minimum(low // 128, WIDTH // 128 - WIN_LANES // 128) * 128
    base = pl.multiple_of(base, 128)
    lane = lax.broadcasted_iota(jnp.int32, (1, WIN_LANES), 1)
    mask = (lane >= low - base) & (lane < low - base + HEAD_DIM)
    return base, mask


def head_rows(ref, base):
    val = ref[:, 0, :, pl.ds(base, WIN_LANES)]
    return val.reshape(val.shape[0] * val.shape[1], WIN_LANES)


def probs_t(keys, queries):
    scores = dot_nt(keys, queries) * ATT_SCALE
    scores = jnp.exp(scores - jnp.max(scores, axis=0, keepdims=True))
    return scores * (1.0 / jnp.sum(scores, axis=0, keepdims=True))


def attn_fwd(q_ref, k_ref, v_ref, out_ref, acc):
    acc[...] = jnp.zeros_like(acc)

    def body(head, _):
        base, mask = head_window(head)
        zero = jnp.zeros((), BF16)
        keys = jnp.where(mask, head_rows(k_ref, base), zero)
        vals = jnp.where(mask, head_rows(v_ref, base), zero)
        probs = probs_t(keys, head_rows(q_ref, base)).astype(BF16)
        acc[:, pl.ds(base, WIN_LANES)] += dot_tn(probs, vals)
        return 0

    lax.fori_loop(0, N_HEADS, body, 0, unroll=UNROLL_F)
    out_ref[...] = acc[...].astype(BF16).reshape(out_ref.shape)


def attn_bwd(q_ref, k_ref, v_ref, do_ref, out_ref, acc):
    acc[...] = jnp.zeros_like(acc)

    def body(head, _):
        base, mask = head_window(head)
        zero = jnp.zeros((), BF16)
        queries = jnp.where(mask, head_rows(q_ref, base), zero)
        keys = jnp.where(mask, head_rows(k_ref, base), zero)
        d_out = jnp.where(mask, head_rows(do_ref, base), zero)
        probs = probs_t(keys, queries)
        d_probs = dot_nt(head_rows(v_ref, base), d_out).astype(BF16).astype(F32)
        prod = d_probs * probs
        d_scores = (prod - probs * jnp.sum(prod, axis=0, keepdims=True)) * ATT_SCALE
        d_scores = d_scores.astype(BF16)
        acc[:, pl.ds(base, WIN_LANES)] += dot_tn(d_scores, keys)
        acc[:, pl.ds(pl.multiple_of(base + WIDTH, 128), WIN_LANES)] += dot_nn(d_scores, queries)
        acc[:, pl.ds(pl.multiple_of(base + 2 * WIDTH, 128), WIN_LANES)] += dot_nn(probs.astype(BF16), d_out)
        return 0

    lax.fori_loop(0, N_HEADS, body, 0, unroll=UNROLL_B)
    out_ref[...] = acc[...].astype(BF16).reshape(out_ref.shape)


def part_spec(groups, toks, part):
    return pl.BlockSpec((groups, 1, toks, WIDTH), lambda i: (0, i, 0, part))


def attention_cost(inputs, parts, out_parts, dots):
    groups, images, toks, _ = inputs[0].shape
    n_tok = groups * toks
    return pl.CostEstimate(flops=dots * 8 * images * n_tok * n_tok * WIN_LANES * N_HEADS,
                           bytes_accessed=images * n_tok * WIDTH * 2 * (len(parts) + out_parts),
                           transcendentals=images * n_tok * n_tok * N_HEADS)


def attention_call(body, inputs, parts, out_parts, dots):
    groups, images, toks, _ = inputs[0].shape
    return pl.pallas_call(
        body, grid=(images,),
        out_shape=jax.ShapeDtypeStruct((groups, images, toks, out_parts * WIDTH), BF16),
        in_specs=[part_spec(groups, toks, p) for p in parts],
        out_specs=pl.BlockSpec((groups, 1, toks, out_parts * WIDTH), lambda i: (0, i, 0, 0)),
        scratch_shapes=[pltpu.VMEM((groups * toks, out_parts * WIDTH), F32)],
        cost_estimate=attention_cost(inputs, parts, out_parts, dots))(*inputs)


def attention_forward(qkv):
    return attention_call(attn_fwd, (qkv,) * 3, (0, 1, 2), 1, 2)


def attention_backward(qkv, d_mixed):
    return attention_call(attn_bwd, (qkv,) * 3 + (d_mixed,), (0, 1, 2, 0), 3, 5)


def tie(val, *deps):
    return lax.optimization_barrier((val,) + deps)[0]


def solution(mesh):
    mesh3 = Mesh(mesh.devices.reshape(2, CHIPS, 2), ALL_AXES)
    tp = ('chip', 'core')
    act_spec = P('dp', tp, None)
    replicated = P()
    head_w = P(None, tp, None)
    head_b = P(tp, None)
    grad_head_w = P('dp', tp, None)
    dp_tp = ('dp', 'chip', 'core')
    grad_head_b = P(dp_tp, None)
    grad_vec = P('dp')
    in_specs = (act_spec, act_spec, replicated, replicated, head_w, head_b, head_w, head_w, head_b,
                P(tp, None, None), replicated, replicated, replicated, P(None, tp), P(tp), P(tp, None), replicated)
    out_specs = (act_spec, act_spec, grad_vec, grad_vec, grad_head_w, grad_head_b, grad_head_w, grad_head_w, grad_head_b,
                 P(dp_tp, None, None), grad_vec, grad_vec, grad_vec, P('dp', tp), P(dp_tp),
                 P(dp_tp, None), grad_vec)

    def tp_perm(fn):
        return [(i, fn(i)) for i in range(8)]

    def permute(val, fn):
        return lax.ppermute(val, tp, tp_perm(fn))

    def core_swap(val):
        return permute(val, lambda i: i ^ 1)

    def pick(val, idx, axis=0):
        return lax.dynamic_index_in_dim(val, idx, axis, keepdims=False)

    def layer_step(x, d_out, ln1_gain, ln1_bias, w_q, b_q, w_k, w_v, b_v, w_o, b_o, ln2_gain, ln2_bias, w_1, b_1, w_2, b_2):
        dp = lax.axis_index('dp')
        chip = lax.axis_index('chip')
        core = lax.axis_index('core')
        cx, cy = chip % 2, chip // 2
        core0 = core == 0
        images = x.shape[0] // 8
        toks = x.shape[1]
        rows = images * toks * 8

        first = lambda i: (i ^ 2) if i % 2 == 0 else (i ^ 4)
        second = lambda i: (i ^ 4) if i % 2 == 0 else (i ^ 2)
        me = jnp.where(core0, cy, cx)
        away = lambda k: jnp.where(core0, k * 2 + (1 - cx), (1 - cy) * 2 + k)
        near = lambda k: jnp.where(core0, k * 2 + cx, cy * 2 + k)

        def stage2(own, got, axis):
            blk = lambda i: pick(own, i, axis) + pick(got, i, axis)
            send = (blk(away(1 - me)), blk(away(me)))
            far = permute(send[0], first)
            close = permute(send[1], first)
            return send, (far, close)

        def stage3(own, got, axis, far):
            send = pick(own, near(1 - me), axis) + pick(got, near(1 - me), axis) + far
            return send, permute(send, second)

        def finish(own, got, axis, close, part):
            return pick(own, near(me), axis) + pick(got, near(me), axis) + close + part

        def gather_all(half0, half1):
            return lax.all_gather(jnp.where(dp == 0, half0, half1), ALL_AXES, axis=0, tiled=False).reshape(2, 8, *half0.shape)

        def gather_own(half0, half1):
            own = lax.all_gather(jnp.where(dp == 0, half0, half1), ('dp', 'chip'), axis=0, tiled=False)
            return own.reshape(2 * CHIPS * HALF, WIDTH)

        def swap_weights(own):
            return [own, core_swap(own)]

        def rows_of(w):
            return jnp.transpose(w, (1, 2, 0)).reshape(QROWS, WIDTH)

        b1_pad = jnp.pad(b_1, (0, MLP_PAD - MLP))

        def bias_rows(head_bias, mlp_bias):
            row = jnp.concatenate([head_bias.reshape(QROWS), mlp_bias])
            return jnp.pad(row[None], ((0, 15), (0, WIDTH - row.shape[0])))

        att0 = jnp.concatenate([rows_of(w_q), rows_of(w_k), bias_rows(b_q, b1_pad[:HALF])])
        att1 = jnp.concatenate([rows_of(w_v), w_o.reshape(QROWS, WIDTH), bias_rows(b_v, b1_pad[HALF:])])
        att = gather_all(att0, att1)
        w1_rows = jnp.pad(w_1.T, ((0, MLP_PAD - MLP), (0, 0)))
        w2_rows = jnp.pad(w_2, ((0, MLP_PAD - MLP), (0, 0)))
        w1_all = swap_weights(gather_own(w1_rows[:HALF], w1_rows[HALF:]))
        w2_own_rows = gather_own(w2_rows[:HALF], w2_rows[HALF:])

        flat = CHIPS * QROWS
        part = lambda half, first: att[half, :, first:first + QROWS].reshape(2 * flat, WIDTH)
        bias = lambda half: att[half, :, 2 * QROWS, :QROWS].reshape(2 * flat)
        wqkv = jnp.concatenate([part(0, 0), part(0, QROWS), part(1, 0)])
        wo_all = part(1, QROWS)
        bqkv = jnp.concatenate([bias(0), jnp.zeros((2 * flat,), BF16), bias(1)]).astype(F32)
        b1_rows = att[:, :, 2 * QROWS, QROWS:QROWS + HALF].reshape(2, CHIPS, 2, HALF)
        b1_all = [pick(b1_rows, c, 2).reshape(2 * CHIPS * HALF).astype(F32) for c in (core, 1 - core)]

        x_rows = lax.all_to_all(x.reshape(8, images * toks, WIDTH), tp, 0, 0).reshape(rows, WIDTH)
        x_f32 = x_rows.astype(F32)
        h_one_f, ln1_pull = jax.vjp(layer_norm, x_f32, ln1_gain, ln1_bias)
        h_one = h_one_f.astype(BF16)
        qkv = (dot_nt(h_one, wqkv) + bqkv).astype(BF16)
        qkv = qkv.reshape(8, images, toks, 3 * WIDTH)
        mixed = attention_forward(qkv).reshape(rows, WIDTH)
        g_out = tie(d_out.reshape(8, images * toks, WIDTH), mixed)
        g_out = lax.all_to_all(g_out, tp, 0, 0).reshape(rows, WIDTH)
        attn_out = dot_nn(mixed, wo_all)
        x_mid = (x_f32 + attn_out + b_o).astype(BF16)
        mid_f32 = x_mid.astype(F32)
        h_two_f, ln2_pull = jax.vjp(layer_norm, mid_f32, ln2_gain, ln2_bias)
        h_two = h_two_f.astype(BF16)
        blocks = (2, CHIPS, HALF, WIDTH)
        hidden, gelu_pulls = [], []
        for w1, b1 in zip(w1_all, b1_all):
            pre_act = dot_nt(tie(h_two, *hidden), w1)
            pre_act = (pre_act + b1).astype(BF16)
            hid_f, gelu_pull = jax.vjp(gelu_tanh, pre_act.astype(F32))
            hidden.append(hid_f.astype(BF16))
            gelu_pulls.append(gelu_pull)
        w2_oth = dot_tn(hidden[1], g_out).reshape(blocks)
        w2_got = core_swap(w2_oth)
        w2_own = dot_tn(tie(hidden[0], w2_oth), g_out).reshape(blocks)
        w2_all = swap_weights(tie(w2_own_rows, w2_own))
        w2_send, w2_in = stage2(w2_own, w2_got, 1)
        g_mlp = tie(g_out, *w2_send)
        d_pre = [None, None]
        for c in (0, 1):
            d_hidden = dot_nt(tie(g_mlp, *d_pre[:c]), w2_all[c]).astype(BF16)
            (d_pre_f,) = gelu_pulls[c](d_hidden.astype(F32))
            d_pre[c] = d_pre_f.astype(BF16)
        w1_oth = dot_tn(d_pre[1], h_two).reshape(blocks)
        w1_got = core_swap(w1_oth)
        w1_own = dot_tn(tie(d_pre[0], w1_oth), h_two).reshape(blocks)
        w1_send, w1_in = stage2(w1_own, w1_got, 1)
        d_pre_t = [tie(d, *w1_send) for d in d_pre]
        d_h_two = (dot_nn(d_pre_t[0], w1_all[0]) + dot_nn(d_pre_t[1], w1_all[1])).astype(BF16)
        d_mid_ln, g_ln2_gain, g_ln2_bias = ln2_pull(d_h_two.astype(F32))
        d_mid = (g_out.astype(F32) + d_mid_ln).astype(BF16)
        d_mixed = dot_nt(d_mid, wo_all).astype(BF16)
        dw_o = dot_tn(mixed, d_mid).reshape(CHIPS, 2, QROWS, WIDTH)
        wo_own, wo_oth = pick(dw_o, core, 1), pick(dw_o, 1 - core, 1)
        wo_got = core_swap(wo_oth)
        w2_last, w2_part = stage3(w2_own, w2_got, 1, w2_in[0])
        mlp_out = dot_nn(tie(hidden[0], d_mixed), w2_all[0])
        mlp_out = mlp_out + dot_nn(hidden[1], w2_all[1])
        y_rows = (mid_f32 + mlp_out + b_2).astype(BF16)
        d_mixed = tie(d_mixed, w2_last).reshape(8, images, toks, WIDTH)
        d_qkv = attention_backward(qkv, d_mixed).reshape(rows, 3 * WIDTH)
        y_out = lax.all_to_all(y_rows.reshape(8, images * toks, WIDTH), tp, 0, 0).reshape(x.shape)
        w1_last, w1_part = stage3(w1_own, w1_got, 1, w1_in[0])
        d_qkv = tie(d_qkv, w1_last)
        own, got, sends, ins = {}, {}, {}, {}
        for n, name in enumerate('qkv'):
            dw = dot_tn(d_qkv[:, n * WIDTH:(n + 1) * WIDTH], h_one).reshape(CHIPS, 2, QROWS, WIDTH)
            own[name], oth = pick(dw, core, 1), pick(dw, 1 - core, 1)
            got[name] = core_swap(oth)
            d_qkv = tie(d_qkv, oth)
        sends['q'], ins['q'] = stage2(own['q'], got['q'], 0)
        wo_send, wo_in = stage2(wo_own, wo_got, 0)
        d_h_one = dot_nn(tie(d_qkv, *sends['q'], *wo_send), wqkv).astype(BF16)
        for name in 'kv':
            sends[name], ins[name] = stage2(own[name], got[name], 0)
        d_h_one = tie(d_h_one, *sends['k'], *sends['v'])
        d_in_ln, g_ln1_gain, g_ln1_bias = ln1_pull(d_h_one.astype(F32))
        g_x = (d_mid.astype(F32) + d_in_ln).astype(BF16)
        grad_x = lax.all_to_all(g_x.reshape(8, images * toks, WIDTH), tp, 0, 0).reshape(x.shape)
        _, wo_part = stage3(wo_own, wo_got, 0, wo_in[0])
        grad_qkv = {}
        for name in 'qkv':
            _, last = stage3(own[name], got[name], 0, ins[name][0])
            grad_qkv[name] = finish(own[name], got[name], 0, ins[name][1], last).astype(BF16)

        grad_w2 = finish(w2_own, w2_got, 1, w2_in[1], w2_part)
        grad_w2 = grad_w2.reshape(MLP_PAD, WIDTH)[:MLP].astype(BF16)
        grad_w1 = finish(w1_own, w1_got, 1, w1_in[1], w1_part)
        grad_w1 = grad_w1.reshape(MLP_PAD, WIDTH)[:MLP].T.astype(BF16)
        grad_wo = finish(wo_own, wo_got, 0, wo_in[1], wo_part)
        grad_wo = grad_wo.reshape(HEADS, HEAD_DIM, WIDTH).astype(BF16)
        unrow = lambda w: jnp.transpose(w.reshape(HEADS, HEAD_DIM, WIDTH), (2, 0, 1))

        col_sum = lambda v: jnp.sum(v, axis=0, dtype=F32)
        vecs = jnp.stack([g_ln1_gain, g_ln1_bias, col_sum(d_mid), g_ln2_gain, g_ln2_bias, col_sum(g_out)])

        qkv_sums = col_sum(d_qkv).reshape(3, CHIPS, 2, QROWS)

        def extra_rows(c):
            sums = pick(qkv_sums, core if c == 0 else 1 - core, 2)
            b1_sum = jnp.transpose(col_sum(d_pre[c]).reshape(2, CHIPS, HALF), (1, 0, 2)).reshape(CHIPS, MLP_PAD)
            row = jnp.concatenate([sums[0], sums[2], b1_sum, jnp.zeros((CHIPS, WIDTH - 2 * QROWS - MLP_PAD), F32)], axis=1)
            return jnp.concatenate([jnp.broadcast_to(vecs, (CHIPS, 6, WIDTH)), row[:, None],
                                    jnp.zeros((CHIPS, 1, WIDTH), F32)], axis=1)

        ex_own, ex_got = extra_rows(0), core_swap(extra_rows(1))
        _, ex_in = stage2(ex_own, ex_got, 0)
        _, ex_part = stage3(ex_own, ex_got, 0, ex_in[0])
        extra = finish(ex_own, ex_got, 0, ex_in[1], ex_part)
        b_row = extra[6].astype(BF16)
        return (y_out, grad_x, extra[0], extra[1], unrow(grad_qkv['q']), b_row[:QROWS].reshape(HEADS, HEAD_DIM),
                unrow(grad_qkv['k']), unrow(grad_qkv['v']), b_row[QROWS:2 * QROWS].reshape(HEADS, HEAD_DIM), grad_wo,
                extra[2].astype(BF16), extra[3], extra[4], grad_w1, b_row[2 * QROWS:2 * QROWS + MLP], grad_w2,
                extra[5].astype(BF16))

    return jax.shard_map(layer_step, mesh=mesh3, in_specs=in_specs, out_specs=out_specs, check_vma=False)
```

time: 839 us -> 685 us (0.82)
  waiting for transfers between devices: 337 us -> 213 us
  Pallas kernels: 72.8 us -> 42.5 us
  starting transfers between devices: 48.9 us -> 40.5 us
    ppermute x51 -> x30, waiting for transfers between devices: 259 us -> 91.8 us  [permute(): return lax.ppermute(val, tp, tp_perm(fn))]
    all_to_all x0 -> x4, waiting for transfers between devices: none -> 41.5 us  [the longest x1 39.6 us: layer_step(): lax.all_to_all(x.reshape(8, images * toks, WIDTH), tp, 0, 0)]
    pallas_call x2, Pallas kernels: 72.8 us -> 42.5 us  [attention_call(): pl.pallas_call(body, grid=(images,), out_shape=jax.ShapeDtypeStruct((grou...]
    ppermute x51 -> x30, starting transfers between devices: 48.7 us -> 22.1 us  [permute(): return lax.ppermute(val, tp, tp_perm(fn))]
    all_to_all x0 -> x4, starting transfers between devices: none -> 18.3 us  [the longest x1 5.44 us: layer_step(): lax.all_to_all(x.reshape(8, images * toks, WIDTH), tp, 0, 0)]
    dot_general x2 -> x8, local copies, waits for them, and re-layouts: 16.8 us -> 34.5 us  [dot_tn(): lax.dot_general(a, b, (((0,), (0,)), ((), ())), preferred_element_type=F32)]
    dot_general x6, matrix products: 61 us -> 49.8 us  [dot_nn(): lax.dot_general(a, b, (((1,), (0,)), ((), ())), preferred_element_type=F32)]
    dot_general x7 -> x8, matrix products: 51.8 us -> 61 us  [dot_tn(): lax.dot_general(a, b, (((0,), (0,)), ((), ())), preferred_element_type=F32)]
  transfers between devices with their start and end apart: 54 -> 37, of which waited for: 21 -> 12; matrix products, arithmetic and copies ran while one was open for 33% -> 47% of each run, Pallas kernels for 9% -> 6%
where the time goes in v1:
time: 685 us; the launch traced here: 675 us
  waiting for transfers between devices  213 us (31%)
  matrix products  180 us (26%)
  other arithmetic  99.7 us (15%)
  local copies, waits for them, and re-layouts  83.7 us (12%)
  Pallas kernels  42.5 us (6%)
  starting transfers between devices  40.5 us (6%)
  between operations  15.2 us (2%)
    ppermute x30, waiting for transfers between devices, permute(): return lax.ppermute(val, tp, tp_perm(fn))  91.8 us
    dot_general x6, matrix products, dot_nt(): lax.dot_general(a, b, (((1,), (1,)), ((), ())), preferred_element_type=F32)  69.4 us
    all_gather x1, waiting for transfers between devices, gather_all(): lax.all_gather(jnp.where(dp == 0, half0, half1), ALL_AXES, axis=0, tiled=...  61 us
    dot_general x8, matrix products, dot_tn(): lax.dot_general(a, b, (((0,), (0,)), ((), ())), preferred_element_type=F32)  61 us
    dot_general x6, matrix products, dot_nn(): lax.dot_general(a, b, (((1,), (0,)), ((), ())), preferred_element_type=F32)  49.8 us
    pallas_call x2, Pallas kernels, attention_call(): pl.pallas_call(body, grid=(images,), out_shape=jax.ShapeDtypeStruct((grou...  42.5 us
    all_to_all x1, waiting for transfers between devices, layer_step(): lax.all_to_all(x.reshape(8, images * toks, WIDTH), tp, 0, 0)  39.6 us
    dot_general x8, local copies, waits for them, and re-layouts, dot_tn(): lax.dot_general(a, b, (((0,), (0,)), ((), ())), preferred_element_type=F32)  34.5 us
  transfers between devices with their start and end apart: 37, of which 12 were waited for; matrix products, arithmetic and copies ran while one was open for 47% of the time, Pallas kernels for 6%

profile of v1, /device:TPU:0, one launch (start us, length us, event | category | flops | bytes accessed | tf_op | source)
XLA Modules:
  0.0 675.0 jit_solution(13251362213822379736)
XLA Ops:
  14.3 5.4 all-to-all-start
  22.2 39.6 %all-to-all-done = bf16[8,128,1152]{2,1,0:T(8,128)(2,1)S(1)} async-done(((bf16[8,128,1152]{2,1,0:T(8,128)(2,1)}), bf16[8,128,1152]{2,1,0:T(8,128)(2,1)S(1)}, u32[]{:S(2)}, u32[]{:S(2)}) %all-to-all-start) | async-done | bytes 2359328 | tf_op jit(solution)/shard_map/all_to_all | solution.py:241
  66.5 18.8 %all-gather.8.cloned.1.call-done = bf16[2176,1152]{1,0:T(8,128)(2,1)} async-done(((bf16[272,1152]{1,0:T(8,128)(2,1)}), bf16[2176,1152]{1,0:T(8,128)(2,1)}) %all-gather.8.cloned.1.call-update) | async-done | bytes 5013520 | tf_op jit(solution)/shard_map/all_gather | solution.py:209
  85.4 61.0 %all-gather.6.cloned.1.call-done = bf16[16,304,1152]{2,1,0:T(8,128)(2,1)} async-done(((bf16[1,304,1152]{2,1,0:T(8,128)(2,1)}), bf16[16,304,1152]{2,1,0:T(8,128)(2,1)}) %all-gather.6.cloned.1.call-update) | async-done | bytes 11206672 | tf_op jit(solution)/shard_map/all_gather | solution.py:206
  148.2 7.7 %fusion.118 = (bf16[1,8,144,1152]{3,2,1,0:T(8,128)(2,1)}, bf16[1,8,144,1152]{3,2,1,0:T(8,128)(2,1)}, bf16[1,8,144,1152]{3,2,1,0:T(8,128)(2,1)}, bf16[1,8,144,1152]{3,2,1,0:T(8,128)(2,1)}) fusion(bf16[2,8,304,1152]{3,2,1,0:T(8,128)(2,1)} %bitcast.397), kind=kLoop, calls=%fused_computation.240 | loop fusion | bytes 21233664 | tf_op jit(solution)/shard_map/slice | solution.py:233
  156.3 15.2 %add_convert_fusion = bf16[1024,3456]{1,0:T(8,128)(2,1)} fusion(bf16[1024,1152]{1,0:T(8,128)(2,1)} %fusion.56, f32[3456]{0:T(1024)S(1)} %maximum_convert_fusion, bf16[1152,1152]{1,0:T(8,128)(2,1)} %bitcast.410, bf16[1152,1152]{1,0:T(8,128)(2,1)} %bitcast.412, bf16[1152,1152]{1,0:T(8,128)(2,1)} %bitcast.414), kind=kOutput, calls=%fused_computation.16 | convolution fusion | flops 8184692736 | bytes 17413632 | tf_op jit(solution)/shard_map/dot_general | solution.py:41
  171.5 13.1 %shard_map.296 = bf16[8,4,32,1152]{3,2,1,0:T(8,128)(2,1)} custom-call(bf16[8,4,32,3456]{3,2,1,0:T(8,128)(2,1)} %bitcast.454, bf16[8,4,32,3456]{3,2,1,0:T(8,128)(2,1)} %bitcast.455, bf16[8,4,32,3456]{3,2,1,0:T(8,128)(2,1)} %bitcast.456), custom_call_target="tpu_custom_call" | custom-call | flops 17179869184 | bytes 9437184 | tf_op jit(solution)/shard_map/pallas_call | solution.py:125
  184.6 4.8 all-to-all-start.1
  189.5 6.2 convert_reduce_fusion.5
  198.1 8.8 %fusion.23 = (bf16[1024,2176]{1,0:T(8,128)(2,1)}, bf16[1024,2176]{1,0:T(8,128)(2,1)}) fusion(f32[2176]{0:T(1024)S(1)} %reshape.513, bf16[1024,1152]{1,0:T(8,128)(2,1)S(1)} %fusion.41, bf16[2176,1152]{1,0:T(8,128)(2,1)S(1)} %bitcast.449), kind=kOutput, calls=%fused_computation.38 | convolution fusion | flops 5160566784 | bytes 16294400 | tf_op jit(solution)/shard_map/dot_general | solution.py:41
  207.0 11.6 %fusion.19 = (bf16[2176,1024]{0,1:T(8,128)(2,1)}, bf16[1024,2176]{1,0:T(8,128)(2,1)}) fusion(f32[2176]{0:T(1024)S(1)} %reshape.514, bf16[1024,1152]{1,0:T(8,128)(2,1)} %copy-done.18, bf16[2176,1152]{1,0:T(8,128)(2,1)} %collective-permute-done), kind=kOutput, calls=%fused_computation.34 | convolution fusion | flops 5160566784 | bytes 16294400 | tf_op jit(solution)/shard_map/dot_general | solution.py:41
  218.6 6.5 copy.123
  227.0 10.9 %fusion.119 = f32[2,4,272,1152]{3,2,1,0:T(8,128)} fusion(bf16[2,4,272,1024]{3,2,1,0:T(8,128)(2,1)} %bitcast.407, bf16[1024,1152,1,1]{1,0,3,2:T(8,128)(2,1)} %bitcast.27), kind=kOutput, calls=%fused_computation.241 | convolution fusion | flops 5133828096 | bytes 16842752 | tf_op jit(solution)/shard_map/dot_general | solution.py:49
  237.9 6.5 copy.124
  244.4 10.6 %fusion.120 = f32[2,4,272,1152]{3,2,1,0:T(8,128)} fusion(bf16[2,4,272,1024]{3,2,1,0:T(8,128)(2,1)} %bitcast.408, bf16[1024,1152,1,1]{1,0,3,2:T(8,128)(2,1)} %bitcast.27), kind=kOutput, calls=%fused_computation.242 | convolution fusion | flops 5133828096 | bytes 16842752 | tf_op jit(solution)/shard_map/dot_general | solution.py:49
  255.6 7.1 %fusion.75 = (f32[2,272,1152]{2,1,0:T(8,128)}, f32[2,272,1152]{2,1,0:T(8,128)}) fusion(f32[2,4,272,1152]{3,2,1,0:T(8,128)} %collective-permute-done.1, s32[]{:T(128)S(6)} %select_n.199, f32[2,4,272,1152]{3,2,1,0:T(8,128)} %fusion.120, s32[]{:T(128)S(6)} %select_n.197), kind=kLoop, calls=%fused_computation.127 | loop fusion | flops 1253376 | bytes 15040520 | tf_op jit(solution)/shard_map/add | solution.py:192
  262.7 15.2 %convert_reduce_fusion.2 = (f32[2176]{0:T(1024)S(1)}, bf16[1024,2176]{1,0:T(8,128)(2,1)}) fusion(bf16[1024,2176]{1,0:T(8,128)(2,1)} %get-tuple-element.106, bf16[1024,1152]{1,0:T(8,128)(2,1)} %bitcast.23, bf16[2176,1152]{1,0:T(8,128)(2,1)S(1)} %copy-done.48), kind=kOutput, calls=%fused_computation.48 | convolution fusion | flops 5189531648 | bytes 16294400 | tf_op jit(solution)/shard_map/dot_general | solution.py:41
  278.0 13.8 %convert_reduce_fusion.1 = (f32[2176]{0:T(1024)S(1)}, bf16[1024,2176]{1,0:T(8,128)(2,1)S(1)}) fusion(bf16[1024,2176]{1,0:T(8,128)(2,1)S(1)} %bitcast.466, bf16[1024,1152]{1,0:T(8,128)(2,1)} %bitcast.23, bf16[2176,1152]{1,0:T(8,128)(2,1)} %collective-permute-done.2), kind=kOutput, calls=%fused_computation.47 | convolution fusion | flops 5189531648 | bytes 16294400 | tf_op jit(solution)/shard_map/dot_general | solution.py:41
  291.9 8.7 %fusion.121 = f32[2176,1152]{1,0:T(8,128)} fusion(bf16[1024,2176]{1,0:T(8,128)(2,1)S(1)} %get-tuple-element.42, bf16[1024,1152]{1,0:T(8,128)(2,1)S(1)} %copy-done.19), kind=kOutput, calls=%fused_computation.243 | convolution fusion | flops 5133828096 | bytes 16842752 | tf_op jit(solution)/shard_map/dot_general | solution.py:49
  304.1 4.8 copy.140
  314.7 8.3 %fusion.122 = f32[2176,1152]{1,0:T(8,128)S(1)} fusion(bf16[1024,2176]{1,0:T(8,128)(2,1)} %get-tuple-element.41, bf16[1024,1152]{1,0:T(8,128)(2,1)S(1)} %copy-done.20), kind=kOutput, calls=%fused_computation.244 | convolution fusion | flops 5133828096 | bytes 16842752 | tf_op jit(solution)/shard_map/dot_general | solution.py:49
  322.9 8.4 %collective-permute-done.4 = f32[2,272,1152]{2,1,0:T(8,128)} collective-permute-done((f32[2,272,1152]{2,1,0:T(8,128)}, f32[2,272,1152]{2,1,0:T(8,128)}, u32[]{:S(2)}, u32[]{:S(2)}) %collective-permute-start.4) | collective-permute-done | bytes 2506784 | tf_op jit(solution)/shard_map/ppermute | solution.py:167
  331.4 5.1 fusion.72
  337.1 5.7 fusion.73
  342.8 6.2 fusion.123
  349.0 9.5 %convert_reduce_fusion.4 = (f32[1152]{0:T(1024)S(1)}, f32[1024]{0:T(1024)S(1)}, bf16[1024,1152]{1,0:T(8,128)(2,1)S(1)}) fusion(f32[1152]{0:T(1024)S(1)} %copy-done.27, f32[1024]{0:T(1024)S(1)} %broadcast_multiply_fusion, bf16[1024,1152]{1,0:T(8,128)(2,1)S(1)} %copy-done.3, f32[1024,1152]{1,0:T(8,128)S(1)} %fusion.123, bf16[1024,2176]{1,0:T(8,128)(2,1)S(1)} %bitcast.464, ...), kind=kOutput, calls=%fused_computation.57 | convolution fusion | flops 5144442880 | bytes 18924544 | tf_op jit(solution)/shard_map/dot_general | solution.py:45
  365.3 4.8 convolution_convert_fusion.3
  372.1 6.2 fusion.124
  378.3 11.9 %fusion.47 = bf16[1024,1152]{1,0:T(8,128)(2,1)} fusion(bf16[1024,1152]{1,0:T(8,128)(2,1)S(1)} %copy-done.3, f32[1024,1152]{1,0:T(8,128)S(1)} %fusion.124, bf16[2176,1152]{1,0:T(8,128)(2,1)} %collective-permute-done.2, bf16[1024,2176]{1,0:T(8,128)(2,1)S(1)} %bitcast.468, f32[1152]{0:T(1024)S(1)} %convert_element_type.236), kind=kOutput, calls=%fused_computation.82 | convolution fusion | flops 5162008576 | bytes 18911744 | tf_op jit(solution)/shard_map/dot_general | solution.py:45
  393.8 5.6 fusion.81
  403.9 29.4 %shard_map.297 = bf16[8,4,32,3456]{3,2,1,0:T(8,128)(2,1)} custom-call(bf16[8,4,32,3456]{3,2,1,0:T(8,128)(2,1)} %bitcast.457, bf16[8,4,32,3456]{3,2,1,0:T(8,128)(2,1)} %bitcast.458, bf16[8,4,32,3456]{3,2,1,0:T(8,128)(2,1)} %bitcast.459, bf16[8,4,32,1152]{3,2,1,0:T(8,128)(2,1)} %bitcast.460), custom_call_target="tpu_custom_call" | custom-call | flops 42949672960 | bytes 16515072 | tf_op jit(solution)/shard_map/pallas_call | solution.py:125
  433.3 18.2 %collective-permute-done.5 = f32[2,272,1152]{2,1,0:T(8,128)} collective-permute-done((f32[2,272,1152]{2,1,0:T(8,128)}, f32[2,272,1152]{2,1,0:T(8,128)}, u32[]{:S(2)}, u32[]{:S(2)}) %collective-permute-start.5) | collective-permute-done | bytes 2506784 | tf_op jit(solution)/shard_map/ppermute | solution.py:167
  451.4 5.1 fusion.70
  460.3 4.7 copy.137
  465.0 5.6 fusion.125
  482.1 5.6 fusion.126
  497.0 4.4 copy.139
  505.9 5.6 fusion.127
  515.6 5.6 collective-permute-done.25
  522.6 5.4 fusion.78
  528.0 4.9 convert_reduce_fusion
  538.5 5.4 fusion.80
  552.0 9.8 %convolution_convert_fusion.2 = bf16[1024,1152]{1,0:T(8,128)(2,1)S(1)} fusion(bf16[1024,3456]{1,0:T(8,128)(2,1)S(1)} %bitcast.394, bf16[1152,1152]{1,0:T(8,128)(2,1)S(1)} %bitcast.411, bf16[1152,1152]{1,0:T(8,128)(2,1)S(1)} %bitcast.413, bf16[1152,1152]{1,0:T(8,128)(2,1)S(1)} %bitcast.415), kind=kOutput, calls=%fused_computation.108 | convolution fusion | flops 8178794496 | bytes 17399808 | tf_op jit(solution)/shard_map/dot_general | solution.py:45
  580.9 20.3 %collective-permute-done.12 = f32[8,1152]{1,0:T(8,128)S(1)} collective-permute-done((f32[8,1152]{1,0:T(8,128)S(1)}, f32[8,1152]{1,0:T(8,128)S(1)}, u32[]{:S(2)}, u32[]{:S(2)}) %collective-permute-start.12) | collective-permute-done | bytes 36896 | tf_op jit(solution)/shard_map/ppermute | solution.py:167
  602.7 4.4 fusion.43
  607.1 4.4 all-to-all-start.3
  616.8 30.2 %collective-permute-done.16 = f32[144,1152]{1,0:T(8,128)} collective-permute-done((f32[144,1152]{1,0:T(8,128)}, f32[144,1152]{1,0:T(8,128)}, u32[]{:S(2)}, u32[]{:S(2)}) %collective-permute-start.16) | collective-permute-done | bytes 663584 | tf_op jit(solution)/shard_map/ppermute | solution.py:167
  656.7 4.5 collective-permute-done.19
  (315 shorter events, 138.2 us)
Async XLA Ops:
  7.2 78.2 %all-gather.8.cloned.1.call-start = ((), (), s32[]{:S(2)}) async-start(), calls=%async_computation.5 | async-start | bytes 5640192 | tf_op jit(solution)/shard_map/all_gather | solution.py:209
  9.5 136.8 %all-gather.6.cloned.1.call-start = ((), (), s32[]{:S(2)}) async-start(), calls=%async_computation.4 | async-start | bytes 11907072 | tf_op jit(solution)/shard_map/all_gather | solution.py:206
  14.3 47.5 %all-to-all-start = ((bf16[8,128,1152]{2,1,0:T(8,128)(2,1)}), bf16[8,128,1152]{2,1,0:T(8,128)(2,1)S(1)}, u32[]{:S(2)}, u32[]{:S(2)}) async-start(bf16[8,128,1152]{2,1,0:T(8,128)(2,1)} %bitcast.418), calls=%async_computation | async-start | bytes 4718592 | tf_op jit(solution)/shard_map/all_to_all | solution.py:241
  19.8 44.4 %copy-start.22 = (f32[1152]{0:T(1024)S(1)}, f32[1152]{0:T(1024)}, u32[]{:S(2)}) copy-start(f32[1152]{0:T(1024)} %param.19) | copy-start | bytes 13828
  19.8 44.4 %copy-start.41 = (f32[1152]{0:T(1024)S(1)}, f32[1152]{0:T(1024)}, u32[]{:S(2)}) copy-start(f32[1152]{0:T(1024)} %param.20) | copy-start | bytes 13828
  19.8 235.3 %all-gather.10.cloned.1.call-start = ((), (), s32[]{:S(2)}) async-start(), calls=%async_computation.6 | async-start | bytes 5640192 | tf_op jit(solution)/shard_map/all_gather | solution.py:209
  61.8 240.0 %copy-start = (bf16[8,128,1152]{2,1,0:T(8,128)(2,1)}, bf16[8,128,1152]{2,1,0:T(8,128)(2,1)S(1)}, u32[]{:S(2)}) copy-start(bf16[8,128,1152]{2,1,0:T(8,128)(2,1)S(1)} %all-to-all-done) | copy-start | bytes 7077892
  85.4 121.6 %collective-permute-start = (bf16[2176,1152]{1,0:T(8,128)(2,1)}, bf16[2176,1152]{1,0:T(8,128)(2,1)}, u32[]{:S(2)}, u32[]{:S(2)}) collective-permute-start(bf16[2176,1152]{1,0:T(8,128)(2,1)} %all-gather.8.cloned.1.call-done), channel_id=1, source_target_pairs={{0,1},{1,0},{2,3},{3,2},{4,5},{5,4},{6,7},{7,6},{8,9},{9,8},{10,11... | collective-permute-start | bytes 15040520 | tf_op jit(solution)/shard_map/ppermute | solution.py:167
  184.6 42.4 %all-to-all-start.1 = ((bf16[8,128,1152]{2,1,0:T(8,128)(2,1)}), bf16[8,128,1152]{2,1,0:T(8,128)(2,1)}, u32[]{:S(2)}, u32[]{:S(2)}) async-start(bf16[8,128,1152]{2,1,0:T(8,128)(2,1)} %bitcast.419), calls=%async_computation.1 | async-start | bytes 4718592 | tf_op jit(solution)/shard_map/all_to_all | solution.py:249
  237.9 17.7 %collective-permute-start.1 = (f32[2,4,272,1152]{3,2,1,0:T(8,128)}, f32[2,4,272,1152]{3,2,1,0:T(8,128)}, u32[]{:S(2)}, u32[]{:S(2)}) collective-permute-start(f32[2,4,272,1152]{3,2,1,0:T(8,128)} %fusion.119), channel_id=1, source_target_pairs={{0,1},{1,0},{2,3},{3,2},{4,5},{5,4},{6,7},{7,6},{8,9},{9,8},{10,11... | collective-permute-start | bytes 30081032 | tf_op jit(solution)/shard_map/ppermute | solution.py:167
  255.1 22.9 %collective-permute-start.2 = (bf16[2176,1152]{1,0:T(8,128)(2,1)}, bf16[2176,1152]{1,0:T(8,128)(2,1)}, u32[]{:S(2)}, u32[]{:S(2)}) collective-permute-start(bf16[2176,1152]{1,0:T(8,128)(2,1)} %all-gather.10.cloned.1.call-done), channel_id=1, source_target_pairs={{0,1},{1,0},{2,3},{3,2},{4,5},{5,4},{6,7},{7,6},{8,9},{9,8},{10,11... | collective-permute-start | bytes 15040520 | tf_op jit(solution)/shard_map/ppermute | solution.py:167
  255.6 22.4 %slice-start.14 = ((s8[4456448]{0:T(1024)(128)(4,1)}), s8[4194304]{0:T(1024)(128)(4,1)S(1)}, s32[]{:S(2)}) async-start(s8[4456448]{0:T(1024)(128)(4,1)} %bitcast.465), calls=%async_computation.21 | async-start | bytes 8388608
  262.7 15.3 %slice-start.15 = ((s8[4456448]{0:T(1024)(128)(4,1)}), s8[262144]{0:T(1024)(128)(4,1)S(1)}, s32[]{:S(2)}) async-start(s8[4456448]{0:T(1024)(128)(4,1)} %bitcast.465), calls=%async_computation.22 | async-start | bytes 524288
  278.0 13.8 %copy-start.19 = (bf16[1024,1152]{1,0:T(8,128)(2,1)S(1)}, bf16[1024,1152]{1,0:T(8,128)(2,1)}, u32[]{:S(2)}) copy-start(bf16[1024,1152]{1,0:T(8,128)(2,1)} %copy-done.18) | copy-start | bytes 7077892
  300.6 36.4 %collective-permute-start.3 = (f32[2,4,272,1152]{3,2,1,0:T(8,128)}, f32[2,4,272,1152]{3,2,1,0:T(8,128)}, u32[]{:S(2)}, u32[]{:S(2)}) collective-permute-start(f32[2,4,272,1152]{3,2,1,0:T(8,128)} %bitcast.32), channel_id=1, source_target_pairs={{0,1},{1,0},{2,3},{3,2},{4,5},{5,4},{6,7},{7,6},{8,9},{9,8},{10,11... | collective-permute-start | bytes 30081032 | tf_op jit(solution)/shard_map/ppermute | solution.py:167
  300.6 30.7 %collective-permute-start.4 = (f32[2,272,1152]{2,1,0:T(8,128)}, f32[2,272,1152]{2,1,0:T(8,128)}, u32[]{:S(2)}, u32[]{:S(2)}) collective-permute-start(f32[2,272,1152]{2,1,0:T(8,128)} %get-tuple-element.76), channel_id=1, source_target_pairs={{0,2},{1,5},{2,0},{3,7},{4,6},{5,1},{6,4},{7,3},{8,10},{9,13},{10,... | collective-permute-start | bytes 7520264 | tf_op jit(solution)/shard_map/ppermute | solution.py:167
  311.6 192.1 %collective-permute-start.28 = (f32[2,272,1152]{2,1,0:T(8,128)}, f32[2,272,1152]{2,1,0:T(8,128)}, u32[]{:S(2)}, u32[]{:S(2)}) collective-permute-start(f32[2,272,1152]{2,1,0:T(8,128)} %get-tuple-element.75), channel_id=1, source_target_pairs={{0,2},{1,5},{2,0},{3,7},{4,6},{5,1},{6,4},{7,3},{8,10},{9,13},{10,... | collective-permute-start | bytes 7520264 | tf_op jit(solution)/shard_map/ppermute | solution.py:167
  322.9 14.1 %copy-start.6 = (f32[2176,1152]{1,0:T(8,128)}, f32[2176,1152]{1,0:T(8,128)S(1)}, u32[]{:S(2)}) copy-start(f32[2176,1152]{1,0:T(8,128)S(1)} %fusion.122) | copy-start | bytes 30081028
  336.5 168.8 %collective-permute-start.29 = (f32[2,272,1152]{2,1,0:T(8,128)}, f32[2,272,1152]{2,1,0:T(8,128)}, u32[]{:S(2)}, u32[]{:S(2)}) collective-permute-start(f32[2,272,1152]{2,1,0:T(8,128)} %fusion.72), channel_id=1, source_target_pairs={{0,4},{1,3},{2,6},{3,1},{4,0},{5,7},{6,2},{7,5},{8,12},{9,11},{10,... | collective-permute-start | bytes 7520264 | tf_op jit(solution)/shard_map/ppermute | solution.py:167
  370.1 168.5 %collective-permute-start.26 = (f32[2,272,1152]{2,1,0:T(8,128)}, f32[2,272,1152]{2,1,0:T(8,128)}, u32[]{:S(2)}, u32[]{:S(2)}) collective-permute-start(f32[2,272,1152]{2,1,0:T(8,128)} %get-tuple-element.73), channel_id=1, source_target_pairs={{0,2},{1,5},{2,0},{3,7},{4,6},{5,1},{6,4},{7,3},{8,10},{9,13},{10,... | collective-permute-start | bytes 7520264 | tf_op jit(solution)/shard_map/ppermute | solution.py:167
  370.9 80.6 %collective-permute-start.5 = (f32[2,272,1152]{2,1,0:T(8,128)}, f32[2,272,1152]{2,1,0:T(8,128)}, u32[]{:S(2)}, u32[]{:S(2)}) collective-permute-start(f32[2,272,1152]{2,1,0:T(8,128)} %get-tuple-element.74), channel_id=1, source_target_pairs={{0,2},{1,5},{2,0},{3,7},{4,6},{5,1},{6,4},{7,3},{8,10},{9,13},{10,... | collective-permute-start | bytes 7520264 | tf_op jit(solution)/shard_map/ppermute | solution.py:167
  390.2 137.8 %all-to-all-start.2 = ((bf16[8,128,1152]{2,1,0:T(8,128)(2,1)}), bf16[8,128,1152]{2,1,0:T(8,128)(2,1)S(1)}, u32[]{:S(2)}, u32[]{:S(2)}) async-start(bf16[8,128,1152]{2,1,0:T(8,128)(2,1)} %bitcast.425), calls=%async_computation.2 | async-start | bytes 4718592 | tf_op jit(solution)/shard_map/all_to_all | solution.py:292
  403.5 84.3 %collective-permute-start.7 = (f32[4,144,1152]{2,1,0:T(8,128)}, f32[4,144,1152]{2,1,0:T(8,128)}, u32[]{:S(2)}, u32[]{:S(2)}) collective-permute-start(f32[4,144,1152]{2,1,0:T(8,128)} %dynamic-slice_bitcast_fusion), channel_id=1, source_target_pairs={{0,1},{1,0},{2,3},{3,2},{4,5},{5,4},{6,7},{7,6},{8,9},{9,8},{10,11... | collective-permute-start | bytes 7962632 | tf_op jit(solution)/shard_map/ppermute | solution.py:167
  456.5 82.0 %collective-permute-start.27 = (f32[2,272,1152]{2,1,0:T(8,128)}, f32[2,272,1152]{2,1,0:T(8,128)}, u32[]{:S(2)}, u32[]{:S(2)}) collective-permute-start(f32[2,272,1152]{2,1,0:T(8,128)} %fusion.70), channel_id=1, source_target_pairs={{0,4},{1,3},{2,6},{3,1},{4,0},{5,7},{6,2},{7,5},{8,12},{9,11},{10,... | collective-permute-start | bytes 7520264 | tf_op jit(solution)/shard_map/ppermute | solution.py:167
  491.0 10.9 %collective-permute-start.24 = (f32[144,1152]{1,0:T(8,128)}, f32[144,1152]{1,0:T(8,128)S(1)}, u32[]{:S(2)}, u32[]{:S(2)}) collective-permute-start(f32[144,1152]{1,0:T(8,128)} %bitcast_add_fusion.22), channel_id=1, source_target_pairs={{0,2},{1,5},{2,0},{3,7},{4,6},{5,1},{6,4},{7,3},{8,10},{9,13},{10,... | collective-permute-start | bytes 1990664 | tf_op jit(solution)/shard_map/ppermute | solution.py:167
  501.9 33.9 %collective-permute-start.6 = (f32[4,144,1152]{2,1,0:T(8,128)}, f32[4,144,1152]{2,1,0:T(8,128)}, u32[]{:S(2)}, u32[]{:S(2)}) collective-permute-start(f32[4,144,1152]{2,1,0:T(8,128)} %dynamic-slice_bitcast_fusion.3), channel_id=1, source_target_pairs={{0,1},{1,0},{2,3},{3,2},{4,5},{5,4},{6,7},{7,6},{8,9},{9,8},{10,11... | collective-permute-start | bytes 7962632 | tf_op jit(solution)/shard_map/ppermute | solution.py:167
  503.7 17.5 %collective-permute-start.25 = (f32[144,1152]{1,0:T(8,128)S(1)}, f32[144,1152]{1,0:T(8,128)S(1)}, u32[]{:S(2)}, u32[]{:S(2)}) collective-permute-start(f32[144,1152]{1,0:T(8,128)S(1)} %get-tuple-element.81), channel_id=1, source_target_pairs={{0,4},{1,3},{2,6},{3,1},{4,0},{5,7},{6,2},{7,5},{8,12},{9,11},{10,... | collective-permute-start | bytes 1990664 | tf_op jit(solution)/shard_map/ppermute | solution.py:167
  505.2 16.0 %collective-permute-start.23 = (f32[144,1152]{1,0:T(8,128)S(1)}, f32[144,1152]{1,0:T(8,128)S(1)}, u32[]{:S(2)}, u32[]{:S(2)}) collective-permute-start(f32[144,1152]{1,0:T(8,128)S(1)} %get-tuple-element.82), channel_id=1, source_target_pairs={{0,2},{1,5},{2,0},{3,7},{4,6},{5,1},{6,4},{7,3},{8,10},{9,13},{10,... | collective-permute-start | bytes 1990664 | tf_op jit(solution)/shard_map/ppermute | solution.py:167
  521.2 25.2 %collective-permute-start.8 = (f32[4,144,1152]{2,1,0:T(8,128)}, f32[4,144,1152]{2,1,0:T(8,128)}, u32[]{:S(2)}, u32[]{:S(2)}) collective-permute-start(f32[4,144,1152]{2,1,0:T(8,128)} %dynamic-slice_bitcast_fusion.2), channel_id=1, source_target_pairs={{0,1},{1,0},{2,3},{3,2},{4,5},{5,4},{6,7},{7,6},{8,9},{9,8},{10,11... | collective-permute-start | bytes 7962632 | tf_op jit(solution)/shard_map/ppermute | solution.py:167
  522.0 21.9 %collective-permute-start.9 = (f32[4,144,1152]{2,1,0:T(8,128)}, f32[4,144,1152]{2,1,0:T(8,128)}, u32[]{:S(2)}, u32[]{:S(2)}) collective-permute-start(f32[4,144,1152]{2,1,0:T(8,128)} %dynamic-slice_bitcast_fusion.1), channel_id=1, source_target_pairs={{0,1},{1,0},{2,3},{3,2},{4,5},{5,4},{6,7},{7,6},{8,9},{9,8},{10,11... | collective-permute-start | bytes 7962632 | tf_op jit(solution)/shard_map/ppermute | solution.py:167
  535.7 16.2 %slice-start = ((s8[7077888]{0:T(1024)(128)(4,1)}), s8[4194304]{0:T(1024)(128)(4,1)S(1)}, s32[]{:S(2)}) async-start(s8[7077888]{0:T(1024)(128)(4,1)} %bitcast.392), calls=%async_computation.7 | async-start | bytes 8388608
  537.2 14.7 %slice-start.1 = ((s8[7077888]{0:T(1024)(128)(4,1)}), s8[2883584]{0:T(1024)(128)(4,1)S(1)}, s32[]{:S(2)}) async-start(s8[7077888]{0:T(1024)(128)(4,1)} %bitcast.392), calls=%async_computation.8 | async-start | bytes 5767168
  537.3 11.7 %collective-permute-start.15 = (f32[144,1152]{1,0:T(8,128)S(1)}, f32[144,1152]{1,0:T(8,128)S(1)}, u32[]{:S(2)}, u32[]{:S(2)}) collective-permute-start(f32[144,1152]{1,0:T(8,128)S(1)} %bitcast_add_fusion.24), channel_id=1, source_target_pairs={{0,2},{1,5},{2,0},{3,7},{4,6},{5,1},{6,4},{7,3},{8,10},{9,13},{10,... | collective-permute-start | bytes 1990664 | tf_op jit(solution)/shard_map/ppermute | solution.py:167
  545.5 16.4 %collective-permute-start.21 = (f32[144,1152]{1,0:T(8,128)S(1)}, f32[144,1152]{1,0:T(8,128)S(1)}, u32[]{:S(2)}, u32[]{:S(2)}) collective-permute-start(f32[144,1152]{1,0:T(8,128)S(1)} %bitcast_add_fusion.18), channel_id=1, source_target_pairs={{0,2},{1,5},{2,0},{3,7},{4,6},{5,1},{6,4},{7,3},{8,10},{9,13},{10,... | collective-permute-start | bytes 1990664 | tf_op jit(solution)/shard_map/ppermute | solution.py:167
  548.1 17.8 %collective-permute-start.18 = (f32[144,1152]{1,0:T(8,128)S(1)}, f32[144,1152]{1,0:T(8,128)S(1)}, u32[]{:S(2)}, u32[]{:S(2)}) collective-permute-start(f32[144,1152]{1,0:T(8,128)S(1)} %bitcast_add_fusion.20), channel_id=1, source_target_pairs={{0,2},{1,5},{2,0},{3,7},{4,6},{5,1},{6,4},{7,3},{8,10},{9,13},{10,... | collective-permute-start | bytes 1990664 | tf_op jit(solution)/shard_map/ppermute | solution.py:167
  572.9 29.8 %copy-start.5 = (bf16[1024,1152]{1,0:T(8,128)(2,1)S(1)}, bf16[1024,1152]{1,0:T(8,128)(2,1)}, u32[]{:S(2)}) copy-start(bf16[1024,1152]{1,0:T(8,128)(2,1)} %copy-done.4) | copy-start | bytes 7077892
  573.1 5.8 collective-permute-start.10
  575.7 71.7 %collective-permute-start.14 = (f32[144,1152]{1,0:T(8,128)}, f32[144,1152]{1,0:T(8,128)}, u32[]{:S(2)}, u32[]{:S(2)}) collective-permute-start(f32[144,1152]{1,0:T(8,128)} %get-tuple-element.88), channel_id=1, source_target_pairs={{0,2},{1,5},{2,0},{3,7},{4,6},{5,1},{6,4},{7,3},{8,10},{9,13},{10,... | collective-permute-start | bytes 1990664 | tf_op jit(solution)/shard_map/ppermute | solution.py:167
  576.8 77.3 %collective-permute-start.20 = (f32[144,1152]{1,0:T(8,128)}, f32[144,1152]{1,0:T(8,128)}, u32[]{:S(2)}, u32[]{:S(2)}) collective-permute-start(f32[144,1152]{1,0:T(8,128)} %get-tuple-element.84), channel_id=1, source_target_pairs={{0,2},{1,5},{2,0},{3,7},{4,6},{5,1},{6,4},{7,3},{8,10},{9,13},{10,... | collective-permute-start | bytes 1990664 | tf_op jit(solution)/shard_map/ppermute | solution.py:167
  577.7 83.5 %collective-permute-start.17 = (f32[144,1152]{1,0:T(8,128)S(1)}, f32[144,1152]{1,0:T(8,128)}, u32[]{:S(2)}, u32[]{:S(2)}) collective-permute-start(f32[144,1152]{1,0:T(8,128)S(1)} %get-tuple-element.86), channel_id=1, source_target_pairs={{0,2},{1,5},{2,0},{3,7},{4,6},{5,1},{6,4},{7,3},{8,10},{9,13},{10,... | collective-permute-start | bytes 1990664 | tf_op jit(solution)/shard_map/ppermute | solution.py:167
  578.9 22.3 %collective-permute-start.12 = (f32[8,1152]{1,0:T(8,128)S(1)}, f32[8,1152]{1,0:T(8,128)S(1)}, u32[]{:S(2)}, u32[]{:S(2)}) collective-permute-start(f32[8,1152]{1,0:T(8,128)S(1)} %get-tuple-element.90), channel_id=1, source_target_pairs={{0,2},{1,5},{2,0},{3,7},{4,6},{5,1},{6,4},{7,3},{8,10},{9,13},{10,... | collective-permute-start | bytes 110600 | tf_op jit(solution)/shard_map/ppermute | solution.py:167
  579.8 31.7 %collective-permute-start.11 = (f32[8,1152]{1,0:T(8,128)S(1)}, f32[8,1152]{1,0:T(8,128)S(1)}, u32[]{:S(2)}, u32[]{:S(2)}) collective-permute-start(f32[8,1152]{1,0:T(8,128)S(1)} %get-tuple-element.89), channel_id=1, source_target_pairs={{0,2},{1,5},{2,0},{3,7},{4,6},{5,1},{6,4},{7,3},{8,10},{9,13},{10,... | collective-permute-start | bytes 110600 | tf_op jit(solution)/shard_map/ppermute | solution.py:167
  601.2 12.2 %collective-permute-start.13 = (f32[8,1152]{1,0:T(8,128)S(1)}, f32[8,1152]{1,0:T(8,128)S(1)}, u32[]{:S(2)}, u32[]{:S(2)}) collective-permute-start(f32[8,1152]{1,0:T(8,128)S(1)} %bitcast_add_fusion.25), channel_id=1, source_target_pairs={{0,4},{1,3},{2,6},{3,1},{4,0},{5,7},{6,2},{7,5},{8,12},{9,11},{10,... | collective-permute-start | bytes 110600 | tf_op jit(solution)/shard_map/ppermute | solution.py:167
  607.1 56.5 %all-to-all-start.3 = ((bf16[8,128,1152]{2,1,0:T(8,128)(2,1)}), bf16[8,128,1152]{2,1,0:T(8,128)(2,1)}, u32[]{:S(2)}, u32[]{:S(2)}) async-start(bf16[8,128,1152]{2,1,0:T(8,128)(2,1)} %bitcast.402), calls=%async_computation.3 | async-start | bytes 4718592 | tf_op jit(solution)/shard_map/all_to_all | solution.py:309
  611.5 52.1 %copy-start.8 = (bf16[8,128,1152]{2,1,0:T(8,128)(2,1)S(1)}, bf16[8,128,1152]{2,1,0:T(8,128)(2,1)}, u32[]{:S(2)}) copy-start(bf16[8,128,1152]{2,1,0:T(8,128)(2,1)} %copy-done.7) | copy-start | bytes 7077892
  611.5 35.6 %collective-permute-start.16 = (f32[144,1152]{1,0:T(8,128)}, f32[144,1152]{1,0:T(8,128)}, u32[]{:S(2)}, u32[]{:S(2)}) collective-permute-start(f32[144,1152]{1,0:T(8,128)} %get-tuple-element.87), channel_id=1, source_target_pairs={{0,4},{1,3},{2,6},{3,1},{4,0},{5,7},{6,2},{7,5},{8,12},{9,11},{10,... | collective-permute-start | bytes 1990664 | tf_op jit(solution)/shard_map/ppermute | solution.py:167
  613.4 40.7 %collective-permute-start.22 = (f32[144,1152]{1,0:T(8,128)}, f32[144,1152]{1,0:T(8,128)}, u32[]{:S(2)}, u32[]{:S(2)}) collective-permute-start(f32[144,1152]{1,0:T(8,128)} %get-tuple-element.83), channel_id=1, source_target_pairs={{0,4},{1,3},{2,6},{3,1},{4,0},{5,7},{6,2},{7,5},{8,12},{9,11},{10,... | collective-permute-start | bytes 1990664 | tf_op jit(solution)/shard_map/ppermute | solution.py:167
  647.1 14.1 %collective-permute-start.19 = (f32[144,1152]{1,0:T(8,128)}, f32[144,1152]{1,0:T(8,128)S(1)}, u32[]{:S(2)}, u32[]{:S(2)}) collective-permute-start(f32[144,1152]{1,0:T(8,128)} %get-tuple-element.85), channel_id=1, source_target_pairs={{0,4},{1,3},{2,6},{3,1},{4,0},{5,7},{6,2},{7,5},{8,12},{9,11},{10,... | collective-permute-start | bytes 1990664 | tf_op jit(solution)/shard_map/ppermute | solution.py:167
  (57 other events, 392.8 us)
Sparse Core Ops, SparseCore 0:
  10.7 74.5 all-gather.7
  88.2 58.1 all-gather.5
  148.5 67.0 all-gather.9

commit v2 on v1

--- a/solution.py
+++ b/solution.py
@@ -21,6 +21,7 @@
 ALL_AXES = ('dp', 'chip', 'core')
 N_HEADS = 16
 WIN_LANES = 256
+GRAD_COLS = 384
 UNROLL_F = 16
 UNROLL_B = 16
 ATT_SCALE = 1.0 / math.sqrt(HEAD_DIM)
@@ -137,6 +138,41 @@
 
 def attention_backward(qkv, d_mixed):
     return attention_call(attn_bwd, (qkv,) * 3 + (d_mixed,), (0, 1, 2, 0), 3, 5)
+
+
+def qkv_grads(d_ref, h_ref, w_ref, dw_ref, dh_ref, sum_ref, acc):
+    step = pl.program_id(0)
+    d_cols = d_ref[...]
+    dw_ref[...] = dot_tn(d_cols, h_ref[...])
+    sum_ref[...] = jnp.sum(d_cols.astype(F32), axis=0, keepdims=True)
+    part = dot_nn(d_cols, w_ref[...])
+
+    @pl.when(step == 0)
+    def _():
+        acc[...] = part
+
+    @pl.when(step > 0)
+    def _():
+        acc[...] += part
+
+    @pl.when(step == pl.num_programs(0) - 1)
+    def _():
+        dh_ref[...] = acc[...].astype(BF16)
+
+
+def projection_backward(d_qkv, h_one, wqkv):
+    rows, cols = d_qkv.shape
+    block = GRAD_COLS
+    whole = pl.BlockSpec((rows, WIDTH), lambda j: (0, 0))
+    piece = pl.BlockSpec((block, WIDTH), lambda j: (j, 0))
+    return pl.pallas_call(
+        qkv_grads, grid=(cols // block,), name='qkv_grads',
+        out_shape=(jax.ShapeDtypeStruct((cols, WIDTH), F32), jax.ShapeDtypeStruct((rows, WIDTH), BF16), jax.ShapeDtypeStruct((1, cols), F32)),
+        in_specs=[pl.BlockSpec((rows, block), lambda j: (0, j)), whole, piece],
+        out_specs=(piece, whole, pl.BlockSpec((1, block), lambda j: (0, j))),
+        scratch_shapes=[pltpu.VMEM((rows, WIDTH), F32)],
+        cost_estimate=pl.CostEstimate(flops=8 * rows * cols * WIDTH, bytes_accessed=cols * WIDTH * 6 + rows * cols * 2, transcendentals=0),
+    )(d_qkv, h_one, wqkv)
 
 
 def tie(val, *deps):
@@ -188,19 +224,21 @@
         away = lambda k: jnp.where(core0, k * 2 + (1 - cx), (1 - cy) * 2 + k)
         near = lambda k: jnp.where(core0, k * 2 + cx, cy * 2 + k)
 
-        def stage2(own, got, axis):
-            blk = lambda i: pick(own, i, axis) + pick(got, i, axis)
-            send = (blk(away(1 - me)), blk(away(me)))
+        def chip_sums(own, got, axis):
+            return lambda i: pick(own, i, axis) + pick(got, i, axis)
+
+        def stage2(blk):
+            send = lax.optimization_barrier((blk(away(1 - me)), blk(away(me))))
             far = permute(send[0], first)
             close = permute(send[1], first)
             return send, (far, close)
 
-        def stage3(own, got, axis, far):
-            send = pick(own, near(1 - me), axis) + pick(got, near(1 - me), axis) + far
+        def stage3(blk, far):
+            send = lax.optimization_barrier(blk(near(1 - me)) + far)
             return send, permute(send, second)
 
-        def finish(own, got, axis, close, part):
-            return pick(own, near(me), axis) + pick(got, near(me), axis) + close + part
+        def finish(blk, close, part):
+            return blk(near(me)) + close + part
 
         def gather_all(half0, half1):
             return lax.all_gather(jnp.where(dp == 0, half0, half1), ALL_AXES, axis=0, tiled=False).reshape(2, 8, *half0.shape)
@@ -264,7 +302,8 @@
         w2_got = core_swap(w2_oth)
         w2_own = dot_tn(tie(hidden[0], w2_oth), g_out).reshape(blocks)
         w2_all = swap_weights(tie(w2_own_rows, w2_own))
-        w2_send, w2_in = stage2(w2_own, w2_got, 1)
+        w2_blk = chip_sums(w2_own, w2_got, 1)
+        w2_send, w2_in = stage2(w2_blk)
         g_mlp = tie(g_out, *w2_send)
         d_pre = [None, None]
         for c in (0, 1):
@@ -274,7 +313,8 @@
         w1_oth = dot_tn(d_pre[1], h_two).reshape(blocks)
         w1_got = core_swap(w1_oth)
         w1_own = dot_tn(tie(d_pre[0], w1_oth), h_two).reshape(blocks)
-        w1_send, w1_in = stage2(w1_own, w1_got, 1)
+        w1_blk = chip_sums(w1_own, w1_got, 1)
+        w1_send, w1_in = stage2(w1_blk)
         d_pre_t = [tie(d, *w1_send) for d in d_pre]
         d_h_two = (dot_nn(d_pre_t[0], w1_all[0]) + dot_nn(d_pre_t[1], w1_all[1])).astype(BF16)
         d_mid_ln, g_ln2_gain, g_ln2_bias = ln2_pull(d_h_two.astype(F32))
@@ -283,63 +323,53 @@
         dw_o = dot_tn(mixed, d_mid).reshape(CHIPS, 2, QROWS, WIDTH)
         wo_own, wo_oth = pick(dw_o, core, 1), pick(dw_o, 1 - core, 1)
         wo_got = core_swap(wo_oth)
-        w2_last, w2_part = stage3(w2_own, w2_got, 1, w2_in[0])
+        w2_last, w2_part = stage3(w2_blk, w2_in[0])
         mlp_out = dot_nn(tie(hidden[0], d_mixed), w2_all[0])
         mlp_out = mlp_out + dot_nn(hidden[1], w2_all[1])
         y_rows = (mid_f32 + mlp_out + b_2).astype(BF16)
         d_mixed = tie(d_mixed, w2_last).reshape(8, images, toks, WIDTH)
         d_qkv = attention_backward(qkv, d_mixed).reshape(rows, 3 * WIDTH)
         y_out = lax.all_to_all(y_rows.reshape(8, images * toks, WIDTH), tp, 0, 0).reshape(x.shape)
-        w1_last, w1_part = stage3(w1_own, w1_got, 1, w1_in[0])
+        w1_last, w1_part = stage3(w1_blk, w1_in[0])
         d_qkv = tie(d_qkv, w1_last)
-        own, got, sends, ins = {}, {}, {}, {}
-        for n, name in enumerate('qkv'):
-            dw = dot_tn(d_qkv[:, n * WIDTH:(n + 1) * WIDTH], h_one).reshape(CHIPS, 2, QROWS, WIDTH)
-            own[name], oth = pick(dw, core, 1), pick(dw, 1 - core, 1)
-            got[name] = core_swap(oth)
-            d_qkv = tie(d_qkv, oth)
-        sends['q'], ins['q'] = stage2(own['q'], got['q'], 0)
-        wo_send, wo_in = stage2(wo_own, wo_got, 0)
-        d_h_one = dot_nn(tie(d_qkv, *sends['q'], *wo_send), wqkv).astype(BF16)
-        for name in 'kv':
-            sends[name], ins[name] = stage2(own[name], got[name], 0)
-        d_h_one = tie(d_h_one, *sends['k'], *sends['v'])
+        wo_blk = chip_sums(wo_own, wo_got, 0)
+        wo_send, wo_in = stage2(wo_blk)
+        dw_qkv, d_h_one, qkv_sums = projection_backward(tie(d_qkv, *wo_send), h_one, wqkv)
+        dw_qkv = dw_qkv.reshape(3, CHIPS, 2, QROWS, WIDTH)
+        qkv_own, qkv_oth = pick(dw_qkv, core, 2), pick(dw_qkv, 1 - core, 2)
+        qkv_got = core_swap(qkv_oth)
+        d_h_one = tie(d_h_one, qkv_oth)
         d_in_ln, g_ln1_gain, g_ln1_bias = ln1_pull(d_h_one.astype(F32))
         g_x = (d_mid.astype(F32) + d_in_ln).astype(BF16)
+        col_sum = lambda v: jnp.sum(v, axis=0, dtype=F32)
+        vecs = jnp.stack([g_ln1_gain, g_ln1_bias, col_sum(d_mid), g_ln2_gain, g_ln2_bias, col_sum(g_out)])
+        head_sums = qkv_sums.reshape(3, CHIPS, 2, QROWS)
+        mlp_sums = [jnp.transpose(col_sum(d).reshape(2, CHIPS, HALF), (1, 0, 2)).reshape(CHIPS, MLP_PAD) for d in d_pre]
+        mlp_sums = jnp.where(core0, jnp.stack(mlp_sums, 1), jnp.stack(mlp_sums[::-1], 1))
+        bias_sums = jnp.concatenate([head_sums[0], head_sums[2], mlp_sums, jnp.zeros((CHIPS, 2, WIDTH - 2 * QROWS - MLP_PAD), F32)], axis=2)
+        small = jnp.concatenate([jnp.broadcast_to(vecs, (CHIPS, 6, WIDTH)), bias_sums], axis=1)
+        qkv_sum = chip_sums(qkv_own, qkv_got, 1)
+        qkv_blk = lambda i: jnp.concatenate([qkv_sum(i).reshape(3 * QROWS, WIDTH), pick(small, i)])
+        _, qkv_in = stage2(qkv_blk)
         grad_x = lax.all_to_all(g_x.reshape(8, images * toks, WIDTH), tp, 0, 0).reshape(x.shape)
-        _, wo_part = stage3(wo_own, wo_got, 0, wo_in[0])
-        grad_qkv = {}
-        for name in 'qkv':
-            _, last = stage3(own[name], got[name], 0, ins[name][0])
-            grad_qkv[name] = finish(own[name], got[name], 0, ins[name][1], last).astype(BF16)
-
-        grad_w2 = finish(w2_own, w2_got, 1, w2_in[1], w2_part)
+        _, wo_part = stage3(wo_blk, wo_in[0])
+        _, qkv_part = stage3(qkv_blk, qkv_in[0])
+        qkv_all = finish(qkv_blk, qkv_in[1], qkv_part)
+        grad_qkv = qkv_all[:3 * QROWS].reshape(3, QROWS, WIDTH).astype(BF16)
+        small_own = qkv_all[3 * QROWS:]
+        extra = small_own + core_swap(small_own)
+        b_row = pick(extra[6:], core).astype(BF16)
+
+        grad_w2 = finish(w2_blk, w2_in[1], w2_part)
         grad_w2 = grad_w2.reshape(MLP_PAD, WIDTH)[:MLP].astype(BF16)
-        grad_w1 = finish(w1_own, w1_got, 1, w1_in[1], w1_part)
+        grad_w1 = finish(w1_blk, w1_in[1], w1_part)
         grad_w1 = grad_w1.reshape(MLP_PAD, WIDTH)[:MLP].T.astype(BF16)
-        grad_wo = finish(wo_own, wo_got, 0, wo_in[1], wo_part)
+        grad_wo = finish(wo_blk, wo_in[1], wo_part)
         grad_wo = grad_wo.reshape(HEADS, HEAD_DIM, WIDTH).astype(BF16)
         unrow = lambda w: jnp.transpose(w.reshape(HEADS, HEAD_DIM, WIDTH), (2, 0, 1))
 
-        col_sum = lambda v: jnp.sum(v, axis=0, dtype=F32)
-        vecs = jnp.stack([g_ln1_gain, g_ln1_bias, col_sum(d_mid), g_ln2_gain, g_ln2_bias, col_sum(g_out)])
-
-        qkv_sums = col_sum(d_qkv).reshape(3, CHIPS, 2, QROWS)
-
-        def extra_rows(c):
-            sums = pick(qkv_sums, core if c == 0 else 1 - core, 2)
-            b1_sum = jnp.transpose(col_sum(d_pre[c]).reshape(2, CHIPS, HALF), (1, 0, 2)).reshape(CHIPS, MLP_PAD)
-            row = jnp.concatenate([sums[0], sums[2], b1_sum, jnp.zeros((CHIPS, WIDTH - 2 * QROWS - MLP_PAD), F32)], axis=1)
-            return jnp.concatenate([jnp.broadcast_to(vecs, (CHIPS, 6, WIDTH)), row[:, None],
-                                    jnp.zeros((CHIPS, 1, WIDTH), F32)], axis=1)
-
-        ex_own, ex_got = extra_rows(0), core_swap(extra_rows(1))
-        _, ex_in = stage2(ex_own, ex_got, 0)
-        _, ex_part = stage3(ex_own, ex_got, 0, ex_in[0])
-        extra = finish(ex_own, ex_got, 0, ex_in[1], ex_part)
-        b_row = extra[6].astype(BF16)
-        return (y_out, grad_x, extra[0], extra[1], unrow(grad_qkv['q']), b_row[:QROWS].reshape(HEADS, HEAD_DIM),
-                unrow(grad_qkv['k']), unrow(grad_qkv['v']), b_row[QROWS:2 * QROWS].reshape(HEADS, HEAD_DIM), grad_wo,
+        return (y_out, grad_x, extra[0], extra[1], unrow(grad_qkv[0]), b_row[:QROWS].reshape(HEADS, HEAD_DIM),
+                unrow(grad_qkv[1]), unrow(grad_qkv[2]), b_row[QROWS:2 * QROWS].reshape(HEADS, HEAD_DIM), grad_wo,
                 extra[2].astype(BF16), extra[3], extra[4], grad_w1, b_row[2 * QROWS:2 * QROWS + MLP], grad_w2,
                 extra[5].astype(BF16))
 

time: 685 us -> 731 us (1.067)
  waiting for transfers between devices: 213 us -> 287 us
  Pallas kernels: 42.5 us -> 74 us
  matrix products: 180 us -> 156 us
  local copies, waits for them, and re-layouts: 83.7 us -> 66.4 us
  other arithmetic: 99.7 us -> 88.2 us
    ppermute x30 -> x19, waiting for transfers between devices: 91.8 us -> 141 us  [permute(): return lax.ppermute(val, tp, tp_perm(fn))]
    pallas_call x0 -> x1, Pallas kernels: none -> 31.4 us  [projection_backward(): pl.pallas_call(qkv_grads, grid=(cols // block,), name='qkv_grads', out_sh...]
    dot_general x8 -> x2, local copies, waits for them, and re-layouts: 34.5 us -> 11 us  [dot_tn(): lax.dot_general(a, b, (((0,), (0,)), ((), ())), preferred_element_type=F32)]
    dot_general x8 -> x5, matrix products: 61 us -> 42 us  [dot_tn(): lax.dot_general(a, b, (((0,), (0,)), ((), ())), preferred_element_type=F32)]
    all_to_all x1, waiting for transfers between devices: 0.01 us -> 13.2 us  [layer_step(): lax.all_to_all(y_rows.reshape(8, images * toks, WIDTH), tp, 0, 0)]
    dynamic_slice x1 -> x3, local copies, waits for them, and re-layouts: 0.02 us -> 11.7 us  [pick(): return lax.dynamic_index_in_dim(val, idx, axis, keepdims=False)]
    all_to_all x1, waiting for transfers between devices: 0.01 us -> 11.4 us  [layer_step(): lax.all_to_all(g_x.reshape(8, images * toks, WIDTH), tp, 0, 0)]
    concatenate x1 -> x3, other arithmetic: 0.09 us -> 9.61 us  [the longest x1 6.75 us: layer_step(): wqkv = jnp.concatenate([part(0, 0), part(0, QROWS), part(1, 0)])]
  transfers between devices with their start and end apart: 37 -> 26, of which waited for: 12 -> 13; matrix products, arithmetic and copies ran while one was open for 47% -> 35% of each run, Pallas kernels for 6% -> 6%
where the time goes in v2:
time: 731 us; the launch traced here: 722 us
  waiting for transfers between devices  287 us (39%)
  matrix products  156 us (21%)
  other arithmetic  88.2 us (12%)
  Pallas kernels  74 us (10%)
  local copies, waits for them, and re-layouts  66.4 us (9%)
  starting transfers between devices  35.4 us (5%)
  between operations  15.1 us (2%)
    ppermute x19, waiting for transfers between devices, permute(): return lax.ppermute(val, tp, tp_perm(fn))  141 us
    dot_general x6, matrix products, dot_nt(): lax.dot_general(a, b, (((1,), (1,)), ((), ())), preferred_element_type=F32)  70 us
    all_gather x1, waiting for transfers between devices, gather_all(): lax.all_gather(jnp.where(dp == 0, half0, half1), ALL_AXES, axis=0, tiled=...  61 us
    dot_general x5, matrix products, dot_nn(): lax.dot_general(a, b, (((1,), (0,)), ((), ())), preferred_element_type=F32)  43.6 us
    pallas_call x2, Pallas kernels, attention_call(): pl.pallas_call(body, grid=(images,), out_shape=jax.ShapeDtypeStruct((grou...  42.6 us
    dot_general x5, matrix products, dot_tn(): lax.dot_general(a, b, (((0,), (0,)), ((), ())), preferred_element_type=F32)  42 us
    all_to_all x1, waiting for transfers between devices, layer_step(): lax.all_to_all(x.reshape(8, images * toks, WIDTH), tp, 0, 0)  39.6 us
    pallas_call x1, Pallas kernels, projection_backward(): pl.pallas_call(qkv_grads, grid=(cols // block,), name='qkv_grads', out_sh...  31.4 us
  transfers between devices with their start and end apart: 26, of which 13 were waited for; matrix products, arithmetic and copies ran while one was open for 35% of the time, Pallas kernels for 6%

profile of v2, /device:TPU:0, one launch (start us, length us, event | category | flops | bytes accessed | tf_op | source)
XLA Modules:
  0.0 722.0 jit_solution(6727228001060760351)
XLA Ops:
  14.3 5.4 all-to-all-start
  22.2 39.6 %all-to-all-done = bf16[8,128,1152]{2,1,0:T(8,128)(2,1)S(1)} async-done(((bf16[8,128,1152]{2,1,0:T(8,128)(2,1)}), bf16[8,128,1152]{2,1,0:T(8,128)(2,1)S(1)}, u32[]{:S(2)}, u32[]{:S(2)}) %all-to-all-start) | async-done | bytes 2359328 | tf_op jit(solution)/shard_map/all_to_all | solution.py:279
  66.5 18.8 %all-gather.8.cloned.1.call-done = bf16[2176,1152]{1,0:T(8,128)(2,1)} async-done(((bf16[272,1152]{1,0:T(8,128)(2,1)}), bf16[2176,1152]{1,0:T(8,128)(2,1)}) %all-gather.8.cloned.1.call-update) | async-done | bytes 5013520 | tf_op jit(solution)/shard_map/all_gather | solution.py:247
  85.4 61.0 %all-gather.6.cloned.1.call-done = bf16[16,304,1152]{2,1,0:T(8,128)(2,1)} async-done(((bf16[1,304,1152]{2,1,0:T(8,128)(2,1)}), bf16[16,304,1152]{2,1,0:T(8,128)(2,1)}) %all-gather.6.cloned.1.call-update) | async-done | bytes 11206672 | tf_op jit(solution)/shard_map/all_gather | solution.py:244
  148.2 7.8 %fusion.107 = (bf16[1,8,144,1152]{3,2,1,0:T(8,128)(2,1)}, bf16[1,8,144,1152]{3,2,1,0:T(8,128)(2,1)}, bf16[1,8,144,1152]{3,2,1,0:T(8,128)(2,1)}, bf16[1,8,144,1152]{3,2,1,0:T(8,128)(2,1)}) fusion(bf16[2,8,304,1152]{3,2,1,0:T(8,128)(2,1)} %bitcast.300), kind=kLoop, calls=%fused_computation.224 | loop fusion | bytes 21233664 | tf_op jit(solution)/shard_map/slice | solution.py:271
  156.4 15.2 %add_convert_fusion = bf16[1024,3456]{1,0:T(8,128)(2,1)} fusion(bf16[1024,1152]{1,0:T(8,128)(2,1)} %fusion.54.h_ref, f32[3456]{0:T(1024)S(1)} %maximum_convert_fusion, bf16[1152,1152]{1,0:T(8,128)(2,1)} %bitcast.292, bf16[1152,1152]{1,0:T(8,128)(2,1)} %bitcast.294, bf16[1152,1152]{1,0:T(8,128)(2,1)} %bitcast.296), kind=kOutput, calls=%fused_computation.15 | convolution fusion | flops 8184692736 | bytes 17413632 | tf_op jit(solution)/shard_map/dot_general | solution.py:42
  171.5 13.1 %shard_map.296 = bf16[8,4,32,1152]{3,2,1,0:T(8,128)(2,1)} custom-call(bf16[8,4,32,3456]{3,2,1,0:T(8,128)(2,1)} %bitcast.335, bf16[8,4,32,3456]{3,2,1,0:T(8,128)(2,1)} %bitcast.336, bf16[8,4,32,3456]{3,2,1,0:T(8,128)(2,1)} %bitcast.337), custom_call_target="tpu_custom_call" | custom-call | flops 17179869184 | bytes 9437184 | tf_op jit(solution)/shard_map/pallas_call | solution.py:126
  184.6 4.6 all-to-all-start.1
  189.3 6.2 convert_reduce_fusion.4
  197.8 8.8 %fusion.23 = (bf16[1024,2176]{1,0:T(8,128)(2,1)}, bf16[1024,2176]{1,0:T(8,128)(2,1)}) fusion(f32[2176]{0:T(1024)S(1)} %reshape.427, bf16[1024,1152]{1,0:T(8,128)(2,1)S(1)} %fusion.41, bf16[2176,1152]{1,0:T(8,128)(2,1)S(1)} %bitcast.332), kind=kOutput, calls=%fused_computation.37 | convolution fusion | flops 5160566784 | bytes 16294400 | tf_op jit(solution)/shard_map/dot_general | solution.py:42
  206.8 11.2 %fusion.19 = (bf16[2176,1024]{0,1:T(8,128)(2,1)}, bf16[1024,2176]{1,0:T(8,128)(2,1)}) fusion(f32[2176]{0:T(1024)S(1)} %reshape.428, bf16[1024,1152]{1,0:T(8,128)(2,1)S(1)} %fusion.41, bf16[2176,1152]{1,0:T(8,128)(2,1)} %collective-permute-done), kind=kOutput, calls=%fused_computation.33 | convolution fusion | flops 5160566784 | bytes 16294400 | tf_op jit(solution)/shard_map/dot_general | solution.py:42
  217.9 6.5 copy.116
  227.0 11.1 %fusion.109 = f32[2,4,272,1152]{3,2,1,0:T(8,128)} fusion(bf16[2,4,272,1024]{3,2,1,0:T(8,128)(2,1)} %bitcast.308, bf16[1024,1152,1,1]{1,0,3,2:T(8,128)(2,1)} %bitcast.27), kind=kOutput, calls=%fused_computation.226 | convolution fusion | flops 5133828096 | bytes 16842752 | tf_op jit(solution)/shard_map/dot_general | solution.py:50
  238.1 6.5 copy.117
  244.6 10.7 %fusion.110 = f32[2,4,272,1152]{3,2,1,0:T(8,128)} fusion(bf16[2,4,272,1024]{3,2,1,0:T(8,128)(2,1)} %bitcast.309, bf16[1024,1152,1,1]{1,0,3,2:T(8,128)(2,1)} %bitcast.27), kind=kOutput, calls=%fused_computation.227 | convolution fusion | flops 5133828096 | bytes 16842752 | tf_op jit(solution)/shard_map/dot_general | solution.py:50
  255.8 7.1 fusion.71
  263.0 15.8 %convert_reduce_fusion.1 = (f32[2176]{0:T(1024)}, bf16[1024,2176]{1,0:T(8,128)(2,1)}) fusion(bf16[1024,2176]{1,0:T(8,128)(2,1)} %get-tuple-element.127, bf16[1024,1152]{1,0:T(8,128)(2,1)} %bitcast.23, bf16[2176,1152]{1,0:T(8,128)(2,1)S(1)} %copy-done.37), kind=kOutput, calls=%fused_computation.47 | convolution fusion | flops 5189531648 | bytes 16294400 | tf_op jit(solution)/shard_map/dot_general | solution.py:42
  278.7 14.3 %convert_reduce_fusion = (f32[2176]{0:T(1024)}, bf16[1024,2176]{1,0:T(8,128)(2,1)S(1)}) fusion(bf16[1024,2176]{1,0:T(8,128)(2,1)S(1)} %bitcast.348, bf16[1024,1152]{1,0:T(8,128)(2,1)} %bitcast.23, bf16[2176,1152]{1,0:T(8,128)(2,1)} %collective-permute-done.2), kind=kOutput, calls=%fused_computation.46 | convolution fusion | flops 5189531648 | bytes 16294400 | tf_op jit(solution)/shard_map/dot_general | solution.py:42
  293.0 8.7 %fusion.111 = f32[2176,1152]{1,0:T(8,128)} fusion(bf16[1024,2176]{1,0:T(8,128)(2,1)S(1)} %get-tuple-element.54, bf16[1024,1152]{1,0:T(8,128)(2,1)S(1)} %fusion.41), kind=kOutput, calls=%fused_computation.228 | convolution fusion | flops 5133828096 | bytes 16842752 | tf_op jit(solution)/shard_map/dot_general | solution.py:50
  302.3 4.4 copy.130
  306.8 6.7 pad_maximum_fusion.w_ref
  313.5 8.3 %fusion.112 = f32[2176,1152]{1,0:T(8,128)S(1)} fusion(bf16[1024,2176]{1,0:T(8,128)(2,1)} %get-tuple-element.53, bf16[1024,1152]{1,0:T(8,128)(2,1)S(1)} %copy-done.15), kind=kOutput, calls=%fused_computation.229 | convolution fusion | flops 5133828096 | bytes 16842752 | tf_op jit(solution)/shard_map/dot_general | solution.py:50
  321.8 10.6 %collective-permute-done.4 = f32[2,272,1152]{2,1,0:T(8,128)} collective-permute-done((f32[2,272,1152]{2,1,0:T(8,128)}, f32[2,272,1152]{2,1,0:T(8,128)}, u32[]{:S(2)}, u32[]{:S(2)}) %collective-permute-start.4) | collective-permute-done | bytes 2506784 | tf_op jit(solution)/shard_map/ppermute | solution.py:203
  332.5 5.2 fusion.68
  337.7 5.9 fusion.69
  344.0 6.2 fusion.113
  350.2 9.8 %convert_reduce_fusion.3 = (f32[1152]{0:T(1024)S(1)}, f32[1024]{0:T(1024)S(1)}, bf16[1024,1152]{1,0:T(8,128)(2,1)S(1)}) fusion(f32[1152]{0:T(1024)S(1)} %copy-done.21, f32[1024]{0:T(1024)S(1)} %broadcast_multiply_fusion, bf16[1024,1152]{1,0:T(8,128)(2,1)S(1)} %copy-done.3, f32[1024,1152]{1,0:T(8,128)S(1)} %fusion.113, bf16[1024,2176]{1,0:T(8,128)(2,1)S(1)} %bitcast.346, ...), kind=kOutput, calls=%fused_computation.57 | convolution fusion | flops 5144442880 | bytes 18924544 | tf_op jit(solution)/shard_map/dot_general | solution.py:46
  362.9 3.7 convert_reduce_fusion.5
  366.7 4.8 convolution_convert_fusion.2
  378.7 29.5 %shard_map.297 = bf16[8,4,32,3456]{3,2,1,0:T(8,128)(2,1)} custom-call(bf16[8,4,32,3456]{3,2,1,0:T(8,128)(2,1)} %bitcast.338, bf16[8,4,32,3456]{3,2,1,0:T(8,128)(2,1)} %bitcast.339, bf16[8,4,32,3456]{3,2,1,0:T(8,128)(2,1)} %bitcast.340, bf16[8,4,32,1152]{3,2,1,0:T(8,128)(2,1)} %bitcast.342), custom_call_target="tpu_custom_call" | custom-call | flops 42949672960 | bytes 16515072 | tf_op jit(solution)/shard_map/pallas_call | solution.py:126
  408.2 5.1 fusion.66
  416.2 31.4 %qkv_grads.1 = (f32[3456,1152]{1,0:T(8,128)}, bf16[1024,1152]{1,0:T(8,128)(2,1)}, f32[1,3456]{1,0:T(1,128)}) custom-call(bf16[1024,3456]{1,0:T(8,128)(2,1)} %bitcast.341, bf16[1024,1152]{1,0:T(8,128)(2,1)} %fusion.54.h_ref, bf16[3456,1152]{1,0:T(8,128)(2,1)} %pad_maximum_fusion.w_ref), custom_call_target="tpu_custom_call" | custom-call | flops 32614907904 | bytes 30965760 | tf_op jit(solution)/shard_map/qkv_grads/pallas_call | solution.py:168
  447.7 7.0 dynamic-slice_bitcast_fusion
  457.4 9.7 %fusion.114 = f32[1024,1152]{1,0:T(8,128)S(1)} fusion(bf16[1024,2176]{1,0:T(8,128)(2,1)} %get-tuple-element.55, bf16[2176,1152]{1,0:T(8,128)(2,1)} %all-gather.10.cloned.1.call-done), kind=kOutput, calls=%fused_computation.231 | convolution fusion | flops 5133828096 | bytes 14188544 | tf_op jit(solution)/shard_map/dot_general | solution.py:46
  467.2 11.7 %fusion.47 = bf16[1024,1152]{1,0:T(8,128)(2,1)} fusion(bf16[1024,1152]{1,0:T(8,128)(2,1)S(1)} %copy-done.3, f32[1024,1152]{1,0:T(8,128)S(1)} %fusion.114, bf16[2176,1152]{1,0:T(8,128)(2,1)} %collective-permute-done.2, bf16[1024,2176]{1,0:T(8,128)(2,1)S(1)} %bitcast.350, f32[1152]{0:T(1024)S(1)} %convert_element_type.213), kind=kOutput, calls=%fused_computation.82 | convolution fusion | flops 5162008576 | bytes 18911744 | tf_op jit(solution)/shard_map/dot_general | solution.py:46
  478.8 4.7 all-to-all-start.2
  486.1 26.6 %collective-permute-done.17 = f32[2,272,1152]{2,1,0:T(8,128)} collective-permute-done((f32[2,272,1152]{2,1,0:T(8,128)}, f32[2,272,1152]{2,1,0:T(8,128)}, u32[]{:S(2)}, u32[]{:S(2)}) %collective-permute-start.17) | collective-permute-done | bytes 2506784 | tf_op jit(solution)/shard_map/ppermute | solution.py:203
  514.4 5.4 fusion.74
  519.8 6.6 collective-permute-start.15
  526.5 13.2 %all-to-all-done.2 = bf16[8,128,1152]{2,1,0:T(8,128)(2,1)} async-done(((bf16[8,128,1152]{2,1,0:T(8,128)(2,1)}), bf16[8,128,1152]{2,1,0:T(8,128)(2,1)}, u32[]{:S(2)}, u32[]{:S(2)}) %all-to-all-start.2) | async-done | bytes 2359328 | tf_op jit(solution)/shard_map/all_to_all | solution.py:332
  549.1 5.8 constant_dynamic-slice_fusion.5
  554.9 5.9 constant_dynamic-slice_fusion.4
  568.7 3.6 all-to-all-start.3
  572.3 32.1 %collective-permute-done.13 = f32[144,1152]{1,0:T(8,128)} collective-permute-done((f32[144,1152]{1,0:T(8,128)}, f32[144,1152]{1,0:T(8,128)}, u32[]{:S(2)}, u32[]{:S(2)}) %collective-permute-start.13) | collective-permute-done | bytes 663584 | tf_op jit(solution)/shard_map/ppermute | solution.py:203
  608.7 38.5 %collective-permute-done.9 = f32[440,1152]{1,0:T(8,128)} collective-permute-done((f32[440,1152]{1,0:T(8,128)}, f32[440,1152]{1,0:T(8,128)}, u32[]{:S(2)}, u32[]{:S(2)}) %collective-permute-start.9) | collective-permute-done | bytes 2027552 | tf_op jit(solution)/shard_map/ppermute | solution.py:203
  655.1 11.4 %all-to-all-done.3 = bf16[8,128,1152]{2,1,0:T(8,128)(2,1)S(1)} async-done(((bf16[8,128,1152]{2,1,0:T(8,128)(2,1)}), bf16[8,128,1152]{2,1,0:T(8,128)(2,1)S(1)}, u32[]{:S(2)}, u32[]{:S(2)}) %all-to-all-start.3) | async-done | bytes 2359328 | tf_op jit(solution)/shard_map/all_to_all | solution.py:354
  666.5 4.5 fusion.76
  672.4 30.9 %collective-permute-done.8 = f32[440,1152]{1,0:T(8,128)} collective-permute-done((f32[440,1152]{1,0:T(8,128)}, f32[440,1152]{1,0:T(8,128)}, u32[]{:S(2)}, u32[]{:S(2)}) %collective-permute-start.8) | collective-permute-done | bytes 2027552 | tf_op jit(solution)/shard_map/ppermute | solution.py:203
  (242 shorter events, 85.1 us)
Async XLA Ops:
  7.2 78.2 %all-gather.8.cloned.1.call-start = ((), (), s32[]{:S(2)}) async-start(), calls=%async_computation.5 | async-start | bytes 5640192 | tf_op jit(solution)/shard_map/all_gather | solution.py:247
  9.5 136.8 %all-gather.6.cloned.1.call-start = ((), (), s32[]{:S(2)}) async-start(), calls=%async_computation.4 | async-start | bytes 11907072 | tf_op jit(solution)/shard_map/all_gather | solution.py:244
  14.3 47.5 %all-to-all-start = ((bf16[8,128,1152]{2,1,0:T(8,128)(2,1)}), bf16[8,128,1152]{2,1,0:T(8,128)(2,1)S(1)}, u32[]{:S(2)}, u32[]{:S(2)}) async-start(bf16[8,128,1152]{2,1,0:T(8,128)(2,1)} %bitcast.313), calls=%async_computation | async-start | bytes 4718592 | tf_op jit(solution)/shard_map/all_to_all | solution.py:279
  19.8 44.4 %copy-start.17 = (f32[1152]{0:T(1024)S(1)}, f32[1152]{0:T(1024)}, u32[]{:S(2)}) copy-start(f32[1152]{0:T(1024)} %param.19) | copy-start | bytes 13828
  19.8 44.4 %copy-start.32 = (f32[1152]{0:T(1024)S(1)}, f32[1152]{0:T(1024)}, u32[]{:S(2)}) copy-start(f32[1152]{0:T(1024)} %param.20) | copy-start | bytes 13828
  19.8 235.6 %all-gather.10.cloned.1.call-start = ((), (), s32[]{:S(2)}) async-start(), calls=%async_computation.6 | async-start | bytes 5640192 | tf_op jit(solution)/shard_map/all_gather | solution.py:247
  61.8 127.4 %copy-start = (bf16[8,128,1152]{2,1,0:T(8,128)(2,1)}, bf16[8,128,1152]{2,1,0:T(8,128)(2,1)S(1)}, u32[]{:S(2)}) copy-start(bf16[8,128,1152]{2,1,0:T(8,128)(2,1)S(1)} %all-to-all-done) | copy-start | bytes 7077892
  85.4 121.4 %collective-permute-start = (bf16[2176,1152]{1,0:T(8,128)(2,1)}, bf16[2176,1152]{1,0:T(8,128)(2,1)}, u32[]{:S(2)}, u32[]{:S(2)}) collective-permute-start(bf16[2176,1152]{1,0:T(8,128)(2,1)} %all-gather.8.cloned.1.call-done), channel_id=1, source_target_pairs={{0,1},{1,0},{2,3},{3,2},{4,5},{5,4},{6,7},{7,6},{8,9},{9,8},{10,11... | collective-permute-start | bytes 15040520 | tf_op jit(solution)/shard_map/ppermute | solution.py:203
  184.6 42.4 %all-to-all-start.1 = ((bf16[8,128,1152]{2,1,0:T(8,128)(2,1)}), bf16[8,128,1152]{2,1,0:T(8,128)(2,1)}, u32[]{:S(2)}, u32[]{:S(2)}) async-start(bf16[8,128,1152]{2,1,0:T(8,128)(2,1)} %bitcast.314), calls=%async_computation.1 | async-start | bytes 4718592 | tf_op jit(solution)/shard_map/all_to_all | solution.py:287
  196.2 10.4 %copy-start.28 = (f32[1024]{0:T(1024)}, f32[1024]{0:T(1024)S(1)}, u32[]{:S(2)}) copy-start(f32[1024]{0:T(1024)S(1)} %fusion.44) | copy-start | bytes 12292
  196.9 9.8 %copy-start.24 = (f32[1024]{0:T(1024)}, f32[1024]{0:T(1024)S(1)}, u32[]{:S(2)}) copy-start(f32[1024]{0:T(1024)S(1)} %fusion.98) | copy-start | bytes 12292
  197.8 95.2 %copy-start.14 = (bf16[1024,1152]{1,0:T(8,128)(2,1)}, bf16[1024,1152]{1,0:T(8,128)(2,1)S(1)}, u32[]{:S(2)}) copy-start(bf16[1024,1152]{1,0:T(8,128)(2,1)S(1)} %fusion.41) | copy-start | bytes 7077892
  238.1 17.7 %collective-permute-start.1 = (f32[2,4,272,1152]{3,2,1,0:T(8,128)}, f32[2,4,272,1152]{3,2,1,0:T(8,128)}, u32[]{:S(2)}, u32[]{:S(2)}) collective-permute-start(f32[2,4,272,1152]{3,2,1,0:T(8,128)} %fusion.109), channel_id=1, source_target_pairs={{0,1},{1,0},{2,3},{3,2},{4,5},{5,4},{6,7},{7,6},{8,9},{9,8},{10,11... | collective-permute-start | bytes 30081032 | tf_op jit(solution)/shard_map/ppermute | solution.py:203
  255.3 23.4 %collective-permute-start.2 = (bf16[2176,1152]{1,0:T(8,128)(2,1)}, bf16[2176,1152]{1,0:T(8,128)(2,1)}, u32[]{:S(2)}, u32[]{:S(2)}) collective-permute-start(bf16[2176,1152]{1,0:T(8,128)(2,1)} %all-gather.10.cloned.1.call-done), channel_id=1, source_target_pairs={{0,1},{1,0},{2,3},{3,2},{4,5},{5,4},{6,7},{7,6},{8,9},{9,8},{10,11... | collective-permute-start | bytes 15040520 | tf_op jit(solution)/shard_map/ppermute | solution.py:203
  255.8 22.9 %slice-start.8 = ((s8[4456448]{0:T(1024)(128)(4,1)}), s8[4194304]{0:T(1024)(128)(4,1)S(1)}, s32[]{:S(2)}) async-start(s8[4456448]{0:T(1024)(128)(4,1)} %bitcast.347), calls=%async_computation.15 | async-start | bytes 8388608
  263.0 15.8 %slice-start.9 = ((s8[4456448]{0:T(1024)(128)(4,1)}), s8[262144]{0:T(1024)(128)(4,1)S(1)}, s32[]{:S(2)}) async-start(s8[4456448]{0:T(1024)(128)(4,1)} %bitcast.347), calls=%async_computation.16 | async-start | bytes 524288
  293.0 8.7 %copy-start.38 = (bf16[1024,2176]{1,0:T(8,128)(2,1)}, bf16[1024,2176]{1,0:T(8,128)(2,1)S(1)}, u32[]{:S(2)}) copy-start(bf16[1024,2176]{1,0:T(8,128)(2,1)S(1)} %get-tuple-element.54) | copy-start | bytes 13369348
  301.7 36.0 %collective-permute-start.3 = (f32[2,4,272,1152]{3,2,1,0:T(8,128)}, f32[2,4,272,1152]{3,2,1,0:T(8,128)}, u32[]{:S(2)}, u32[]{:S(2)}) collective-permute-start(f32[2,4,272,1152]{3,2,1,0:T(8,128)} %bitcast.32), channel_id=1, source_target_pairs={{0,1},{1,0},{2,3},{3,2},{4,5},{5,4},{6,7},{7,6},{8,9},{9,8},{10,11... | collective-permute-start | bytes 30081032 | tf_op jit(solution)/shard_map/ppermute | solution.py:203
  301.7 30.8 %collective-permute-start.4 = (f32[2,272,1152]{2,1,0:T(8,128)}, f32[2,272,1152]{2,1,0:T(8,128)}, u32[]{:S(2)}, u32[]{:S(2)}) collective-permute-start(f32[2,272,1152]{2,1,0:T(8,128)} %get-tuple-element.45), channel_id=1, source_target_pairs={{0,2},{1,5},{2,0},{3,7},{4,6},{5,1},{6,4},{7,3},{8,10},{9,13},{10,... | collective-permute-start | bytes 7520264 | tf_op jit(solution)/shard_map/ppermute | solution.py:203
  321.8 15.8 %copy-start.7 = (f32[2176,1152]{1,0:T(8,128)}, f32[2176,1152]{1,0:T(8,128)S(1)}, u32[]{:S(2)}) copy-start(f32[2176,1152]{1,0:T(8,128)S(1)} %fusion.112) | copy-start | bytes 30081028
  332.5 11.5 %slice-start.2 = ((s8[5013504]{0:T(1024)(128)(4,1)}), s8[4194304]{0:T(1024)(128)(4,1)S(1)}, s32[]{:S(2)}) async-start(s8[5013504]{0:T(1024)(128)(4,1)} %bitcast.333), calls=%async_computation.9 | async-start | bytes 8388608
  332.5 11.5 %slice-start.4 = ((s8[4456448]{0:T(1024)(128)(4,1)}), s8[4194304]{0:T(1024)(128)(4,1)S(1)}, s32[]{:S(2)}) async-start(s8[4456448]{0:T(1024)(128)(4,1)} %bitcast.343), calls=%async_computation.11 | async-start | bytes 8388608
  343.6 64.6 %collective-permute-start.5 = (f32[2,272,1152]{2,1,0:T(8,128)}, f32[2,272,1152]{2,1,0:T(8,128)}, u32[]{:S(2)}, u32[]{:S(2)}) collective-permute-start(f32[2,272,1152]{2,1,0:T(8,128)} %get-tuple-element.51), channel_id=1, source_target_pairs={{0,2},{1,5},{2,0},{3,7},{4,6},{5,1},{6,4},{7,3},{8,10},{9,13},{10,... | collective-permute-start | bytes 7520264 | tf_op jit(solution)/shard_map/ppermute | solution.py:203
  350.2 9.9 %copy-start.29 = (f32[1024]{0:T(1024)S(1)}, f32[1024]{0:T(1024)}, u32[]{:S(2)}) copy-start(f32[1024]{0:T(1024)} %copy-done.28) | copy-start | bytes 12292
  350.2 9.9 %copy-start.25 = (f32[1024]{0:T(1024)S(1)}, f32[1024]{0:T(1024)}, u32[]{:S(2)}) copy-start(f32[1024]{0:T(1024)} %copy-done.24) | copy-start | bytes 12292
  378.7 34.6 %collective-permute-start.6 = (f32[4,144,1152]{2,1,0:T(8,128)}, f32[4,144,1152]{2,1,0:T(8,128)}, u32[]{:S(2)}, u32[]{:S(2)}) collective-permute-start(f32[4,144,1152]{2,1,0:T(8,128)} %dynamic-slice_bitcast_fusion.1), channel_id=1, source_target_pairs={{0,1},{1,0},{2,3},{3,2},{4,5},{5,4},{6,7},{7,6},{8,9},{9,8},{10,11... | collective-permute-start | bytes 7962632 | tf_op jit(solution)/shard_map/ppermute | solution.py:203
  454.6 100.2 %collective-permute-start.7 = (f32[3,4,144,1152]{3,2,1,0:T(8,128)}, f32[3,4,144,1152]{3,2,1,0:T(8,128)}, u32[]{:S(2)}, u32[]{:S(2)}) collective-permute-start(f32[3,4,144,1152]{3,2,1,0:T(8,128)} %dynamic-slice_bitcast_fusion), channel_id=1, source_target_pairs={{0,1},{1,0},{2,3},{3,2},{4,5},{5,4},{6,7},{7,6},{8,9},{9,8},{10,11... | collective-permute-start | bytes 23887880 | tf_op jit(solution)/shard_map/ppermute | solution.py:203
  455.1 12.1 %slice-start.10 = ((s8[4456448]{0:T(1024)(128)(4,1)}), s8[4194304]{0:T(1024)(128)(4,1)S(1)}, s32[]{:S(2)}) async-start(s8[4456448]{0:T(1024)(128)(4,1)} %bitcast.349), calls=%async_computation.17 | async-start | bytes 8388608
  455.1 12.1 %slice-start.11 = ((s8[4456448]{0:T(1024)(128)(4,1)}), s8[262144]{0:T(1024)(128)(4,1)S(1)}, s32[]{:S(2)}) async-start(s8[4456448]{0:T(1024)(128)(4,1)} %bitcast.349), calls=%async_computation.18 | async-start | bytes 524288
  455.1 57.6 %collective-permute-start.17 = (f32[2,272,1152]{2,1,0:T(8,128)}, f32[2,272,1152]{2,1,0:T(8,128)}, u32[]{:S(2)}, u32[]{:S(2)}) collective-permute-start(f32[2,272,1152]{2,1,0:T(8,128)} %get-tuple-element.46), channel_id=1, source_target_pairs={{0,2},{1,5},{2,0},{3,7},{4,6},{5,1},{6,4},{7,3},{8,10},{9,13},{10,... | collective-permute-start | bytes 7520264 | tf_op jit(solution)/shard_map/ppermute | solution.py:203
  456.8 57.6 %collective-permute-start.18 = (f32[2,272,1152]{2,1,0:T(8,128)}, f32[2,272,1152]{2,1,0:T(8,128)}, u32[]{:S(2)}, u32[]{:S(2)}) collective-permute-start(f32[2,272,1152]{2,1,0:T(8,128)} %fusion.68), channel_id=1, source_target_pairs={{0,4},{1,3},{2,6},{3,1},{4,0},{5,7},{6,2},{7,5},{8,12},{9,11},{10,... | collective-permute-start | bytes 7520264 | tf_op jit(solution)/shard_map/ppermute | solution.py:203
  478.8 60.9 %all-to-all-start.2 = ((bf16[8,128,1152]{2,1,0:T(8,128)(2,1)}), bf16[8,128,1152]{2,1,0:T(8,128)(2,1)}, u32[]{:S(2)}, u32[]{:S(2)}) async-start(bf16[8,128,1152]{2,1,0:T(8,128)(2,1)} %bitcast.317), calls=%async_computation.2 | async-start | bytes 4718592 | tf_op jit(solution)/shard_map/all_to_all | solution.py:332
  486.1 56.3 %copy-start.34 = (f32[1,3456]{1,0:T(1,128)S(1)}, f32[1,3456]{1,0:T(1,128)}, u32[]{:S(2)}) copy-start(f32[1,3456]{1,0:T(1,128)} %get-tuple-element.64) | copy-start | bytes 41476
  486.1 56.7 %copy-start.1 = (bf16[8,128,1152]{2,1,0:T(8,128)(2,1)S(1)}, bf16[8,128,1152]{2,1,0:T(8,128)(2,1)}, u32[]{:S(2)}) copy-start(bf16[8,128,1152]{2,1,0:T(8,128)(2,1)} %copy-done) | copy-start | bytes 7077892
  486.1 56.7 %copy-start.18 = (f32[1152]{0:T(1024)S(1)}, f32[1152]{0:T(1024)}, u32[]{:S(2)}) copy-start(f32[1152]{0:T(1024)} %param.19) | copy-start | bytes 13828
  486.1 56.7 %copy-start.20 = (f32[1024]{0:T(1024)S(1)}, f32[1024]{0:T(1024)}, u32[]{:S(2)}) copy-start(f32[1024]{0:T(1024)} %copy-done.19) | copy-start | bytes 12292
  519.8 26.2 %copy-start.27 = (f32[8,128]{1,0:T(8,128)S(1)}, f32[8,128]{1,0:T(8,128)}, u32[]{:S(2)}) copy-start(f32[8,128]{1,0:T(8,128)} %copy-done.26) | copy-start | bytes 12292
  519.8 26.3 %copy-start.23 = (f32[1024]{0:T(1024)S(1)}, f32[1024]{0:T(1024)}, u32[]{:S(2)}) copy-start(f32[1024]{0:T(1024)} %copy-done.22) | copy-start | bytes 12292
  519.8 146.7 %collective-permute-start.15 = (f32[2,272,1152]{2,1,0:T(8,128)}, f32[2,272,1152]{2,1,0:T(8,128)}, u32[]{:S(2)}, u32[]{:S(2)}) collective-permute-start(f32[2,272,1152]{2,1,0:T(8,128)} %get-tuple-element.52), channel_id=1, source_target_pairs={{0,2},{1,5},{2,0},{3,7},{4,6},{5,1},{6,4},{7,3},{8,10},{9,13},{10,... | collective-permute-start | bytes 7520264 | tf_op jit(solution)/shard_map/ppermute | solution.py:203
  539.7 126.8 %collective-permute-start.16 = (f32[2,272,1152]{2,1,0:T(8,128)}, f32[2,272,1152]{2,1,0:T(8,128)}, u32[]{:S(2)}, u32[]{:S(2)}) collective-permute-start(f32[2,272,1152]{2,1,0:T(8,128)} %fusion.66), channel_id=1, source_target_pairs={{0,4},{1,3},{2,6},{3,1},{4,0},{5,7},{6,2},{7,5},{8,12},{9,11},{10,... | collective-permute-start | bytes 7520264 | tf_op jit(solution)/shard_map/ppermute | solution.py:203
  540.3 64.1 %collective-permute-start.13 = (f32[144,1152]{1,0:T(8,128)}, f32[144,1152]{1,0:T(8,128)}, u32[]{:S(2)}, u32[]{:S(2)}) collective-permute-start(f32[144,1152]{1,0:T(8,128)} %get-tuple-element.58), channel_id=1, source_target_pairs={{0,2},{1,5},{2,0},{3,7},{4,6},{5,1},{6,4},{7,3},{8,10},{9,13},{10,... | collective-permute-start | bytes 1990664 | tf_op jit(solution)/shard_map/ppermute | solution.py:203
  540.6 111.1 %collective-permute-start.12 = (f32[144,1152]{1,0:T(8,128)}, f32[144,1152]{1,0:T(8,128)S(1)}, u32[]{:S(2)}, u32[]{:S(2)}) collective-permute-start(f32[144,1152]{1,0:T(8,128)} %get-tuple-element.59), channel_id=1, source_target_pairs={{0,2},{1,5},{2,0},{3,7},{4,6},{5,1},{6,4},{7,3},{8,10},{9,13},{10,... | collective-permute-start | bytes 1990664 | tf_op jit(solution)/shard_map/ppermute | solution.py:203
  564.0 83.2 %collective-permute-start.9 = (f32[440,1152]{1,0:T(8,128)}, f32[440,1152]{1,0:T(8,128)}, u32[]{:S(2)}, u32[]{:S(2)}) collective-permute-start(f32[440,1152]{1,0:T(8,128)} %pad_maximum_fusion.1), channel_id=1, source_target_pairs={{0,2},{1,5},{2,0},{3,7},{4,6},{5,1},{6,4},{7,3},{8,10},{9,13},{10,... | collective-permute-start | bytes 6082568 | tf_op jit(solution)/shard_map/ppermute | solution.py:203
  568.7 97.8 %all-to-all-start.3 = ((bf16[8,128,1152]{2,1,0:T(8,128)(2,1)}), bf16[8,128,1152]{2,1,0:T(8,128)(2,1)S(1)}, u32[]{:S(2)}, u32[]{:S(2)}) async-start(bf16[8,128,1152]{2,1,0:T(8,128)(2,1)} %bitcast.305), calls=%async_computation.3 | async-start | bytes 4718592 | tf_op jit(solution)/shard_map/all_to_all | solution.py:354
  606.0 46.9 %collective-permute-start.14 = (f32[144,1152]{1,0:T(8,128)S(1)}, f32[144,1152]{1,0:T(8,128)S(1)}, u32[]{:S(2)}, u32[]{:S(2)}) collective-permute-start(f32[144,1152]{1,0:T(8,128)S(1)} %fusion.80), channel_id=1, source_target_pairs={{0,4},{1,3},{2,6},{3,1},{4,0},{5,7},{6,2},{7,5},{8,12},{9,11},{10,... | collective-permute-start | bytes 1990664 | tf_op jit(solution)/shard_map/ppermute | solution.py:203
  647.2 56.1 %collective-permute-start.8 = (f32[440,1152]{1,0:T(8,128)}, f32[440,1152]{1,0:T(8,128)}, u32[]{:S(2)}, u32[]{:S(2)}) collective-permute-start(f32[440,1152]{1,0:T(8,128)} %pad_maximum_fusion.2), channel_id=1, source_target_pairs={{0,2},{1,5},{2,0},{3,7},{4,6},{5,1},{6,4},{7,3},{8,10},{9,13},{10,... | collective-permute-start | bytes 6082568 | tf_op jit(solution)/shard_map/ppermute | solution.py:203
  651.7 51.6 %collective-permute-start.10 = (f32[440,1152]{1,0:T(8,128)}, f32[440,1152]{1,0:T(8,128)}, u32[]{:S(2)}, u32[]{:S(2)}) collective-permute-start(f32[440,1152]{1,0:T(8,128)} %maximum_add_fusion.1), channel_id=1, source_target_pairs={{0,4},{1,3},{2,6},{3,1},{4,0},{5,7},{6,2},{7,5},{8,12},{9,11},{10,... | collective-permute-start | bytes 6082568 | tf_op jit(solution)/shard_map/ppermute | solution.py:203
  705.8 1.2 collective-permute-start.11
  (29 other events, 152.9 us)
Sparse Core Ops, SparseCore 0:
  10.7 74.5 all-gather.7
  88.2 58.1 all-gather.5
  148.5 67.2 all-gather.9

commit v3 on v2

--- a/solution.py
+++ b/solution.py
@@ -264,7 +264,7 @@
         att = gather_all(att0, att1)
         w1_rows = jnp.pad(w_1.T, ((0, MLP_PAD - MLP), (0, 0)))
         w2_rows = jnp.pad(w_2, ((0, MLP_PAD - MLP), (0, 0)))
-        w1_all = swap_weights(gather_own(w1_rows[:HALF], w1_rows[HALF:]))
+        w1_own_rows = gather_own(w1_rows[:HALF], w1_rows[HALF:])
         w2_own_rows = gather_own(w2_rows[:HALF], w2_rows[HALF:])
 
         flat = CHIPS * QROWS
@@ -283,13 +283,14 @@
         qkv = (dot_nt(h_one, wqkv) + bqkv).astype(BF16)
         qkv = qkv.reshape(8, images, toks, 3 * WIDTH)
         mixed = attention_forward(qkv).reshape(rows, WIDTH)
-        g_out = tie(d_out.reshape(8, images * toks, WIDTH), mixed)
+        g_out = tie(d_out.reshape(8, images * toks, WIDTH), h_one, wqkv)
         g_out = lax.all_to_all(g_out, tp, 0, 0).reshape(rows, WIDTH)
         attn_out = dot_nn(mixed, wo_all)
         x_mid = (x_f32 + attn_out + b_o).astype(BF16)
         mid_f32 = x_mid.astype(F32)
         h_two_f, ln2_pull = jax.vjp(layer_norm, mid_f32, ln2_gain, ln2_bias)
         h_two = h_two_f.astype(BF16)
+        w1_all = swap_weights(tie(w1_own_rows, h_two))
         blocks = (2, CHIPS, HALF, WIDTH)
         hidden, gelu_pulls = [], []
         for w1, b1 in zip(w1_all, b1_all):
@@ -324,12 +325,8 @@
         wo_own, wo_oth = pick(dw_o, core, 1), pick(dw_o, 1 - core, 1)
         wo_got = core_swap(wo_oth)
         w2_last, w2_part = stage3(w2_blk, w2_in[0])
-        mlp_out = dot_nn(tie(hidden[0], d_mixed), w2_all[0])
-        mlp_out = mlp_out + dot_nn(hidden[1], w2_all[1])
-        y_rows = (mid_f32 + mlp_out + b_2).astype(BF16)
         d_mixed = tie(d_mixed, w2_last).reshape(8, images, toks, WIDTH)
         d_qkv = attention_backward(qkv, d_mixed).reshape(rows, 3 * WIDTH)
-        y_out = lax.all_to_all(y_rows.reshape(8, images * toks, WIDTH), tp, 0, 0).reshape(x.shape)
         w1_last, w1_part = stage3(w1_blk, w1_in[0])
         d_qkv = tie(d_qkv, w1_last)
         wo_blk = chip_sums(wo_own, wo_got, 0)
@@ -338,7 +335,12 @@
         dw_qkv = dw_qkv.reshape(3, CHIPS, 2, QROWS, WIDTH)
         qkv_own, qkv_oth = pick(dw_qkv, core, 2), pick(dw_qkv, 1 - core, 2)
         qkv_got = core_swap(qkv_oth)
-        d_h_one = tie(d_h_one, qkv_oth)
+        grad_w2 = finish(w2_blk, w2_in[1], w2_part)
+        grad_w2 = grad_w2.reshape(MLP_PAD, WIDTH)[:MLP].astype(BF16)
+        qkv_blk = chip_sums(qkv_own, tie(qkv_got, grad_w2), 1)
+        qkv_far = lax.optimization_barrier(qkv_blk(away(1 - me)))
+        far_in = permute(qkv_far, first)
+        d_h_one = tie(d_h_one, qkv_oth, qkv_far)
         d_in_ln, g_ln1_gain, g_ln1_bias = ln1_pull(d_h_one.astype(F32))
         g_x = (d_mid.astype(F32) + d_in_ln).astype(BF16)
         col_sum = lambda v: jnp.sum(v, axis=0, dtype=F32)
@@ -348,23 +350,28 @@
         mlp_sums = jnp.where(core0, jnp.stack(mlp_sums, 1), jnp.stack(mlp_sums[::-1], 1))
         bias_sums = jnp.concatenate([head_sums[0], head_sums[2], mlp_sums, jnp.zeros((CHIPS, 2, WIDTH - 2 * QROWS - MLP_PAD), F32)], axis=2)
         small = jnp.concatenate([jnp.broadcast_to(vecs, (CHIPS, 6, WIDTH)), bias_sums], axis=1)
-        qkv_sum = chip_sums(qkv_own, qkv_got, 1)
-        qkv_blk = lambda i: jnp.concatenate([qkv_sum(i).reshape(3 * QROWS, WIDTH), pick(small, i)])
-        _, qkv_in = stage2(qkv_blk)
+        small_send = lax.optimization_barrier(jnp.stack([pick(small, away(me)), pick(small, away(1 - me))]))
+        small_in = permute(small_send, first)
+        near_send = lax.optimization_barrier(qkv_blk(away(me)))
+        near_in = permute(near_send, first)
         grad_x = lax.all_to_all(g_x.reshape(8, images * toks, WIDTH), tp, 0, 0).reshape(x.shape)
         _, wo_part = stage3(wo_blk, wo_in[0])
-        _, qkv_part = stage3(qkv_blk, qkv_in[0])
-        qkv_all = finish(qkv_blk, qkv_in[1], qkv_part)
-        grad_qkv = qkv_all[:3 * QROWS].reshape(3, QROWS, WIDTH).astype(BF16)
-        small_own = qkv_all[3 * QROWS:]
+        mlp_out = dot_nn(tie(hidden[0], near_send, g_x), w2_all[0])
+        mlp_out = mlp_out + dot_nn(hidden[1], w2_all[1])
+        y_rows = (mid_f32 + mlp_out + b_2).astype(BF16)
+        y_out = lax.all_to_all(tie(y_rows, grad_x).reshape(8, images * toks, WIDTH), tp, 0, 0).reshape(x.shape)
+        qkv_last, qkv_part = stage3(qkv_blk, tie(far_in, near_send))
+        grad_w1 = finish(w1_blk, w1_in[1], tie(w1_part, qkv_last))
+        grad_w1 = grad_w1.reshape(MLP_PAD, WIDTH)[:MLP].T.astype(BF16)
+        near_in = tie(near_in, qkv_last, grad_w1)
+        small_far = pick(small, near(1 - me)) + small_in[1]
+        small_part = permute(small_far, second)
+        grad_qkv = finish(qkv_blk, near_in, qkv_part).astype(BF16)
+        small_own = pick(small, near(me)) + small_in[0] + small_part
         extra = small_own + core_swap(small_own)
         b_row = pick(extra[6:], core).astype(BF16)
 
-        grad_w2 = finish(w2_blk, w2_in[1], w2_part)
-        grad_w2 = grad_w2.reshape(MLP_PAD, WIDTH)[:MLP].astype(BF16)
-        grad_w1 = finish(w1_blk, w1_in[1], w1_part)
-        grad_w1 = grad_w1.reshape(MLP_PAD, WIDTH)[:MLP].T.astype(BF16)
-        grad_wo = finish(wo_blk, wo_in[1], wo_part)
+        grad_wo = finish(wo_blk, wo_in[1], tie(wo_part, qkv_last))
         grad_wo = grad_wo.reshape(HEADS, HEAD_DIM, WIDTH).astype(BF16)
         unrow = lambda w: jnp.transpose(w.reshape(HEADS, HEAD_DIM, WIDTH), (2, 0, 1))
 

time: 731 us -> 717 us (0.981)
  local copies, waits for them, and re-layouts: 66.4 us -> 55 us
    ppermute x19 -> x21, waiting for transfers between devices: 141 us -> 182 us  [permute(): return lax.ppermute(val, tp, tp_perm(fn))]
    all_gather x1, waiting for transfers between devices: 61 us -> 26.5 us  [gather_all(): lax.all_gather(jnp.where(dp == 0, half0, half1), ALL_AXES, axis=0, tiled=...]
    all_gather x2, waiting for transfers between devices: 18.8 us -> 5.53 us  [gather_own(): lax.all_gather(jnp.where(dp == 0, half0, half1), ('dp', 'chip'), axis=0,...]
    dynamic_slice x3 -> x1, local copies, waits for them, and re-layouts: 11.7 us -> 0.02 us  [pick(): return lax.dynamic_index_in_dim(val, idx, axis, keepdims=False)]
    all_to_all x1, waiting for transfers between devices: 11.4 us -> 0.01 us  [layer_step(): lax.all_to_all(g_x.reshape(8, images * toks, WIDTH), tp, 0, 0)]
    add x7 -> x4, other arithmetic: 18.9 us -> 21.8 us  [chip_sums(): return lambda i: pick(own, i, axis) + pick(got, i, axis)]
    ppermute x19 -> x21, starting transfers between devices: 16.9 us -> 15.2 us  [permute(): return lax.ppermute(val, tp, tp_perm(fn))]
  transfers between devices with their start and end apart: 26 -> 28, of which waited for: 13 -> 10; matrix products, arithmetic and copies ran while one was open for 35% -> 36% of each run, Pallas kernels for 6% -> 6%
where the time goes in v3:
time: 717 us; the launch traced here: 708 us
  waiting for transfers between devices  281 us (39%)
  matrix products  160 us (22%)
  other arithmetic  89.9 us (13%)
  Pallas kernels  74.4 us (10%)
  local copies, waits for them, and re-layouts  55 us (8%)
  starting transfers between devices  32.9 us (5%)
  between operations  15 us (2%)
    ppermute x21, waiting for transfers between devices, permute(): return lax.ppermute(val, tp, tp_perm(fn))  182 us
    dot_general x6, matrix products, dot_nt(): lax.dot_general(a, b, (((1,), (1,)), ((), ())), preferred_element_type=F32)  73.4 us
    dot_general x5, matrix products, dot_nn(): lax.dot_general(a, b, (((1,), (0,)), ((), ())), preferred_element_type=F32)  45.2 us
    pallas_call x2, Pallas kernels, attention_call(): pl.pallas_call(body, grid=(images,), out_shape=jax.ShapeDtypeStruct((grou...  42.9 us
    dot_general x5, matrix products, dot_tn(): lax.dot_general(a, b, (((0,), (0,)), ((), ())), preferred_element_type=F32)  41 us
    all_to_all x1, waiting for transfers between devices, layer_step(): lax.all_to_all(x.reshape(8, images * toks, WIDTH), tp, 0, 0)  38 us
    pallas_call x1, Pallas kernels, projection_backward(): pl.pallas_call(qkv_grads, grid=(cols // block,), name='qkv_grads', out_sh...  31.5 us
    all_gather x1, waiting for transfers between devices, gather_all(): lax.all_gather(jnp.where(dp == 0, half0, half1), ALL_AXES, axis=0, tiled=...  26.5 us
  transfers between devices with their start and end apart: 28, of which 10 were waited for; matrix products, arithmetic and copies ran while one was open for 36% of the time, Pallas kernels for 6%

profile of v3, /device:TPU:0, one launch (start us, length us, event | category | flops | bytes accessed | tf_op | source)
XLA Modules:
  0.0 707.6 jit_solution(12315964822561270898)
XLA Ops:
  12.0 5.4 all-to-all-start
  19.8 38.0 %all-to-all-done = bf16[8,128,1152]{2,1,0:T(8,128)(2,1)S(1)} async-done(((bf16[8,128,1152]{2,1,0:T(8,128)(2,1)}), bf16[8,128,1152]{2,1,0:T(8,128)(2,1)S(1)}, u32[]{:S(2)}, u32[]{:S(2)}) %all-to-all-start) | async-done | bytes 2359328 | tf_op jit(solution)/shard_map/all_to_all | solution.py:279
  62.6 26.5 %all-gather.6.cloned.1.call-done = bf16[16,304,1152]{2,1,0:T(8,128)(2,1)} async-done(((bf16[1,304,1152]{2,1,0:T(8,128)(2,1)}), bf16[16,304,1152]{2,1,0:T(8,128)(2,1)}) %all-gather.6.cloned.1.call-update) | async-done | bytes 11206672 | tf_op jit(solution)/shard_map/all_gather | solution.py:244
  90.2 6.4 fusion.109
  96.6 18.4 %add_convert_fusion = bf16[1024,3456]{1,0:T(8,128)(2,1)} fusion(bf16[1024,1152]{1,0:T(8,128)(2,1)} %fusion.54.h_ref, f32[3456]{0:T(1024)S(1)} %maximum_convert_fusion, bf16[1152,1152]{1,0:T(8,128)(2,1)S(1)} %bitcast.304, bf16[1152,1152]{1,0:T(8,128)(2,1)S(1)} %bitcast.306, bf16[1152,1152]{1,0:T(8,128)(2,1)} %bitcast.308), kind=kOutput, calls=%fused_computation.15 | convolution fusion | flops 8184692736 | bytes 17413632 | tf_op jit(solution)/shard_map/dot_general | solution.py:42
  115.0 13.4 %shard_map.296 = bf16[8,4,32,1152]{3,2,1,0:T(8,128)(2,1)} custom-call(bf16[8,4,32,3456]{3,2,1,0:T(8,128)(2,1)} %bitcast.347, bf16[8,4,32,3456]{3,2,1,0:T(8,128)(2,1)} %bitcast.348, bf16[8,4,32,3456]{3,2,1,0:T(8,128)(2,1)} %bitcast.349), custom_call_target="tpu_custom_call" | custom-call | flops 17179869184 | bytes 9437184 | tf_op jit(solution)/shard_map/pallas_call | solution.py:126
  128.5 6.1 convert_reduce_fusion.4
  138.8 5.5 all-gather.8.cloned.1.call-done
  147.8 6.5 pad_maximum_fusion.w_ref
  154.3 3.8 all-to-all-start.1
  158.0 11.5 %fusion.23 = (bf16[1024,2176]{1,0:T(8,128)(2,1)}, bf16[1024,2176]{1,0:T(8,128)(2,1)}) fusion(f32[2176]{0:T(1024)S(1)} %reshape.409, bf16[1024,1152]{1,0:T(8,128)(2,1)} %fusion.41, bf16[2176,1152]{1,0:T(8,128)(2,1)} %all-gather.8.cloned.1.call-done), kind=kOutput, calls=%fused_computation.37 | convolution fusion | flops 5160566784 | bytes 16294400 | tf_op jit(solution)/shard_map/dot_general | solution.py:42
  169.7 11.6 %fusion.19 = (bf16[2176,1024]{0,1:T(8,128)(2,1)}, bf16[1024,2176]{1,0:T(8,128)(2,1)}) fusion(f32[2176]{0:T(1024)S(1)} %reshape.410, bf16[1024,1152]{1,0:T(8,128)(2,1)} %fusion.41, bf16[2176,1152]{1,0:T(8,128)(2,1)} %collective-permute-done), kind=kOutput, calls=%fused_computation.33 | convolution fusion | flops 5160566784 | bytes 16294400 | tf_op jit(solution)/shard_map/dot_general | solution.py:42
  181.2 6.5 copy.116
  187.7 8.6 %all-to-all-done.1 = bf16[8,128,1152]{2,1,0:T(8,128)(2,1)S(1)} async-done(((bf16[8,128,1152]{2,1,0:T(8,128)(2,1)}), bf16[8,128,1152]{2,1,0:T(8,128)(2,1)S(1)}, u32[]{:S(2)}, u32[]{:S(2)}) %all-to-all-start.1) | async-done | bytes 2359328 | tf_op jit(solution)/shard_map/all_to_all | solution.py:287
  196.4 10.0 %fusion.111 = f32[2,4,272,1152]{3,2,1,0:T(8,128)} fusion(bf16[2,4,272,1024]{3,2,1,0:T(8,128)(2,1)} %bitcast.322, bf16[1024,1152,1,1]{1,0,3,2:T(8,128)(2,1)S(1)} %bitcast.296), kind=kOutput, calls=%fused_computation.217 | convolution fusion | flops 5133828096 | bytes 16842752 | tf_op jit(solution)/shard_map/dot_general | solution.py:50
  206.4 6.6 copy.117
  212.9 10.0 %fusion.112 = f32[2,4,272,1152]{3,2,1,0:T(8,128)} fusion(bf16[2,4,272,1024]{3,2,1,0:T(8,128)(2,1)} %bitcast.323, bf16[1024,1152,1,1]{1,0,3,2:T(8,128)(2,1)S(1)} %bitcast.297), kind=kOutput, calls=%fused_computation.218 | convolution fusion | flops 5133828096 | bytes 16842752 | tf_op jit(solution)/shard_map/dot_general | solution.py:50
  223.4 7.1 %fusion.71 = (f32[2,272,1152]{2,1,0:T(8,128)}, f32[2,272,1152]{2,1,0:T(8,128)}) fusion(f32[2,4,272,1152]{3,2,1,0:T(8,128)} %collective-permute-done.1, s32[]{:T(128)S(6)} %select_n.162, f32[2,4,272,1152]{3,2,1,0:T(8,128)} %fusion.112, s32[]{:T(128)S(6)} %select_n.160), kind=kLoop, calls=%fused_computation.119 | loop fusion | flops 1253376 | bytes 15040520 | tf_op jit(solution)/shard_map/add | solution.py:228
  230.6 13.6 %convert_reduce_fusion.1 = (f32[2176]{0:T(1024)}, bf16[1024,2176]{1,0:T(8,128)(2,1)}) fusion(bf16[1024,2176]{1,0:T(8,128)(2,1)} %get-tuple-element.127, bf16[1024,1152]{1,0:T(8,128)(2,1)S(1)} %bitcast.298, bf16[2176,1152]{1,0:T(8,128)(2,1)S(1)} %copy-done.37), kind=kOutput, calls=%fused_computation.47 | convolution fusion | flops 5189531648 | bytes 16294400 | tf_op jit(solution)/shard_map/dot_general | solution.py:42
  244.1 13.5 %convert_reduce_fusion = (f32[2176]{0:T(1024)}, bf16[1024,2176]{1,0:T(8,128)(2,1)S(1)}) fusion(bf16[1024,2176]{1,0:T(8,128)(2,1)S(1)} %bitcast.360, bf16[1024,1152]{1,0:T(8,128)(2,1)S(1)} %bitcast.299, bf16[2176,1152]{1,0:T(8,128)(2,1)} %collective-permute-done.2), kind=kOutput, calls=%fused_computation.46 | convolution fusion | flops 5189531648 | bytes 16294400 | tf_op jit(solution)/shard_map/dot_general | solution.py:42
  257.6 8.7 %fusion.113 = f32[2176,1152]{1,0:T(8,128)} fusion(bf16[1024,2176]{1,0:T(8,128)(2,1)S(1)} %get-tuple-element.60, bf16[1024,1152]{1,0:T(8,128)(2,1)S(1)} %copy-done.13), kind=kOutput, calls=%fused_computation.219 | convolution fusion | flops 5133828096 | bytes 16842752 | tf_op jit(solution)/shard_map/dot_general | solution.py:50
  267.6 4.5 copy.130
  272.1 9.0 %fusion.114 = f32[2176,1152]{1,0:T(8,128)S(1)} fusion(bf16[1024,2176]{1,0:T(8,128)(2,1)} %get-tuple-element.59, bf16[1024,1152]{1,0:T(8,128)(2,1)} %fusion.41), kind=kOutput, calls=%fused_computation.220 | convolution fusion | flops 5133828096 | bytes 16842752 | tf_op jit(solution)/shard_map/dot_general | solution.py:50
  281.1 16.0 %collective-permute-done.4 = f32[2,272,1152]{2,1,0:T(8,128)} collective-permute-done((f32[2,272,1152]{2,1,0:T(8,128)}, f32[2,272,1152]{2,1,0:T(8,128)}, u32[]{:S(2)}, u32[]{:S(2)}) %collective-permute-start.4) | collective-permute-done | bytes 2506784 | tf_op jit(solution)/shard_map/ppermute | solution.py:203
  297.1 5.1 fusion.68
  302.2 6.0 fusion.69
  309.2 6.2 fusion.115
  315.5 9.8 %convert_reduce_fusion.3 = (f32[1152]{0:T(1024)S(1)}, f32[1024]{0:T(1024)S(1)}, bf16[1024,1152]{1,0:T(8,128)(2,1)S(1)}) fusion(f32[1152]{0:T(1024)S(1)} %copy-done.21, f32[1024]{0:T(1024)S(1)} %broadcast_multiply_fusion, bf16[1024,1152]{1,0:T(8,128)(2,1)S(1)} %copy-done.3, f32[1024,1152]{1,0:T(8,128)S(1)} %fusion.115, bf16[1024,2176]{1,0:T(8,128)(2,1)S(1)} %bitcast.358, ...), kind=kOutput, calls=%fused_computation.57 | convolution fusion | flops 5144442880 | bytes 18924544 | tf_op jit(solution)/shard_map/dot_general | solution.py:46
  330.7 4.8 convolution_convert_fusion.2
  342.9 29.5 %shard_map.297 = bf16[8,4,32,3456]{3,2,1,0:T(8,128)(2,1)} custom-call(bf16[8,4,32,3456]{3,2,1,0:T(8,128)(2,1)} %bitcast.350, bf16[8,4,32,3456]{3,2,1,0:T(8,128)(2,1)} %bitcast.351, bf16[8,4,32,3456]{3,2,1,0:T(8,128)(2,1)} %bitcast.352, bf16[8,4,32,1152]{3,2,1,0:T(8,128)(2,1)} %bitcast.354), custom_call_target="tpu_custom_call" | custom-call | flops 42949672960 | bytes 16515072 | tf_op jit(solution)/shard_map/pallas_call | solution.py:126
  372.4 5.0 fusion.66
  380.3 31.5 %qkv_grads.1 = (f32[3456,1152]{1,0:T(8,128)}, bf16[1024,1152]{1,0:T(8,128)(2,1)}, f32[1,3456]{1,0:T(1,128)}) custom-call(bf16[1024,3456]{1,0:T(8,128)(2,1)} %bitcast.353, bf16[1024,1152]{1,0:T(8,128)(2,1)} %fusion.54.h_ref, bf16[3456,1152]{1,0:T(8,128)(2,1)} %pad_maximum_fusion.w_ref), custom_call_target="tpu_custom_call" | custom-call | flops 32614907904 | bytes 30965760 | tf_op jit(solution)/shard_map/qkv_grads/pallas_call | solution.py:168
  411.8 6.9 dynamic-slice_bitcast_fusion
  422.4 53.7 %collective-permute-done.8 = f32[2,272,1152]{2,1,0:T(8,128)} collective-permute-done((f32[2,272,1152]{2,1,0:T(8,128)}, f32[2,272,1152]{2,1,0:T(8,128)}, u32[]{:S(2)}, u32[]{:S(2)}) %collective-permute-start.8) | collective-permute-done | bytes 2506784 | tf_op jit(solution)/shard_map/ppermute | solution.py:203
  477.9 5.4 fusion.76
  489.2 5.8 bitcast_add_fusion.11
  501.5 4.7 fusion.43
  506.2 62.5 %collective-permute-done.10 = f32[2,8,1152]{2,1,0:T(8,128)S(1)} collective-permute-done((f32[2,8,1152]{2,1,0:T(8,128)S(1)}, f32[2,8,1152]{2,1,0:T(8,128)S(1)}, u32[]{:S(2)}, u32[]{:S(2)}) %collective-permute-start.10) | collective-permute-done | bytes 73760 | tf_op jit(solution)/shard_map/ppermute | solution.py:203
  569.1 10.2 %fusion.116 = f32[1024,1152]{1,0:T(8,128)} fusion(bf16[1024,2176]{1,0:T(8,128)(2,1)S(1)} %bitcast.321, bf16[2176,1152]{1,0:T(8,128)(2,1)} %all-gather.10.cloned.1.call-done), kind=kOutput, calls=%fused_computation.222 | convolution fusion | flops 5133828096 | bytes 14188544 | tf_op jit(solution)/shard_map/dot_general | solution.py:46
  579.3 4.8 all-to-all-start.2
  584.6 12.9 %fusion.47 = bf16[1024,1152]{1,0:T(8,128)(2,1)} fusion(bf16[1024,1152]{1,0:T(8,128)(2,1)S(1)} %copy-done.4, f32[1024,1152]{1,0:T(8,128)} %fusion.116, bf16[2176,1152]{1,0:T(8,128)(2,1)} %collective-permute-done.2, bf16[1024,2176]{1,0:T(8,128)(2,1)} %get-tuple-element.129, f32[1152]{0:T(1024)S(1)} %convert_element_type.217), kind=kOutput, calls=%fused_computation.82 | convolution fusion | flops 5162008576 | bytes 18911744 | tf_op jit(solution)/shard_map/dot_general | solution.py:46
  601.1 4.3 fusion.79
  608.7 5.4 fusion.74
  614.2 48.0 %collective-permute-done.20 = f32[144,1152]{1,0:T(8,128)S(1)} collective-permute-done((f32[144,1152]{1,0:T(8,128)S(1)}, f32[144,1152]{1,0:T(8,128)S(1)}, u32[]{:S(2)}, u32[]{:S(2)}) %collective-permute-start.20) | collective-permute-done | bytes 663584 | tf_op jit(solution)/shard_map/ppermute | solution.py:203
  663.0 3.6 all-to-all-start.3
  671.4 3.7 fusion.82
  676.1 19.9 %all-to-all-done.3 = bf16[8,128,1152]{2,1,0:T(8,128)(2,1)S(1)} async-done(((bf16[8,128,1152]{2,1,0:T(8,128)(2,1)}), bf16[8,128,1152]{2,1,0:T(8,128)(2,1)S(1)}, u32[]{:S(2)}, u32[]{:S(2)}) %all-to-all-start.3) | async-done | bytes 2359328 | tf_op jit(solution)/shard_map/all_to_all | solution.py:362
  697.4 3.3 copy.157
  (236 shorter events, 72.5 us)
Async XLA Ops:
  7.2 81.9 %all-gather.6.cloned.1.call-start = ((), (), s32[]{:S(2)}) async-start(), calls=%async_computation.4 | async-start | bytes 11907072 | tf_op jit(solution)/shard_map/all_gather | solution.py:244
  12.0 45.9 %all-to-all-start = ((bf16[8,128,1152]{2,1,0:T(8,128)(2,1)}), bf16[8,128,1152]{2,1,0:T(8,128)(2,1)S(1)}, u32[]{:S(2)}, u32[]{:S(2)}) async-start(bf16[8,128,1152]{2,1,0:T(8,128)(2,1)} %bitcast.327), calls=%async_computation | async-start | bytes 4718592 | tf_op jit(solution)/shard_map/all_to_all | solution.py:279
  17.4 42.8 %copy-start.17 = (f32[1152]{0:T(1024)S(1)}, f32[1152]{0:T(1024)}, u32[]{:S(2)}) copy-start(f32[1152]{0:T(1024)} %param.19) | copy-start | bytes 13828
  17.4 42.8 %copy-start.32 = (f32[1152]{0:T(1024)S(1)}, f32[1152]{0:T(1024)}, u32[]{:S(2)}) copy-start(f32[1152]{0:T(1024)} %param.20) | copy-start | bytes 13828
  17.5 126.9 %all-gather.8.cloned.1.call-start = ((), (), s32[]{:S(2)}) async-start(), calls=%async_computation.5 | async-start | bytes 5640192 | tf_op jit(solution)/shard_map/all_gather | solution.py:247
  19.8 203.1 %all-gather.10.cloned.1.call-start = ((), (), s32[]{:S(2)}) async-start(), calls=%async_computation.6 | async-start | bytes 5640192 | tf_op jit(solution)/shard_map/all_gather | solution.py:247
  57.9 70.6 %copy-start = (bf16[8,128,1152]{2,1,0:T(8,128)(2,1)}, bf16[8,128,1152]{2,1,0:T(8,128)(2,1)S(1)}, u32[]{:S(2)}) copy-start(bf16[8,128,1152]{2,1,0:T(8,128)(2,1)S(1)} %all-to-all-done) | copy-start | bytes 7077892
  96.5 18.5 %copy-start.6 = (bf16[1,8,144,1152]{3,2,1,0:T(8,128)(2,1)}, bf16[1,8,144,1152]{3,2,1,0:T(8,128)(2,1)S(1)}, u32[]{:S(2)}) copy-start(bf16[1,8,144,1152]{3,2,1,0:T(8,128)(2,1)S(1)} %get-tuple-element.108) | copy-start | bytes 7962628
  96.6 18.5 %copy-start.8 = (bf16[1,8,144,1152]{3,2,1,0:T(8,128)(2,1)}, bf16[1,8,144,1152]{3,2,1,0:T(8,128)(2,1)S(1)}, u32[]{:S(2)}) copy-start(bf16[1,8,144,1152]{3,2,1,0:T(8,128)(2,1)S(1)} %get-tuple-element.109) | copy-start | bytes 7962628
  134.5 13.3 %copy-start.7 = (bf16[1,8,144,1152]{3,2,1,0:T(8,128)(2,1)S(1)}, bf16[1,8,144,1152]{3,2,1,0:T(8,128)(2,1)}, u32[]{:S(2)}) copy-start(bf16[1,8,144,1152]{3,2,1,0:T(8,128)(2,1)} %copy-done.6) | copy-start | bytes 7962628
  144.4 25.3 %collective-permute-start = (bf16[2176,1152]{1,0:T(8,128)(2,1)}, bf16[2176,1152]{1,0:T(8,128)(2,1)}, u32[]{:S(2)}, u32[]{:S(2)}) collective-permute-start(bf16[2176,1152]{1,0:T(8,128)(2,1)} %all-gather.8.cloned.1.call-done), channel_id=1, source_target_pairs={{0,1},{1,0},{2,3},{3,2},{4,5},{5,4},{6,7},{7,6},{8,9},{9,8},{10,11... | collective-permute-start | bytes 15040520 | tf_op jit(solution)/shard_map/ppermute | solution.py:203
  154.3 42.1 %all-to-all-start.1 = ((bf16[8,128,1152]{2,1,0:T(8,128)(2,1)}), bf16[8,128,1152]{2,1,0:T(8,128)(2,1)S(1)}, u32[]{:S(2)}, u32[]{:S(2)}) async-start(bf16[8,128,1152]{2,1,0:T(8,128)(2,1)} %bitcast.328), calls=%async_computation.1 | async-start | bytes 4718592 | tf_op jit(solution)/shard_map/all_to_all | solution.py:287
  206.4 17.0 %collective-permute-start.1 = (f32[2,4,272,1152]{3,2,1,0:T(8,128)}, f32[2,4,272,1152]{3,2,1,0:T(8,128)}, u32[]{:S(2)}, u32[]{:S(2)}) collective-permute-start(f32[2,4,272,1152]{3,2,1,0:T(8,128)} %fusion.111), channel_id=1, source_target_pairs={{0,1},{1,0},{2,3},{3,2},{4,5},{5,4},{6,7},{7,6},{8,9},{9,8},{10,11... | collective-permute-start | bytes 30081032 | tf_op jit(solution)/shard_map/ppermute | solution.py:203
  222.9 21.2 %collective-permute-start.2 = (bf16[2176,1152]{1,0:T(8,128)(2,1)}, bf16[2176,1152]{1,0:T(8,128)(2,1)}, u32[]{:S(2)}, u32[]{:S(2)}) collective-permute-start(bf16[2176,1152]{1,0:T(8,128)(2,1)} %all-gather.10.cloned.1.call-done), channel_id=1, source_target_pairs={{0,1},{1,0},{2,3},{3,2},{4,5},{5,4},{6,7},{7,6},{8,9},{9,8},{10,11... | collective-permute-start | bytes 15040520 | tf_op jit(solution)/shard_map/ppermute | solution.py:203
  223.4 20.7 %slice-start.8 = ((s8[4456448]{0:T(1024)(128)(4,1)}), s8[4194304]{0:T(1024)(128)(4,1)S(1)}, s32[]{:S(2)}) async-start(s8[4456448]{0:T(1024)(128)(4,1)} %bitcast.359), calls=%async_computation.15 | async-start | bytes 8388608
  230.6 13.6 %slice-start.9 = ((s8[4456448]{0:T(1024)(128)(4,1)}), s8[262144]{0:T(1024)(128)(4,1)S(1)}, s32[]{:S(2)}) async-start(s8[4456448]{0:T(1024)(128)(4,1)} %bitcast.359), calls=%async_computation.16 | async-start | bytes 524288
  244.1 13.5 %copy-start.13 = (bf16[1024,1152]{1,0:T(8,128)(2,1)S(1)}, bf16[1024,1152]{1,0:T(8,128)(2,1)}, u32[]{:S(2)}) copy-start(bf16[1024,1152]{1,0:T(8,128)(2,1)} %fusion.41) | copy-start | bytes 7077892
  266.3 35.9 %collective-permute-start.3 = (f32[2,4,272,1152]{3,2,1,0:T(8,128)}, f32[2,4,272,1152]{3,2,1,0:T(8,128)}, u32[]{:S(2)}, u32[]{:S(2)}) collective-permute-start(f32[2,4,272,1152]{3,2,1,0:T(8,128)} %bitcast.32), channel_id=1, source_target_pairs={{0,1},{1,0},{2,3},{3,2},{4,5},{5,4},{6,7},{7,6},{8,9},{9,8},{10,11... | collective-permute-start | bytes 30081032 | tf_op jit(solution)/shard_map/ppermute | solution.py:203
  266.4 30.7 %collective-permute-start.4 = (f32[2,272,1152]{2,1,0:T(8,128)}, f32[2,272,1152]{2,1,0:T(8,128)}, u32[]{:S(2)}, u32[]{:S(2)}) collective-permute-start(f32[2,272,1152]{2,1,0:T(8,128)} %get-tuple-element.51), channel_id=1, source_target_pairs={{0,2},{1,5},{2,0},{3,7},{4,6},{5,1},{6,4},{7,3},{8,10},{9,13},{10,... | collective-permute-start | bytes 7520264 | tf_op jit(solution)/shard_map/ppermute | solution.py:203
  281.1 21.1 %copy-start.9 = (f32[2176,1152]{1,0:T(8,128)}, f32[2176,1152]{1,0:T(8,128)S(1)}, u32[]{:S(2)}) copy-start(f32[2176,1152]{1,0:T(8,128)S(1)} %fusion.114) | copy-start | bytes 30081028
  297.1 12.1 %slice-start.2 = ((s8[5013504]{0:T(1024)(128)(4,1)}), s8[4194304]{0:T(1024)(128)(4,1)S(1)}, s32[]{:S(2)}) async-start(s8[5013504]{0:T(1024)(128)(4,1)} %bitcast.345), calls=%async_computation.9 | async-start | bytes 8388608
  297.1 12.1 %slice-start.4 = ((s8[4456448]{0:T(1024)(128)(4,1)}), s8[4194304]{0:T(1024)(128)(4,1)S(1)}, s32[]{:S(2)}) async-start(s8[4456448]{0:T(1024)(128)(4,1)} %bitcast.355), calls=%async_computation.11 | async-start | bytes 8388608
  308.2 64.2 %collective-permute-start.5 = (f32[2,272,1152]{2,1,0:T(8,128)}, f32[2,272,1152]{2,1,0:T(8,128)}, u32[]{:S(2)}, u32[]{:S(2)}) collective-permute-start(f32[2,272,1152]{2,1,0:T(8,128)} %get-tuple-element.57), channel_id=1, source_target_pairs={{0,2},{1,5},{2,0},{3,7},{4,6},{5,1},{6,4},{7,3},{8,10},{9,13},{10,... | collective-permute-start | bytes 7520264 | tf_op jit(solution)/shard_map/ppermute | solution.py:203
  315.5 9.9 %copy-start.29 = (f32[1024]{0:T(1024)S(1)}, f32[1024]{0:T(1024)}, u32[]{:S(2)}) copy-start(f32[1024]{0:T(1024)} %copy-done.28) | copy-start | bytes 12292
  315.5 9.9 %copy-start.25 = (f32[1024]{0:T(1024)S(1)}, f32[1024]{0:T(1024)}, u32[]{:S(2)}) copy-start(f32[1024]{0:T(1024)} %copy-done.24) | copy-start | bytes 12292
  342.9 34.5 %collective-permute-start.6 = (f32[4,144,1152]{2,1,0:T(8,128)}, f32[4,144,1152]{2,1,0:T(8,128)}, u32[]{:S(2)}, u32[]{:S(2)}) collective-permute-start(f32[4,144,1152]{2,1,0:T(8,128)} %dynamic-slice_bitcast_fusion.1), channel_id=1, source_target_pairs={{0,1},{1,0},{2,3},{3,2},{4,5},{5,4},{6,7},{7,6},{8,9},{9,8},{10,11... | collective-permute-start | bytes 7962632 | tf_op jit(solution)/shard_map/ppermute | solution.py:203
  411.8 10.0 %copy-start.30 = (f32[2176]{0:T(1024)S(1)}, f32[2176]{0:T(1024)}, u32[]{:S(2)}) copy-start(f32[2176]{0:T(1024)} %get-tuple-element.133) | copy-start | bytes 26116
  411.8 10.2 %copy-start.31 = (f32[2176]{0:T(1024)S(1)}, f32[2176]{0:T(1024)}, u32[]{:S(2)}) copy-start(f32[2176]{0:T(1024)} %get-tuple-element.131) | copy-start | bytes 26116
  418.8 70.4 %collective-permute-start.7 = (f32[3,4,144,1152]{3,2,1,0:T(8,128)}, f32[3,4,144,1152]{3,2,1,0:T(8,128)}, u32[]{:S(2)}, u32[]{:S(2)}) collective-permute-start(f32[3,4,144,1152]{3,2,1,0:T(8,128)} %dynamic-slice_bitcast_fusion), channel_id=1, source_target_pairs={{0,1},{1,0},{2,3},{3,2},{4,5},{5,4},{6,7},{7,6},{8,9},{9,8},{10,11... | collective-permute-start | bytes 23887880 | tf_op jit(solution)/shard_map/ppermute | solution.py:203
  419.3 56.8 %collective-permute-start.8 = (f32[2,272,1152]{2,1,0:T(8,128)}, f32[2,272,1152]{2,1,0:T(8,128)}, u32[]{:S(2)}, u32[]{:S(2)}) collective-permute-start(f32[2,272,1152]{2,1,0:T(8,128)} %get-tuple-element.52), channel_id=1, source_target_pairs={{0,2},{1,5},{2,0},{3,7},{4,6},{5,1},{6,4},{7,3},{8,10},{9,13},{10,... | collective-permute-start | bytes 7520264 | tf_op jit(solution)/shard_map/ppermute | solution.py:203
  420.3 57.6 %collective-permute-start.9 = (f32[2,272,1152]{2,1,0:T(8,128)}, f32[2,272,1152]{2,1,0:T(8,128)}, u32[]{:S(2)}, u32[]{:S(2)}) collective-permute-start(f32[2,272,1152]{2,1,0:T(8,128)} %fusion.68), channel_id=1, source_target_pairs={{0,4},{1,3},{2,6},{3,1},{4,0},{5,7},{6,2},{7,5},{8,12},{9,11},{10,... | collective-permute-start | bytes 7520264 | tf_op jit(solution)/shard_map/ppermute | solution.py:203
  422.2 64.3 %copy-start.34 = (f32[1,3456]{1,0:T(1,128)S(1)}, f32[1,3456]{1,0:T(1,128)}, u32[]{:S(2)}) copy-start(f32[1,3456]{1,0:T(1,128)} %get-tuple-element.72) | copy-start | bytes 41476
  422.3 64.7 %collective-permute-start.19 = (f32[144,1152]{1,0:T(8,128)}, f32[144,1152]{1,0:T(8,128)S(1)}, u32[]{:S(2)}, u32[]{:S(2)}) collective-permute-start(f32[144,1152]{1,0:T(8,128)} %get-tuple-element.63), channel_id=1, source_target_pairs={{0,2},{1,5},{2,0},{3,7},{4,6},{5,1},{6,4},{7,3},{8,10},{9,13},{10,... | collective-permute-start | bytes 1990664 | tf_op jit(solution)/shard_map/ppermute | solution.py:203
  483.4 125.4 %collective-permute-start.15 = (f32[2,272,1152]{2,1,0:T(8,128)}, f32[2,272,1152]{2,1,0:T(8,128)}, u32[]{:S(2)}, u32[]{:S(2)}) collective-permute-start(f32[2,272,1152]{2,1,0:T(8,128)} %get-tuple-element.58), channel_id=1, source_target_pairs={{0,2},{1,5},{2,0},{3,7},{4,6},{5,1},{6,4},{7,3},{8,10},{9,13},{10,... | collective-permute-start | bytes 7520264 | tf_op jit(solution)/shard_map/ppermute | solution.py:203
  484.3 123.9 %collective-permute-start.16 = (f32[2,272,1152]{2,1,0:T(8,128)}, f32[2,272,1152]{2,1,0:T(8,128)}, u32[]{:S(2)}, u32[]{:S(2)}) collective-permute-start(f32[2,272,1152]{2,1,0:T(8,128)} %fusion.66), channel_id=1, source_target_pairs={{0,4},{1,3},{2,6},{3,1},{4,0},{5,7},{6,2},{7,5},{8,12},{9,11},{10,... | collective-permute-start | bytes 7520264 | tf_op jit(solution)/shard_map/ppermute | solution.py:203
  484.6 184.5 %collective-permute-start.18 = (f32[144,1152]{1,0:T(8,128)}, f32[144,1152]{1,0:T(8,128)S(1)}, u32[]{:S(2)}, u32[]{:S(2)}) collective-permute-start(f32[144,1152]{1,0:T(8,128)} %get-tuple-element.64), channel_id=1, source_target_pairs={{0,2},{1,5},{2,0},{3,7},{4,6},{5,1},{6,4},{7,3},{8,10},{9,13},{10,... | collective-permute-start | bytes 1990664 | tf_op jit(solution)/shard_map/ppermute | solution.py:203
  495.0 106.1 %collective-permute-start.14 = (f32[3,144,1152]{2,1,0:T(8,128)}, f32[3,144,1152]{2,1,0:T(8,128)}, u32[]{:S(2)}, u32[]{:S(2)}) collective-permute-start(f32[3,144,1152]{2,1,0:T(8,128)} %get-tuple-element.101), channel_id=1, source_target_pairs={{0,2},{1,5},{2,0},{3,7},{4,6},{5,1},{6,4},{7,3},{8,10},{9,13},{10,... | collective-permute-start | bytes 5971976 | tf_op jit(solution)/shard_map/ppermute | solution.py:203
  499.5 69.5 %slice-start = ((s8[4456448]{0:T(1024)(128)(4,1)}), s8[4194304]{0:T(1024)(128)(4,1)S(1)}, s32[]{:S(2)}) async-start(s8[4456448]{0:T(1024)(128)(4,1)} %bitcast.320), calls=%async_computation.7 | async-start | bytes 8388608
  499.5 69.5 %slice-start.1 = ((s8[4456448]{0:T(1024)(128)(4,1)}), s8[262144]{0:T(1024)(128)(4,1)S(1)}, s32[]{:S(2)}) async-start(s8[4456448]{0:T(1024)(128)(4,1)} %bitcast.320), calls=%async_computation.8 | async-start | bytes 524288
  499.6 69.1 %collective-permute-start.10 = (f32[2,8,1152]{2,1,0:T(8,128)S(1)}, f32[2,8,1152]{2,1,0:T(8,128)S(1)}, u32[]{:S(2)}, u32[]{:S(2)}) collective-permute-start(f32[2,8,1152]{2,1,0:T(8,128)S(1)} %pad_maximum_fusion.1), channel_id=1, source_target_pairs={{0,2},{1,5},{2,0},{3,7},{4,6},{5,1},{6,4},{7,3},{8,10},{9,13},{10,... | collective-permute-start | bytes 221192 | tf_op jit(solution)/shard_map/ppermute | solution.py:203
  568.7 15.3 %collective-permute-start.11 = (f32[8,1152]{1,0:T(8,128)S(1)}, f32[8,1152]{1,0:T(8,128)S(1)}, u32[]{:S(2)}, u32[]{:S(2)}) collective-permute-start(f32[8,1152]{1,0:T(8,128)S(1)} %fusion.91), channel_id=1, source_target_pairs={{0,4},{1,3},{2,6},{3,1},{4,0},{5,7},{6,2},{7,5},{8,12},{9,11},{10,... | collective-permute-start | bytes 110600 | tf_op jit(solution)/shard_map/ppermute | solution.py:203
  579.3 82.9 %all-to-all-start.2 = ((bf16[8,128,1152]{2,1,0:T(8,128)(2,1)}), bf16[8,128,1152]{2,1,0:T(8,128)(2,1)}, u32[]{:S(2)}, u32[]{:S(2)}) async-start(bf16[8,128,1152]{2,1,0:T(8,128)(2,1)} %bitcast.317), calls=%async_computation.2 | async-start | bytes 4718592 | tf_op jit(solution)/shard_map/all_to_all | solution.py:357
  584.1 13.4 %collective-permute-start.12 = (f32[8,1152]{1,0:T(8,128)S(1)}, f32[8,1152]{1,0:T(8,128)S(1)}, u32[]{:S(2)}, u32[]{:S(2)}) collective-permute-start(f32[8,1152]{1,0:T(8,128)S(1)} %fusion.95), channel_id=1, source_target_pairs={{0,1},{1,0},{2,3},{3,2},{4,5},{5,4},{6,7},{7,6},{8,9},{9,8},{10,11... | collective-permute-start | bytes 110600 | tf_op jit(solution)/shard_map/ppermute | solution.py:203
  597.4 10.8 %copy-start.15 = (f32[144,1152]{1,0:T(8,128)S(1)}, f32[144,1152]{1,0:T(8,128)}, u32[]{:S(2)}) copy-start(f32[144,1152]{1,0:T(8,128)} %fusion.83) | copy-start | bytes 1990660
  597.4 71.6 %collective-permute-start.13 = (f32[3,144,1152]{2,1,0:T(8,128)}, f32[3,144,1152]{2,1,0:T(8,128)}, u32[]{:S(2)}, u32[]{:S(2)}) collective-permute-start(f32[3,144,1152]{2,1,0:T(8,128)} %get-tuple-element.102), channel_id=1, source_target_pairs={{0,2},{1,5},{2,0},{3,7},{4,6},{5,1},{6,4},{7,3},{8,10},{9,13},{10,... | collective-permute-start | bytes 5971976 | tf_op jit(solution)/shard_map/ppermute | solution.py:203
  605.4 66.0 %collective-permute-start.17 = (f32[3,144,1152]{2,1,0:T(8,128)}, f32[3,144,1152]{2,1,0:T(8,128)}, u32[]{:S(2)}, u32[]{:S(2)}) collective-permute-start(f32[3,144,1152]{2,1,0:T(8,128)} %fusion.79), channel_id=1, source_target_pairs={{0,4},{1,3},{2,6},{3,1},{4,0},{5,7},{6,2},{7,5},{8,12},{9,11},{10,... | collective-permute-start | bytes 5971976 | tf_op jit(solution)/shard_map/ppermute | solution.py:203
  608.2 54.0 %collective-permute-start.20 = (f32[144,1152]{1,0:T(8,128)S(1)}, f32[144,1152]{1,0:T(8,128)S(1)}, u32[]{:S(2)}, u32[]{:S(2)}) collective-permute-start(f32[144,1152]{1,0:T(8,128)S(1)} %copy-done.15), channel_id=1, source_target_pairs={{0,4},{1,3},{2,6},{3,1},{4,0},{5,7},{6,2},{7,5},{8,12},{9,11},{10,... | collective-permute-start | bytes 1990664 | tf_op jit(solution)/shard_map/ppermute | solution.py:203
  663.0 33.0 %all-to-all-start.3 = ((bf16[8,128,1152]{2,1,0:T(8,128)(2,1)}), bf16[8,128,1152]{2,1,0:T(8,128)(2,1)S(1)}, u32[]{:S(2)}, u32[]{:S(2)}) async-start(bf16[8,128,1152]{2,1,0:T(8,128)(2,1)} %bitcast.331), calls=%async_computation.3 | async-start | bytes 4718592 | tf_op jit(solution)/shard_map/all_to_all | solution.py:362
  (29 other events, 138.0 us)
Sparse Core Ops, SparseCore 0:
  12.1 76.9 all-gather.5
  91.8 52.4 all-gather.7
  147.1 68.5 all-gather.9
